TPU v7x, 128 devices: a whole 4x4x4 slice. The times are simulated.
128 devices in a mesh: bx: 16 (over x, z_lo, core), by: 8 (over z_hi, y).
Axes of the slice: x: 4, y: 4, z: 4 (z_hi: 2, z_lo: 2; z = z_hi * 2 + z_lo), core: 2. Of those that a mesh axis runs over, the one named last changes fastest.
Arguments:
- photon_data: float32 [6, 1024, 256, 128], P(None, 'bx', 'by'), may hold values from 0 to 1, as said below
- block_counts: int32 [1024, 256], P('bx', 'by'), may hold values from 1 to 128
- gather_offsets: float32 [3, 524288], P(None, ('bx', 'by')), may hold values from 0 to 1, as said below
- gather_blocks: int32 [4, 524288], P(None, ('bx', 'by')), may hold values from 0 to 262143, as said below
- albedo: float32 [3, 524288], P(None, ('bx', 'by')), may hold values from 0.1 to 1
- gather_pixels: int32 [524288], P(('bx', 'by')), may hold values from 0 to 262143, as said below
- tile_slot: int32 [1024], replicated, may hold values from 0 to 1023, as said below
Outputs:
- film: float32 [3, 1024, 256], P(None, ('bx', 'by'))
Inputs may be any that keep to these rules, and one draw needn't show every extreme that they name: `photon_data`: per point and channel in cell units: entries 0 to 2 are a position in [0, 1), entries 3 to 5 a positive power. `gather_offsets`: each coordinate lies in [0, 1). `gather_blocks`: entry 0 is the point's own cell, inside the brick of the device that holds the point; the 4 entries are the four different cells of a 2 x 2 square of cells (periodic) that contains it. `gather_pixels`: in the rows of one device, at most 96 gather points lie in tiles whose slots s share s // 8; in every draw some such owner group receives exactly 96 from every device. `tile_slot`: A permutation of 0 to 1023.
All inputs are finite; a program needn't handle non-finite values.
Results may differ from a plain program's by a relative error of at most 0.0003.
Values sent between devices are 32-bit elements; how exact they have to be, the bound alone decides.
No kernel may reach another device: no remote copies, remote signals or barrier semaphores. Data moves between devices by JAX's collectives and lax.ppermute only.
A program may use at most 512 MiB of HBM per device.

v0:
```python
import jax
import jax.numpy as jnp
from jax import lax
from jax.sharding import Mesh
from jax.sharding import PartitionSpec as P

TILE_PIX = 256
BX = ("bx_0", "bx_1", "bx_2")
BY = ("by_0", "by_1")
BX_BY = ("bx_0", "bx_1", "bx_2", "by_0", "by_1")


RADIUS_SQ = 0.25


def extended(x, sides, width):
    for axis, dim in sides:
        peers, length = (lax.axis_size(axis), x.shape[dim])
        up = [(i, (i + 1) % peers) for i in range(peers)]
        down = [(j, i) for i, j in up]
        last = lax.slice_in_dim(x, length - width, length, axis=dim)
        initial = lax.slice_in_dim(x, 0, width, axis=dim)
        before = lax.ppermute(last, axis, up)
        after = lax.ppermute(initial, axis, down)
        x = jnp.concatenate([before, x, after], axis=dim)
    return x


def cut_along(x, dim, peers):
    before, after = (x.shape[:dim], x.shape[dim + 1 :])
    return jnp.moveaxis(x.reshape(*before, peers, -1, *after), dim, 0)


def edges_of(length, count):
    turn = length // count
    if turn >= 8:
        turn -= turn % 8
    return [turn * k for k in range(1, count)]


def sum_in_order(blocks, axes, sequence):
    inside = blocks.shape[1:]
    blocks = blocks.reshape(*(lax.axis_size(a) for a in axes), *inside)
    blocks = jnp.moveaxis(blocks, sequence, range(len(axes))).reshape(-1, *inside)
    for k in sequence:
        blocks = lax.psum_scatter(blocks, axes[k], scatter_dimension=0, tiled=True)
    return blocks[0]


def sum_all_axes(x, axes, dim):
    blocks = cut_along(x, dim, lax.axis_size(axes))
    cut = max(range(1, max(2, blocks.ndim - 1)), key=lambda d: blocks.shape[d])
    count, finished = (len(axes), [])
    for initial, share in enumerate(
        jnp.split(blocks, edges_of(blocks.shape[cut], count), axis=cut)
    ):
        if share.size:
            sequence = [(initial + k) % count for k in range(count)]
            finished.append(sum_in_order(share, axes, sequence))
    return jnp.concatenate(finished, axis=cut - 1)


def kernel_sum(blocks, shift_x, shift_y, offsets, albedo):
    delta_x = shift_x[:, :, None] + blocks[0] - offsets[0][:, None, None]
    delta_y = shift_y[:, :, None] + blocks[1] - offsets[1][:, None, None]
    delta_z = blocks[2] - offsets[2][:, None, None]
    dist_sq = delta_x * delta_x + delta_y * delta_y + delta_z * delta_z
    weight = jnp.maximum(1.0 - dist_sq / RADIUS_SQ, 0.0)
    sums = jnp.sum(weight[None] * blocks[3:6], axis=(2, 3))
    return albedo * sums


def per_device(
    photon_data, block_counts, gather_offsets, gather_blocks, albedo, gather_pixels, tile_slot
):
    cells_x, cells_y, slots = (photon_data.shape[1], photon_data.shape[2], photon_data.shape[3])
    span_x = lax.axis_size(BX)
    span_y = lax.axis_size(BY)
    grid_x = cells_x * span_x
    grid_y = cells_y * span_y
    occupied = (
        lax.broadcasted_iota(jnp.int32, (cells_x, cells_y, slots), 2) < block_counts[:, :, None]
    )
    photons = jnp.concatenate(
        [photon_data[:3], photon_data[3:] * occupied.astype(jnp.float32)[None]], axis=0
    )
    padded = extended(photons, ((BX, 1), (BY, 2)), 1)
    table = padded.reshape(6, (cells_x + 2) * (cells_y + 2), slots)
    first_x = lax.axis_index(BX) * cells_x
    first_y = lax.axis_index(BY) * cells_y
    local_x = (gather_blocks // grid_y - first_x + 1) % grid_x
    local_y = (gather_blocks % grid_y - first_y + 1) % grid_y
    shift_x = (local_x - local_x[:1]).astype(jnp.float32)
    shift_y = (local_y - local_y[:1]).astype(jnp.float32)
    index = local_x * (cells_y + 2) + local_y
    listed = gather_blocks.shape[0]
    points = gather_offsets.shape[1]
    group = min(512, points)
    groups = points // group
    idx_stack = index.reshape(listed, groups, group).transpose(1, 2, 0)
    sx_stack = shift_x.reshape(listed, groups, group).transpose(1, 2, 0)
    sy_stack = shift_y.reshape(listed, groups, group).transpose(1, 2, 0)
    off_stack = gather_offsets.reshape(3, groups, group).transpose(1, 0, 2)
    alb_stack = albedo.reshape(3, groups, group).transpose(1, 0, 2)

    def one_group(packed):
        idb, move_x, move_y, off, alb = packed
        blocks = jnp.take(table, idb.reshape(-1), axis=1).reshape(6, group, listed, slots)
        return kernel_sum(blocks, move_x, move_y, off, alb)

    rad = lax.map(one_group, (idx_stack, sx_stack, sy_stack, off_stack, alb_stack))
    radiance = rad.transpose(1, 0, 2).reshape(3, points)
    tiles = tile_slot.shape[0]
    tile = gather_pixels // TILE_PIX
    matched = tile[:, None] == jnp.arange(tiles, dtype=jnp.int32)[None, :]
    slot = jnp.sum(jnp.where(matched, tile_slot[None, :], 0), axis=1)
    within_tile = gather_pixels % TILE_PIX
    target = slot * TILE_PIX + within_tile
    partial_film = jnp.zeros((3, tiles * TILE_PIX), jnp.float32).at[:, target].add(radiance)
    partial_film = partial_film.reshape(3, tiles, TILE_PIX)
    return sum_all_axes(partial_film, BX_BY, 1)


def solution(mesh):
    split = Mesh(mesh.devices.reshape(4, 2, 2, 2, 4), ("bx_0", "bx_1", "bx_2", "by_0", "by_1"))
    in_specs = (
        P(None, BX, BY, None),
        P(BX, BY),
        P(None, BX_BY),
        P(None, BX_BY),
        P(None, BX_BY),
        P(BX_BY),
        P(),
    )
    out_specs = P(None, BX_BY, None)
    return jax.shard_map(
        per_device, mesh=split, in_specs=in_specs, out_specs=out_specs, check_vma=False
    )
```

profile of v0, /device:TPU:1, one launch (start us, length us, event | category | flops | bytes accessed | tf_op | source)
XLA Modules:
  0.0 1016.2 jit_solution(8119169532902245180)
XLA Ops:
  53.7 412.1 %while.10 = (s32[]{:T(128)}, f32[8,3,512]{2,1,0:T(4,128)S(1)}, f32[8,3,512]{2,1,0:T(4,128)}, f32[8,512,4]{2,1,0:T(8,128)}, s32[8,512,4]{2,1,0:T(8,128)}, /*index...) while((s32[]{:T(128)}, f32[8,3,512]{2,1,0:T(4,128)S(1)}, ...), condition=%wide.region_4.5_spmd, body=%wide.region_1.4_spmd.sunk | while | flops 6574084 | bytes 65403084 | solution.py:111
  54.9 19.5 %gather_fusion = f32[2048,6,128]{2,1,0:T(8,128)} fusion(f32[6,2244,128]{2,0,1:T(8,128)} %get-tuple-element.240, s32[2048]{0:T(1024)S(1)} %broadcast_clamp_fusion.3), kind=kCustom, calls=%fused_computation.clone.1 | custom fusion | bytes 12591104 | tf_op jit(solution)/shard_map/while/body/eval_jaxpr/jit(_take)/gather | solution.py:108
  74.5 11.2 %select_bitcast_fusion.2 = f32[6,2048,128]{2,0,1:T(8,128)S(1)} fusion(f32[2048,6,128]{2,1,0:T(8,128)} %gather_fusion, pred[2048]{0:T(1024)(128)(4,1)S(1)} %compare_and_fusion.2), kind=kLoop, calls=%fused_computation.3.clone.1 | loop fusion | flops 1572864 | bytes 12584960 | tf_op jit(solution)/shard_map/while/body/eval_jaxpr/jit(_take)/select_n | solution.py:108
  97.9 5.8 fusion.30
  106.4 19.5 %gather_fusion = f32[2048,6,128]{2,1,0:T(8,128)} fusion(f32[6,2244,128]{2,0,1:T(8,128)} %get-tuple-element.240, s32[2048]{0:T(1024)S(1)} %broadcast_clamp_fusion.3), kind=kCustom, calls=%fused_computation.clone.1 | custom fusion | bytes 12591104 | tf_op jit(solution)/shard_map/while/body/eval_jaxpr/jit(_take)/gather | solution.py:108
  126.0 11.2 %select_bitcast_fusion.2 = f32[6,2048,128]{2,0,1:T(8,128)S(1)} fusion(f32[2048,6,128]{2,1,0:T(8,128)} %gather_fusion, pred[2048]{0:T(1024)(128)(4,1)S(1)} %compare_and_fusion.2), kind=kLoop, calls=%fused_computation.3.clone.1 | loop fusion | flops 1572864 | bytes 12584960 | tf_op jit(solution)/shard_map/while/body/eval_jaxpr/jit(_take)/select_n | solution.py:108
  157.9 19.5 %gather_fusion = f32[2048,6,128]{2,1,0:T(8,128)} fusion(f32[6,2244,128]{2,0,1:T(8,128)} %get-tuple-element.240, s32[2048]{0:T(1024)S(1)} %broadcast_clamp_fusion.3), kind=kCustom, calls=%fused_computation.clone.1 | custom fusion | bytes 12591104 | tf_op jit(solution)/shard_map/while/body/eval_jaxpr/jit(_take)/gather | solution.py:108
  177.6 11.2 %select_bitcast_fusion.2 = f32[6,2048,128]{2,0,1:T(8,128)S(1)} fusion(f32[2048,6,128]{2,1,0:T(8,128)} %gather_fusion, pred[2048]{0:T(1024)(128)(4,1)S(1)} %compare_and_fusion.2), kind=kLoop, calls=%fused_computation.3.clone.1 | loop fusion | flops 1572864 | bytes 12584960 | tf_op jit(solution)/shard_map/while/body/eval_jaxpr/jit(_take)/select_n | solution.py:108
  209.4 19.5 %gather_fusion = f32[2048,6,128]{2,1,0:T(8,128)} fusion(f32[6,2244,128]{2,0,1:T(8,128)} %get-tuple-element.240, s32[2048]{0:T(1024)S(1)} %broadcast_clamp_fusion.3), kind=kCustom, calls=%fused_computation.clone.1 | custom fusion | bytes 12591104 | tf_op jit(solution)/shard_map/while/body/eval_jaxpr/jit(_take)/gather | solution.py:108
  229.1 11.2 %select_bitcast_fusion.2 = f32[6,2048,128]{2,0,1:T(8,128)S(1)} fusion(f32[2048,6,128]{2,1,0:T(8,128)} %gather_fusion, pred[2048]{0:T(1024)(128)(4,1)S(1)} %compare_and_fusion.2), kind=kLoop, calls=%fused_computation.3.clone.1 | loop fusion | flops 1572864 | bytes 12584960 | tf_op jit(solution)/shard_map/while/body/eval_jaxpr/jit(_take)/select_n | solution.py:108
  260.9 19.5 %gather_fusion = f32[2048,6,128]{2,1,0:T(8,128)} fusion(f32[6,2244,128]{2,0,1:T(8,128)} %get-tuple-element.240, s32[2048]{0:T(1024)S(1)} %broadcast_clamp_fusion.3), kind=kCustom, calls=%fused_computation.clone.1 | custom fusion | bytes 12591104 | tf_op jit(solution)/shard_map/while/body/eval_jaxpr/jit(_take)/gather | solution.py:108
  280.6 11.2 %select_bitcast_fusion.2 = f32[6,2048,128]{2,0,1:T(8,128)S(1)} fusion(f32[2048,6,128]{2,1,0:T(8,128)} %gather_fusion, pred[2048]{0:T(1024)(128)(4,1)S(1)} %compare_and_fusion.2), kind=kLoop, calls=%fused_computation.3.clone.1 | loop fusion | flops 1572864 | bytes 12584960 | tf_op jit(solution)/shard_map/while/body/eval_jaxpr/jit(_take)/select_n | solution.py:108
  312.4 19.5 %gather_fusion = f32[2048,6,128]{2,1,0:T(8,128)} fusion(f32[6,2244,128]{2,0,1:T(8,128)} %get-tuple-element.240, s32[2048]{0:T(1024)S(1)} %broadcast_clamp_fusion.3), kind=kCustom, calls=%fused_computation.clone.1 | custom fusion | bytes 12591104 | tf_op jit(solution)/shard_map/while/body/eval_jaxpr/jit(_take)/gather | solution.py:108
  332.1 11.2 %select_bitcast_fusion.2 = f32[6,2048,128]{2,0,1:T(8,128)S(1)} fusion(f32[2048,6,128]{2,1,0:T(8,128)} %gather_fusion, pred[2048]{0:T(1024)(128)(4,1)S(1)} %compare_and_fusion.2), kind=kLoop, calls=%fused_computation.3.clone.1 | loop fusion | flops 1572864 | bytes 12584960 | tf_op jit(solution)/shard_map/while/body/eval_jaxpr/jit(_take)/select_n | solution.py:108
  363.9 19.5 %gather_fusion = f32[2048,6,128]{2,1,0:T(8,128)} fusion(f32[6,2244,128]{2,0,1:T(8,128)} %get-tuple-element.240, s32[2048]{0:T(1024)S(1)} %broadcast_clamp_fusion.3), kind=kCustom, calls=%fused_computation.clone.1 | custom fusion | bytes 12591104 | tf_op jit(solution)/shard_map/while/body/eval_jaxpr/jit(_take)/gather | solution.py:108
  383.6 11.2 %select_bitcast_fusion.2 = f32[6,2048,128]{2,0,1:T(8,128)S(1)} fusion(f32[2048,6,128]{2,1,0:T(8,128)} %gather_fusion, pred[2048]{0:T(1024)(128)(4,1)S(1)} %compare_and_fusion.2), kind=kLoop, calls=%fused_computation.3.clone.1 | loop fusion | flops 1572864 | bytes 12584960 | tf_op jit(solution)/shard_map/while/body/eval_jaxpr/jit(_take)/select_n | solution.py:108
  415.4 19.5 %gather_fusion = f32[2048,6,128]{2,1,0:T(8,128)} fusion(f32[6,2244,128]{2,0,1:T(8,128)} %get-tuple-element.240, s32[2048]{0:T(1024)S(1)} %broadcast_clamp_fusion.3), kind=kCustom, calls=%fused_computation.clone.1 | custom fusion | bytes 12591104 | tf_op jit(solution)/shard_map/while/body/eval_jaxpr/jit(_take)/gather | solution.py:108
  435.1 11.2 %select_bitcast_fusion.2 = f32[6,2048,128]{2,0,1:T(8,128)S(1)} fusion(f32[2048,6,128]{2,1,0:T(8,128)} %gather_fusion, pred[2048]{0:T(1024)(128)(4,1)S(1)} %compare_and_fusion.2), kind=kLoop, calls=%fused_computation.3.clone.1 | loop fusion | flops 1572864 | bytes 12584960 | tf_op jit(solution)/shard_map/while/body/eval_jaxpr/jit(_take)/select_n | solution.py:108
  466.4 97.2 %scatter_custom_fusion = f32[3,262144]{0,1:T(8,128)} fusion(s32[4096]{0:T(1024)} %get-tuple-element.80, f32[]{:T(128)} %constant.118.clone.1, f32[4096,3]{1,0:T(8,128)S(1)} %copy.81, s32[4096]{0:T(1024)S(1)} %broadcast_clamp_fusion.1), kind=kCustom, calls=%fused_computation.19 | custom fusion | flops 12288 | bytes 3146240 | tf_op jit(solution)/shard_map/scatter-add | solution.py:119
  563.7 69.1 %copy.82 = f32[3,128,8,256]{3,0,2,1:T(4,128)} copy(f32[3,128,8,256]{0,3,2,1:T(8,128)} %bitcast.26) | data formatting | bytes 6291456 | tf_op jit(solution)/shard_map/reshape;reshape | solution.py:31
  638.7 36.6 %all-reduce.44.cloned.1.call-done = f32[128,3,1,256]{3,1,2,0:T(4,128)} async-done(((f32[128,3,1,256]{3,1,2,0:T(4,128)}), f32[128,3,1,256]{3,1,2,0:T(4,128)}) %all-reduce.44.cloned.1.call-update) | async-done | bytes 393232
  680.0 24.1 %all-reduce.56.cloned.1.call-done = (f32[128,3,1,256]{3,1,2,0:T(4,128)}, f32[64,3,1,256]{3,1,2,0:T(4,128)}) async-done(((f32[128,3,1,256]{3,1,2,0:T(4,128)}, f32[64,3,1,256]{3,1,2,0:T(4,128)}), (f32[128,3,1,256]{3,1,2,0:T(4,128)}, f32[64,3,1,256]{3,1,2,0:T(4,128)})) %all-reduce.56.cloned.1.call-update) | async-done | bytes 589840
  713.2 40.5 %all-reduce.52.cloned.1.call-done = (f32[64,3,1,256]{3,1,2,0:T(4,128)}, f32[128,3,1,256]{3,1,2,0:T(4,128)}, f32[32,3,1,256]{3,1,2,0:T(4,128)}) async-done(((f32[64,3,1,256]{3,1,2,0:T(4,128)}, f32[128,3,1,256]{3,1,2,0:T(4,128)}, f32[32,3,1,256]{3,1,2,0:T(4,128)}), (f32[64,3,1,256]{3,1,2,0:T(4,128)}, f32[128,3,1,256]{3,1,2,0:T(4,128)}, f32[32,3,1,256]{3,1,2,0:T(4,128)})) %all-reduce.52.cloned.1.call-update) | async-done | bytes 688144
  758.3 54.7 %all-reduce.46.cloned.1.call-done = (f32[32,3,1,256]{3,1,2,0:T(4,128)}, f32[64,3,1,256]{3,1,2,0:T(4,128)}, f32[128,3,4,256]{3,2,1,0:T(4,128)}) async-done(((f32[32,3,1,256]{3,1,2,0:T(4,128)}, f32[64,3,1,256]{3,1,2,0:T(4,128)}, f32[128,3,4,256]{3,2,1,0:T(4,128)}), (f32[32,3,1,256]{3,1,2,0:T(4,128)}, f32[64,3,1,256]{3,1,2,0:T(4,128)}, f32[128,3,4,256]{3,2,1,0:T(4,128)})) %all-reduce.46.cloned.1.call-update) | async-done | bytes 1867792
  824.7 33.7 %all-reduce.50.cloned.1.call-done = (f32[128,3,1,256]{3,1,2,0:T(4,128)}, f32[32,3,4,256]{3,2,1,0:T(4,128)}) async-done(((f32[128,3,1,256]{3,1,2,0:T(4,128)}, f32[32,3,4,256]{3,2,1,0:T(4,128)}), (f32[128,3,1,256]{3,1,2,0:T(4,128)}, f32[32,3,4,256]{3,2,1,0:T(4,128)})) %all-reduce.50.cloned.1.call-update) | async-done | bytes 786448
  863.1 30.6 %all-reduce.58.cloned.1.call-done = (f32[32,3,1,256]{3,1,2,0:T(4,128)}, f32[8,3,4,256]{3,2,1,0:T(4,128)}) async-done(((f32[32,3,1,256]{3,1,2,0:T(4,128)}, f32[8,3,4,256]{3,2,1,0:T(4,128)}), (f32[32,3,1,256]{3,1,2,0:T(4,128)}, f32[8,3,4,256]{3,2,1,0:T(4,128)})) %all-reduce.58.cloned.1.call-update) | async-done | bytes 196624
  898.1 24.2 %all-reduce.54.cloned.1.call-done = (f32[16,3,1,256]{3,1,2,0:T(4,128)}, f32[4,3,4,256]{3,2,1,0:T(4,128)}) async-done(((f32[16,3,1,256]{3,1,2,0:T(4,128)}, f32[4,3,4,256]{3,2,1,0:T(4,128)}), (f32[16,3,1,256]{3,1,2,0:T(4,128)}, f32[4,3,4,256]{3,2,1,0:T(4,128)})) %all-reduce.54.cloned.1.call-update) | async-done | bytes 98320
  923.8 10.0 all-reduce.29
  933.8 14.1 %all-reduce.25 = (f32[4,3,1,256]{3,1,2,0:T(4,128)S(1)}, f32[16,3,1,256]{3,1,2,0:T(4,128)S(1)}) all-reduce(f32[4,3,1,256]{3,1,2,0:T(4,128)S(1)} %constant_dynamic-slice_fusion.26, f32[16,3,1,256]{3,1,2,0:T(4,128)S(1)} %constant_dynamic-slice_fusion.22), channel_id=6, replica_groups=mesh['bx_0'=4,'bx_1'=2,'bx_2'=2,'by_0'=2,'by_1'=4] {'by_1'}, use_global_device_ids=true, to_apply=%region_10.11.clone | all-reduce | flops 15360 | bytes 122880
  949.8 40.9 %all-reduce.48.cloned.1.call-done = (f32[4,3,1,256]{3,1,2,0:T(4,128)}, f32[8,3,1,256]{3,1,2,0:T(4,128)}, f32[16,3,1,256]{3,1,2,0:T(4,128)}) async-done(((f32[4,3,1,256]{3,1,2,0:T(4,128)}, f32[8,3,1,256]{3,1,2,0:T(4,128)}, f32[16,3,1,256]{3,1,2,0:T(4,128)}), (f32[4,3,1,256]{3,1,2,0:T(4,128)}, f32[8,3,1,256]{3,1,2,0:T(4,128)}, f32[16,3,1,256]{3,1,2,0:T(4,128)})) %all-reduce.48.cloned.1.call-update) | async-done | bytes 86032
  992.2 6.3 all-reduce.33
  998.5 7.1 all-reduce.19
  (306 shorter events, 247.5 us)
Async XLA Ops:
  6.5 668.8 %all-reduce.44.cloned.1.call-start = ((), (), s32[]{:S(2)}) async-start(), calls=%async_computation | async-start | bytes 1048576
  11.4 1.6 copy-start.1
  11.4 5.3 copy-start.6
  11.4 5.6 copy-start.4
  13.8 19.5 %collective-permute-start = (f32[6,1,32,128]{3,2,1,0:T(8,128)}, f32[6,1,32,128]{3,2,1,0:T(8,128)S(1)}, u32[]{:S(2)}, u32[]{:S(2)}) collective-permute-start(f32[6,1,32,128]{3,2,1,0:T(8,128)} %get-tuple-element.134), channel_id=1, source_target_pairs={{0,8},{8,16},{16,24},{24,32},{32,40},{40,48},{48,56},{56,64},{64,7... | collective-permute-start | bytes 294920 | tf_op jit(solution)/shard_map/ppermute | solution.py:23
  16.8 16.5 %collective-permute-start.1 = (f32[6,1,32,128]{3,2,1,0:T(8,128)}, f32[6,1,32,128]{3,2,1,0:T(8,128)S(1)}, u32[]{:S(2)}, u32[]{:S(2)}) collective-permute-start(f32[6,1,32,128]{3,2,1,0:T(8,128)} %get-tuple-element.135), channel_id=1, source_target_pairs={{8,0},{16,8},{24,16},{32,24},{40,32},{48,40},{56,48},{64,56},{72,6... | collective-permute-start | bytes 294920 | tf_op jit(solution)/shard_map/ppermute | solution.py:24
  21.5 6.0 copy-start.5
  33.3 11.5 %copy-start.2 = (f32[3,64,32,128]{3,2,1,0:T(8,128)S(1)}, f32[3,64,32,128]{3,2,1,0:T(8,128)}, u32[]{:S(2)}) copy-start(f32[3,64,32,128]{3,2,1,0:T(8,128)} %copy-done.1) | copy-start | bytes 9437188
  35.2 9.1 collective-permute-start.2
  36.5 8.0 collective-permute-start.3
  47.9 5.8 copy-start.3
  85.7 3.3 copy-start
  137.3 3.3 copy-start
  188.8 3.3 copy-start
  240.3 3.3 copy-start
  291.8 3.3 copy-start
  343.3 3.3 copy-start
  394.8 3.3 copy-start
  446.3 3.3 copy-start
  632.8 3.8 copy-start.12
  632.8 44.3 %copy-start.11 = (u32[128]{0:T(128)S(1)}, u32[128]{0:T(128)}, u32[]{:S(2)}) copy-start(u32[128]{0:T(128)} %constant.148) | copy-start | bytes 1540
  635.5 71.9 %copy-start.10 = (u32[128]{0:T(128)S(1)}, u32[128]{0:T(128)}, u32[]{:S(2)}) copy-start(u32[128]{0:T(128)} %constant.152) | copy-start | bytes 1540
  636.5 67.6 %all-reduce.56.cloned.1.call-start = ((), (), s32[]{:S(2)}) async-start(), calls=%async_computation.6 | async-start | bytes 1572864
  677.1 76.6 %all-reduce.52.cloned.1.call-start = ((), (), s32[]{:S(2)}) async-start(), calls=%async_computation.4 | async-start | bytes 1835008
  707.4 105.6 %all-reduce.46.cloned.1.call-start = ((), (), s32[]{:S(2)}) async-start(), calls=%async_computation.1 | async-start | bytes 3932160
  711.5 45.6 %copy-start.9 = (u32[128]{0:T(128)S(1)}, u32[128]{0:T(128)}, u32[]{:S(2)}) copy-start(u32[128]{0:T(128)} %constant.156) | copy-start | bytes 1540
  711.5 103.4 %copy-start.8 = (u32[128]{0:T(128)S(1)}, u32[128]{0:T(128)}, u32[]{:S(2)}) copy-start(u32[128]{0:T(128)} %constant.140) | copy-start | bytes 1540
  753.7 107.9 %copy-start.7 = (f32[32,3,1,256]{3,1,2,0:T(4,128)S(1)}, f32[32,3,1,256]{3,1,2,0:T(4,128)}, u32[]{:S(2)}) copy-start(f32[32,3,1,256]{3,1,2,0:T(4,128)} %get-tuple-element.112) | copy-start | bytes 294916
  757.0 101.4 %all-reduce.50.cloned.1.call-start = ((), (), s32[]{:S(2)}) async-start(), calls=%async_computation.3 | async-start | bytes 1835008
  814.8 79.0 %all-reduce.58.cloned.1.call-start = ((), (), s32[]{:S(2)}) async-start(), calls=%async_computation.7 | async-start | bytes 458752
  861.6 60.7 %all-reduce.54.cloned.1.call-start = ((), (), s32[]{:S(2)}) async-start(), calls=%async_computation.5 | async-start | bytes 229376
  896.7 94.1 %all-reduce.48.cloned.1.call-start = ((), (), s32[]{:S(2)}) async-start(), calls=%async_computation.2 | async-start | bytes 229376
Sparse Core Ops, SparseCore 0:
  636.6 38.6 all-reduce.43
  677.8 26.1 all-reduce.55
  707.5 46.1 all-reduce.51
  757.2 55.7 all-reduce.45
  815.3 43.1 all-reduce.49
  861.7 32.0 all-reduce.57
  896.8 25.4 all-reduce.53
  949.2 41.4 all-reduce.47
where the time goes:
time: 1030 us; the launch traced here: 1020 us
  local copies, waits for them, and re-layouts  373 us (36%)
  waiting for transfers between devices  288 us (28%)
  other arithmetic  279 us (27%)
  blocking collectives  37.5 us (4%)
  between operations  27.4 us (3%)
    unnamed x16, waiting for transfers between devices  285 us
    gather x8, local copies, waits for them, and re-layouts, one_group(): jnp.take(table, idb.reshape(-1), axis=1).reshape(6, group, listed, slots)  156 us
    scatter-add x3, other arithmetic, per_device(): jnp.zeros((3, tiles * TILE_PIX), jnp.float32).at[:, target].add(radiance)  103 us
    select_n x16, other arithmetic, one_group(): jnp.take(table, idb.reshape(-1), axis=1).reshape(6, group, listed, slots)  89.7 us
    another operation x1, local copies, waits for them, and re-layouts, cut_along(): return jnp.moveaxis(x.reshape(*before, peers, -1, *after), dim, 0)  69.1 us
    reduce_sum x16, other arithmetic, kernel_sum(): sums = jnp.sum(weight[None] * blocks[3:6], axis=(2, 3))  51.5 us
    unnamed x4, blocking collectives  37.5 us
    unnamed x50, local copies, waits for them, and re-layouts  28.1 us
  transfers between devices with their start and end apart: 12, of which 9 were waited for; matrix products, arithmetic and copies ran while one was open for 3% of the time, Pallas kernels for 0%

commit v1 on v0

v1 whole, which is shorter than its diff:
```python
import jax
import jax.numpy as jnp
from jax import lax
from jax.experimental import pallas as pl
from jax.experimental.pallas import tpu as pltpu
from jax.sharding import PartitionSpec as P

AXES = ("bx", "by")
CX, CY = 64, 32
EX, EY = CX + 2, CY + 2
NXC, NYC = 1024, 256
LANES = 128
POINTS = 4096
ROWS = POINTS // LANES
CAP = 96
OWNERS = 128
COMP = 2 * EY
PAIR = 6 * COMP
FRONT = 8
TABLE_ROWS = FRONT + (CX + 1) * PAIR + 16
GROUPS = 4
i32, f32, bf16 = jnp.int32, jnp.float32, jnp.bfloat16
VMEM = pl.BlockSpec(memory_space=pltpu.VMEM)
SMEM = pl.BlockSpec(memory_space=pltpu.SMEM)
NT = (((1,), (1,)), ((), ()))


def params():
    return pltpu.CompilerParams(vmem_limit_bytes=60 * 1024 * 1024)


def iota(shape, dim):
    return lax.broadcasted_iota(i32, shape, dim)


def lane_take(x, idx):
    return jnp.take_along_axis(x, idx, axis=1, mode="promise_in_bounds")


def prep_kernel(first, blocks, offs, pix, tile_slot, start, rel, owner, rank, target, sb, so):
    for k in range(4):
        for r in range(ROWS):
            sb[k, r : r + 1, :] = blocks[k : k + 1, r * LANES : (r + 1) * LANES]
    for c in range(3):
        for r in range(ROWS):
            so[c, r : r + 1, :] = offs[c : c + 1, r * LANES : (r + 1) * LANES]
    fx, fy = first[0], first[1]
    lx = [((sb[k] >> 8) - fx + 1) & (NXC - 1) for k in range(4)]
    ly = [((sb[k] & (NYC - 1)) - fy + 1) & (NYC - 1) for k in range(4)]
    qx = jnp.minimum(jnp.minimum(lx[0], lx[1]), jnp.minimum(lx[2], lx[3]))
    qy = jnp.minimum(jnp.minimum(ly[0], ly[1]), jnp.minimum(ly[2], ly[3]))
    odd = (iota((ROWS, LANES), 0) >> 2) & 1
    start[...] = FRONT + qx * PAIR + qy * 2 - 4 * odd
    rel[0] = 2.0 * (so[0] + (lx[0] - qx).astype(f32))
    rel[1] = 2.0 * (so[1] + (ly[0] - qy).astype(f32))
    rel[2] = 2.0 * so[2]
    for i in range(ROWS // 8):
        p = pix[8 * i : 8 * i + 8, :]
        tile = p >> 8
        low, high = tile & (LANES - 1), tile >> 7
        slot = jnp.zeros((8, LANES), i32)
        for t in range(8):
            row = jnp.broadcast_to(tile_slot[t : t + 1, :], (8, LANES))
            slot = jnp.where(high == t, lane_take(row, low), slot)
        owner[8 * i : 8 * i + 8, :] = slot >> 3
        target[8 * i : 8 * i + 8, :] = (slot & 7) * 256 + (p & 255)
    sub = iota((OWNERS, LANES), 0)
    upper = (iota((LANES, 2 * LANES), 0) <= iota((LANES, 2 * LANES), 1)).astype(f32).astype(bf16)

    def step(r, seen):
        hit = sub == jnp.broadcast_to(owner[pl.ds(r, 1), :], (OWNERS, LANES))
        counts = jnp.dot(jnp.where(hit, 1.0, 0.0).astype(bf16), upper, preferred_element_type=f32)
        rank[pl.ds(r, 1), :] = (
            jnp.sum(jnp.where(hit, counts[:, :LANES] + seen, 0.0), axis=0, keepdims=True) - 1.0
        ).astype(i32)
        return seen + counts[:, LANES:]

    lax.fori_loop(0, ROWS, step, jnp.zeros((OWNERS, LANES), f32), unroll=4)


def main_kernel(start, ph, counts, xm, xp, ym, yp, rel, alb, owner, rank, target, send, table, wide, prod, sums, rad):
    lane = iota((CY, LANES), 1)

    def put(c, x, value):
        table[pl.ds(FRONT + (x + 1) * PAIR + c * COMP + 2, CY, stride=2), :] = value
        table[pl.ds(FRONT + x * PAIR + c * COMP + 3, CY, stride=2), :] = value

    def column(x, _):
        at = jnp.full((CY, LANES), x, i32)
        live = lane < lane_take(counts[...], at)
        for c in range(6):
            v = ph[c, x]
            put(c, x, v + v if c < 3 else jnp.where(live, v, 0.0))
        return 0

    lax.fori_loop(0, CX, column, 0, unroll=2)
    for c in range(6):
        scale = 2.0 if c < 3 else 1.0
        table[pl.ds(FRONT + c * COMP + 2, CY, stride=2), :] = xm[c] * scale
        table[pl.ds(FRONT + CX * PAIR + c * COMP + 3, CY, stride=2), :] = xp[c] * scale
        for side, at in ((ym, 0), (yp, 2 * EY - 2)):
            table[pl.ds(FRONT + c * COMP + at, CX + 1, stride=PAIR), :] = side[c, : CX + 1] * scale
            table[pl.ds(FRONT + c * COMP + at + 1, CX + 1, stride=PAIR), :] = side[c, 1:] * scale
    sub = iota((8, LANES), 0)
    upper = sub < 4
    place = ((sub & 1).astype(f32) * 2.0, ((sub >> 1) & 1).astype(f32) * 2.0, None)
    for v in range(4):
        for c in range(3):
            for p in range(4):
                a = jnp.broadcast_to(rel[c, 8 * p + v : 8 * p + v + 1, :], (8, LANES))
                b = jnp.broadcast_to(rel[c, 8 * p + 4 + v : 8 * p + 5 + v, :], (8, LANES))
                both = jnp.where(upper, a, b)
                wide[v, c, p] = both if place[c] is None else both - place[c]

    def block(v, _):
        def groups(g, _):
            for u in range(GROUPS):
                L = g * GROUPS + u
                at = jnp.full((8, LANES), L, i32)
                rows = [start[s * 512 + v * LANES + L] for s in range(8)]
                for p in range(4):
                    ra, rb = rows[2 * p], rows[2 * p + 1]

                    def load(c):
                        return jnp.where(
                            upper, table[pl.ds(ra + c * COMP, 8), :], table[pl.ds(rb + c * COMP, 8), :]
                        )

                    d = [load(c) - lane_take(wide[v, c, p], at) for c in range(3)]
                    dist = d[0] * d[0] + d[1] * d[1] + d[2] * d[2]
                    weight = jnp.maximum(1.0 - dist, 0.0)
                    for c in range(3):
                        prod[u, c, 8 * p : 8 * p + 8, :] = weight * load(3 + c)
                for c in range(3):
                    part = [prod[u, c, pl.ds(i, 8, stride=4), :] for i in range(4)]
                    sums[c, L] = (part[0] + part[1]) + (part[2] + part[3])
            return 0

        lax.fori_loop(0, LANES // GROUPS, groups, 0)
        lanes = iota((8, LANES), 1)

        def reduce(c, first, size):
            if size == 1:
                return sums[c, first]
            half = size // 2
            a, b = reduce(c, first, half), reduce(c, first + half, half)
            mine = (lanes & half) == 0
            return jnp.where(mine, a, b) + pltpu.roll(jnp.where(mine, b, a), half, 1)

        def channel(c, _):
            rad[c, pl.ds(v, 8, stride=4), :] = reduce(c, 0, LANES)
            return 0

        lax.fori_loop(0, 3, channel, 0)
        return 0

    lax.fori_loop(0, 4, block, 0)
    for c in range(3):
        for r in range(ROWS):
            rad[c, r : r + 1, :] = rad[c, r : r + 1, :] * alb[c : c + 1, r * LANES : (r + 1) * LANES]
    wide_sub = iota((OWNERS, 2 * LANES), 0)
    rank_sub = iota((CAP, 2 * LANES), 0)

    def two(ref, r):
        return jnp.concatenate([ref[pl.ds(2 * r, 1), :], ref[pl.ds(2 * r + 1, 1), :]], axis=1)

    def scatter(r, total):
        mine = jnp.where(wide_sub == two(owner, r), 1.0, 0.0).astype(bf16)
        hit = rank_sub == two(rank, r)
        where = two(target, r)
        vals = [two(rad.at[c], r) for c in range(3)]
        high = [x.astype(bf16).astype(f32) for x in vals]
        low = [x - h for x, h in zip(vals, high)]
        high.append((where & ~255).astype(f32))
        low.append((where & 255).astype(f32))
        for part in (high, low):
            rows = jnp.concatenate([jnp.where(hit, x, 0.0) for x in part], axis=0).astype(bf16)
            total = total + lax.dot_general(mine, rows, NT, preferred_element_type=f32)
        return total

    send[...] = lax.fori_loop(0, ROWS // 2, scatter, jnp.zeros((OWNERS, 4 * CAP), f32), unroll=2)


def film_kernel(got, film, flipped, total):
    for j in range(3):
        flipped[LANES * j : LANES * j + LANES, :] = jnp.transpose(got[:, LANES * j : LANES * j + LANES])
    lo_sub = iota((LANES, 2 * LANES), 0)
    hi_sub = iota((16, 2 * LANES), 0)

    def two(row):
        return jnp.concatenate(
            [flipped[pl.ds(row, 1), :], flipped[pl.ds(row + CAP // 2, 1), :]], axis=1
        )

    def step(k, acc):
        where = two(3 * CAP + k).astype(i32)
        low_hit = jnp.where(lo_sub == (where & 127), 1.0, 0.0).astype(bf16)
        hit = hi_sub == (where >> 7)
        high, low = [], []
        for c in range(3):
            x = two(c * CAP + k)
            h = x.astype(bf16).astype(f32)
            high.append(jnp.where(hit, h, 0.0))
            low.append(jnp.where(hit, x - h, 0.0))
        rows = jnp.concatenate(high + low, axis=0).astype(bf16)
        return acc + lax.dot_general(rows, low_hit, NT, preferred_element_type=f32)

    acc = lax.fori_loop(0, CAP // 2, step, jnp.zeros((96, LANES), f32), unroll=4)
    total[...] = acc[:48] + acc[48:]
    for c in range(3):
        film[c, :, :LANES] = total[pl.ds(16 * c, 8, stride=2), :]
        film[c, :, LANES:] = total[pl.ds(16 * c + 1, 8, stride=2), :]


def shift(x, axis, by):
    n = lax.axis_size(axis)
    return lax.ppermute(x, axis, [(i, (i + by) % n) for i in range(n)])


def live_only(x, counts):
    slots = lax.broadcasted_iota(i32, x.shape[1:], x.ndim - 2)
    return jnp.concatenate([x[:3], jnp.where(slots < counts[..., None], x[3:], 0.0)], axis=0)


def per_device(photon_data, block_counts, gather_offsets, gather_blocks, albedo, gather_pixels, tile_slot):
    first = jnp.stack([lax.axis_index("bx") * CX, lax.axis_index("by") * CY]).astype(i32)
    xm = shift(live_only(photon_data[:, -1], block_counts[-1]), "bx", 1)
    xp = shift(live_only(photon_data[:, 0], block_counts[0]), "bx", -1)
    top = live_only(photon_data[:, :, -1], block_counts[:, -1])
    bottom = live_only(photon_data[:, :, 0], block_counts[:, 0])
    ym = shift(jnp.concatenate([xm[:, -1:], top, xp[:, -1:]], axis=1), "by", 1)
    yp = shift(jnp.concatenate([xm[:, :1], bottom, xp[:, :1]], axis=1), "by", -1)
    small_i = jax.ShapeDtypeStruct((ROWS, LANES), i32)
    start, rel, owner, rank, target = pl.pallas_call(
        prep_kernel,
        in_specs=[SMEM, VMEM, VMEM, VMEM, VMEM],
        out_specs=[VMEM] * 5,
        out_shape=[small_i, jax.ShapeDtypeStruct((3, ROWS, LANES), f32), small_i, small_i, small_i],
        scratch_shapes=[pltpu.VMEM((4, ROWS, LANES), i32), pltpu.VMEM((3, ROWS, LANES), f32)],
        compiler_params=params(),
        cost_estimate=pl.CostEstimate(flops=20_000_000, bytes_accessed=300_000, transcendentals=0),
        name="prep",
    )(first, gather_blocks, gather_offsets, gather_pixels.reshape(ROWS, LANES), tile_slot.reshape(8, LANES))
    counts = jnp.pad(block_counts.T, ((0, 0), (0, LANES - CX)))
    send = pl.pallas_call(
        main_kernel,
        in_specs=[SMEM] + [VMEM] * 11,
        out_specs=VMEM,
        out_shape=jax.ShapeDtypeStruct((OWNERS, 4 * CAP), f32),
        scratch_shapes=[
            pltpu.VMEM((TABLE_ROWS, LANES), f32),
            pltpu.VMEM((4, 3, 4, 8, LANES), f32),
            pltpu.VMEM((GROUPS, 3, 32, LANES), f32),
            pltpu.VMEM((3, LANES, 8, LANES), f32),
            pltpu.VMEM((3, ROWS, LANES), f32),
        ],
        compiler_params=params(),
        name="radiance",
    )(start.reshape(POINTS), photon_data, counts, xm, xp, ym, yp, rel, albedo, owner, rank, target)
    got = lax.all_to_all(send, AXES, 0, 0, tiled=True)
    return pl.pallas_call(
        film_kernel,
        in_specs=[VMEM],
        out_specs=VMEM,
        out_shape=jax.ShapeDtypeStruct((3, 8, 256), f32),
        scratch_shapes=[pltpu.VMEM((4 * CAP, LANES), f32), pltpu.VMEM((48, LANES), f32)],
        compiler_params=params(),
        name="film",
    )(got)


def solution(mesh):
    in_specs = (P(None, "bx", "by", None), P("bx", "by"), P(None, AXES), P(None, AXES), P(None, AXES), P(AXES), P())
    return jax.shard_map(per_device, mesh=mesh, in_specs=in_specs, out_specs=P(None, AXES, None), check_vma=False)
```

time: 1030 us -> 88.3 us (0.09); the launches traced: 1020 us -> 87.8 us
  local copies, waits for them, and re-layouts: 373 us -> 8.57 us
  waiting for transfers between devices: 288 us -> 6.02 us
  other arithmetic: 279 us -> 1.7 us
  Pallas kernels: 0 us -> 46.4 us
  between operations: 27.4 us -> 0.12 us
  blocking collectives: 37.5 us -> 15.7 us
    unnamed x16 -> x0, waiting for transfers between devices: 285 us -> none
    gather x8 -> x0, local copies, waits for them, and re-layouts: 156 us -> none  [one_group(): jnp.take(table, idb.reshape(-1), axis=1).reshape(6, group, listed, slots)]
    scatter-add x3 -> x0, other arithmetic: 103 us -> none  [per_device(): jnp.zeros((3, tiles * TILE_PIX), jnp.float32).at[:, target].add(radiance)]
    select_n x18 -> x3, other arithmetic: 90.4 us -> 0.87 us  [live_only(): jnp.where(slots < counts[..., None], x[3:], 0.0)]
    another operation x1 -> x0, local copies, waits for them, and re-layouts: 69.1 us -> none  [cut_along(): return jnp.moveaxis(x.reshape(*before, peers, -1, *after), dim, 0)]
    reduce_sum x17 -> x0, other arithmetic: 55.3 us -> none  [the longest x16 51.5 us: kernel_sum(): sums = jnp.sum(weight[None] * blocks[3:6], axis=(2, 3))]
    pallas_call x0 -> x3, Pallas kernels: none -> 46.4 us  [the longest x1 38.4 us: per_device(): pl.pallas_call(main_kernel, in_specs=[SMEM] + [VMEM] * 11, out_specs=VMEM...]
    unnamed x4 -> x0, blocking collectives: 37.5 us -> none
  transfers between devices with their start and end apart: 12 -> 4, of which waited for: 9 -> 2; matrix products, arithmetic and copies ran while one was open for 3% -> 6% of each run, Pallas kernels for 0% -> 4%
where the time goes in v1:
time: 88.3 us; the launch traced here: 87.8 us
  Pallas kernels  46.4 us (53%)
  blocking collectives  15.7 us (18%)
  starting transfers between devices  9.34 us (11%)
  local copies, waits for them, and re-layouts  8.57 us (10%)
  waiting for transfers between devices  6.02 us (7%)
  other arithmetic  1.7 us (2%)
    pallas_call x1, Pallas kernels, per_device(): pl.pallas_call(main_kernel, in_specs=[SMEM] + [VMEM] * 11, out_specs=VMEM...  38.4 us
    all_to_all x1, blocking collectives, per_device(): got = lax.all_to_all(send, AXES, 0, 0, tiled=True)  15.7 us
    ppermute x4, starting transfers between devices, shift(): return lax.ppermute(x, axis, [(i, (i + by) % n) for i in range(n)])  9.34 us
    ppermute x4, waiting for transfers between devices, shift(): return lax.ppermute(x, axis, [(i, (i + by) % n) for i in range(n)])  6.02 us
    pallas_call x1, Pallas kernels, per_device(): pl.pallas_call(film_kernel, in_specs=[VMEM], out_specs=VMEM, out_shape=ja...  4.5 us
    pallas_call x1, Pallas kernels, per_device(): pl.pallas_call(prep_kernel, in_specs=[SMEM, VMEM, VMEM, VMEM, VMEM], out_...  3.45 us
    slice x2, local copies, waits for them, and re-layouts, live_only(): x[:3]  3.02 us
  transfers between devices with their start and end apart: 4, of which 2 were waited for; matrix products, arithmetic and copies ran while one was open for 6% of the time, Pallas kernels for 4%

profile of v1, /device:TPU:1, one launch (start us, length us, event | category | flops | bytes accessed | tf_op | source)
XLA Modules:
  0.0 87.8 jit_solution(11139109613346021265)
XLA Ops:
  0.0 1.0 %slice_reduce_fusion = (s32[32]{0:T(128)S(1)}, s32[32]{0:T(128)S(1)}) fusion(s32[64,32]{0,1:T(8,128)} %param.8), kind=kLoop, calls=%fused_computation.13 | loop fusion | bytes 512 | tf_op jit(solution)/shard_map/slice | solution.py:228
  1.0 0.8 slice_bitcast_fusion
  1.8 0.1 iota_compare_fusion.2
  1.9 0.8 bitcast_select_fusion
  2.7 3.1 %collective-permute-start = (f32[6,32,128]{2,1,0:T(8,128)S(1)}, f32[6,32,128]{2,1,0:T(8,128)S(1)}, u32[]{:S(2)}, u32[]{:S(2)}) collective-permute-start(f32[6,32,128]{2,1,0:T(8,128)S(1)} %pad_maximum_fusion.2), channel_id=1, source_target_pairs={{0,8},{8,16},{16,24},{24,32},{32,40},{40,48},{48,56},{56,64},{64,7... | collective-permute-start | bytes 294920 | tf_op jit(solution)/shard_map/ppermute | solution.py:217
  5.8 0.1 collective-permute-start.1
  5.9 2.2 %fusion = (f32[3,64,1,128]{3,2,1,0:T(1,128)S(1)}, f32[3,64,1,128]{3,2,1,0:T(1,128)S(1)}, f32[3,64,1,128]{3,2,1,0:T(1,128)S(1)}, f32[3,64,1,128]{3,2,1,0:T(1,128)S(1)}) fusion(f32[6,64,32,128]{3,2,1,0:T(8,128)} %ph.1), kind=kLoop, calls=%fused_computation.20 | loop fusion | bytes 786432 | tf_op jit(solution)/shard_map/slice | solution.py:222
  8.1 0.7 slice_bitcast_fusion.2
  8.8 0.1 iota_compare_fusion
  8.9 0.0 collective-permute-done.xm
  9.0 0.0 copy-start.2
  9.0 1.7 %collective-permute-done.1.xp = f32[6,32,128]{2,1,0:T(8,128)S(1)} collective-permute-done((f32[6,32,128]{2,1,0:T(8,128)S(1)}, f32[6,32,128]{2,1,0:T(8,128)S(1)}, u32[]{:S(2)}, u32[]{:S(2)}) %collective-permute-start.1) | collective-permute-done | bytes 98336 | tf_op jit(solution)/shard_map/ppermute | solution.py:217
  10.7 0.0 copy-start.3
  10.8 6.1 %collective-permute-start.3 = (f32[6,66,128]{2,1,0:T(8,128)S(1)}, f32[6,66,128]{2,1,0:T(8,128)S(1)}, u32[]{:S(2)}, u32[]{:S(2)}) collective-permute-start(f32[6,66,128]{2,1,0:T(8,128)S(1)} %pad_maximum_fusion.1), channel_id=1, source_target_pairs={{0,7},{1,0},{2,1},{3,2},{4,3},{5,4},{6,5},{7,6},{8,15},{9,8},{10,9... | collective-permute-start | bytes 608264 | tf_op jit(solution)/shard_map/ppermute | solution.py:217
  16.9 0.1 collective-permute-start.2
  17.0 1.3 %pad.4.counts = s32[32,128]{1,0:T(8,128)} pad(s32[32,64]{1,0:T(8,128)} %bitcast.48, s32[]{:T(128)} %constant.15.clone.1), padding=0_0x0_64 | pad | bytes 24580 | tf_op jit(solution)/shard_map/jit(_pad)/pad | solution.py:244
  18.3 0.6 pad_add_fusion.first
  18.9 3.5 %prep.1 = (s32[32,128]{1,0:T(8,128)}, f32[3,32,128]{2,1,0:T(8,128)}, s32[32,128]{1,0:T(8,128)}, s32[32,128]{1,0:T(8,128)}, s32[32,128]{1,0:T(8,128)}) custom-call(s32[2]{0:T(128)} %pad_add_fusion.first, s32[4,4096]{1,0:T(4,128)} %blocks.1, f32[3,4096]{1,0:T(4,128)} %offs.1, s32[32,128]{1,0:T(8,128)} %bitcast.50, s32[8,128]{1,0:T(8,128)} %bitcast.51), custom_call_target="tpu_custom_call" | custom-call | flops 20000000 | bytes 300000 | tf_op jit(solution)/shard_map/prep/pallas_call | solution.py:234
  22.4 0.0 collective-permute-done.3.yp
  22.4 0.0 copy-start
  22.4 4.3 %collective-permute-done.2.ym = f32[6,66,128]{2,1,0:T(8,128)S(1)} collective-permute-done((f32[6,66,128]{2,1,0:T(8,128)S(1)}, f32[6,66,128]{2,1,0:T(8,128)S(1)}, u32[]{:S(2)}, u32[]{:S(2)}) %collective-permute-start.2) | collective-permute-done | bytes 202784 | tf_op jit(solution)/shard_map/ppermute | solution.py:217
  26.7 0.0 copy-start.1
  26.7 0.0 copy-done.2
  26.7 0.0 copy-done.3
  26.7 0.0 copy-done
  26.7 0.7 copy-done.1
  27.4 38.4 %radiance.1 = f32[128,384]{1,0:T(8,128)} custom-call(s32[4096]{0:T(1024)} %bitcast.49, f32[6,64,32,128]{3,2,1,0:T(8,128)} %ph.1, s32[32,128]{1,0:T(8,128)} %pad.4.counts, f32[6,32,128]{2,1,0:T(8,128)} %copy-done.2, f32[6,32,128]{2,1,0:T(8,128)} %copy-done.3, f32[6,66,128]{2,1,0:T(8,128)} %copy-done.1, f32[6,66,128]{2,1,0:T(8,128)} %copy-done, ...), custom_call_target="tpu_custom_call" | custom-call | tf_op jit(solution)/shard_map/radiance/pallas_call | solution.py:245
  65.8 1.1 %copy.32 = f32[128,1,384]{2,1,0:T(1,128)S(1)} copy(f32[128,1,384]{2,0,1:T(8,128)} %bitcast.43) | data formatting | bytes 393216 | tf_op jit(solution)/shard_map/all_to_all | solution.py:260
  67.0 15.7 %all_to_all.11 = f32[128,1,384]{2,1,0:T(1,128)S(1)} all-to-all(f32[128,1,384]{2,1,0:T(1,128)S(1)} %copy.32), channel_id=1, replica_groups=mesh['bx'=16,'by'=8] {'bx','by'}, dimensions={0} | all-to-all | bytes 393216 | tf_op jit(solution)/shard_map/all_to_all | solution.py:260
  82.6 0.7 copy.43
  83.3 4.5 %film.1 = f32[3,8,256]{2,1,0:T(8,128)} custom-call(f32[128,384]{1,0:T(8,128)} %bitcast.42), custom_call_target="tpu_custom_call" | custom-call | tf_op jit(solution)/shard_map/film/pallas_call | solution.py:261
  (8 shorter events, 0.1 us)
Async XLA Ops:
  2.7 6.2 %collective-permute-start = (f32[6,32,128]{2,1,0:T(8,128)S(1)}, f32[6,32,128]{2,1,0:T(8,128)S(1)}, u32[]{:S(2)}, u32[]{:S(2)}) collective-permute-start(f32[6,32,128]{2,1,0:T(8,128)S(1)} %pad_maximum_fusion.2), channel_id=1, source_target_pairs={{0,8},{8,16},{16,24},{24,32},{32,40},{40,48},{48,56},{56,64},{64,7... | collective-permute-start | bytes 294920 | tf_op jit(solution)/shard_map/ppermute | solution.py:217
  5.8 4.9 %collective-permute-start.1 = (f32[6,32,128]{2,1,0:T(8,128)S(1)}, f32[6,32,128]{2,1,0:T(8,128)S(1)}, u32[]{:S(2)}, u32[]{:S(2)}) collective-permute-start(f32[6,32,128]{2,1,0:T(8,128)S(1)} %pad_maximum_fusion.3), channel_id=1, source_target_pairs={{0,120},{8,0},{16,8},{24,16},{32,24},{40,32},{48,40},{56,48},{64,5... | collective-permute-start | bytes 294920 | tf_op jit(solution)/shard_map/ppermute | solution.py:217
  9.0 17.7 %copy-start.2 = (f32[6,32,128]{2,1,0:T(8,128)}, f32[6,32,128]{2,1,0:T(8,128)S(1)}, u32[]{:S(2)}) copy-start(f32[6,32,128]{2,1,0:T(8,128)S(1)} %collective-permute-done.xm) | copy-start | bytes 294916
  10.7 16.0 %copy-start.3 = (f32[6,32,128]{2,1,0:T(8,128)}, f32[6,32,128]{2,1,0:T(8,128)S(1)}, u32[]{:S(2)}) copy-start(f32[6,32,128]{2,1,0:T(8,128)S(1)} %collective-permute-done.1.xp) | copy-start | bytes 294916
  10.8 11.6 %collective-permute-start.3 = (f32[6,66,128]{2,1,0:T(8,128)S(1)}, f32[6,66,128]{2,1,0:T(8,128)S(1)}, u32[]{:S(2)}, u32[]{:S(2)}) collective-permute-start(f32[6,66,128]{2,1,0:T(8,128)S(1)} %pad_maximum_fusion.1), channel_id=1, source_target_pairs={{0,7},{1,0},{2,1},{3,2},{4,3},{5,4},{6,5},{7,6},{8,15},{9,8},{10,9... | collective-permute-start | bytes 608264 | tf_op jit(solution)/shard_map/ppermute | solution.py:217
  16.9 9.8 %collective-permute-start.2 = (f32[6,66,128]{2,1,0:T(8,128)S(1)}, f32[6,66,128]{2,1,0:T(8,128)S(1)}, u32[]{:S(2)}, u32[]{:S(2)}) collective-permute-start(f32[6,66,128]{2,1,0:T(8,128)S(1)} %pad_maximum_fusion), channel_id=1, source_target_pairs={{0,1},{1,2},{2,3},{3,4},{4,5},{5,6},{6,7},{7,0},{8,9},{9,10},{10,1... | collective-permute-start | bytes 608264 | tf_op jit(solution)/shard_map/ppermute | solution.py:217
  22.4 4.3 %copy-start = (f32[6,66,128]{2,1,0:T(8,128)}, f32[6,66,128]{2,1,0:T(8,128)S(1)}, u32[]{:S(2)}) copy-start(f32[6,66,128]{2,1,0:T(8,128)S(1)} %collective-permute-done.3.yp) | copy-start | bytes 608260
  26.7 0.7 copy-start.1

commit v2 on v1

--- a/solution.py
+++ b/solution.py
@@ -14,11 +14,11 @@
 ROWS = POINTS // LANES
 CAP = 96
 OWNERS = 128
-COMP = 2 * EY
-PAIR = 6 * COMP
-FRONT = 8
-TABLE_ROWS = FRONT + (CX + 1) * PAIR + 16
-GROUPS = 4
+TWO = 4 * EY
+PAIR = 3 * TWO
+TABLE_ROWS = (CX + 1) * PAIR
+STEP = 9
+GROUPS = 2
 i32, f32, bf16 = jnp.int32, jnp.float32, jnp.bfloat16
 VMEM = pl.BlockSpec(memory_space=pltpu.VMEM)
 SMEM = pl.BlockSpec(memory_space=pltpu.SMEM)
@@ -49,8 +49,7 @@
     ly = [((sb[k] & (NYC - 1)) - fy + 1) & (NYC - 1) for k in range(4)]
     qx = jnp.minimum(jnp.minimum(lx[0], lx[1]), jnp.minimum(lx[2], lx[3]))
     qy = jnp.minimum(jnp.minimum(ly[0], ly[1]), jnp.minimum(ly[2], ly[3]))
-    odd = (iota((ROWS, LANES), 0) >> 2) & 1
-    start[...] = FRONT + qx * PAIR + qy * 2 - 4 * odd
+    start[...] = qx * PAIR + qy * 4
     rel[0] = 2.0 * (so[0] + (lx[0] - qx).astype(f32))
     rel[1] = 2.0 * (so[1] + (ly[0] - qy).astype(f32))
     rel[2] = 2.0 * so[2]
@@ -78,83 +77,88 @@
     lax.fori_loop(0, ROWS, step, jnp.zeros((OWNERS, LANES), f32), unroll=4)
 
 
-def main_kernel(start, ph, counts, xm, xp, ym, yp, rel, alb, owner, rank, target, send, table, wide, prod, sums, rad):
+def main_kernel(start, ph, counts, xm, xp, ym, yp, rel, alb, owner, rank, target, send, table, stage_a, stage_b, near_a, near_b, sums, rad):
     lane = iota((CY, LANES), 1)
 
-    def put(c, x, value):
-        table[pl.ds(FRONT + (x + 1) * PAIR + c * COMP + 2, CY, stride=2), :] = value
-        table[pl.ds(FRONT + x * PAIR + c * COMP + 3, CY, stride=2), :] = value
+    def row(c, x, y, right):
+        return x * PAIR + (c // 2) * TWO + y * 4 + 2 * right + c % 2
 
     def column(x, _):
         at = jnp.full((CY, LANES), x, i32)
         live = lane < lane_take(counts[...], at)
         for c in range(6):
             v = ph[c, x]
-            put(c, x, v + v if c < 3 else jnp.where(live, v, 0.0))
+            v = v + v if c < 3 else jnp.where(live, v, 0.0)
+            table[pl.ds(row(c, x + 1, 1, 0), CY, stride=4), :] = v
+            table[pl.ds(row(c, x, 1, 1), CY, stride=4), :] = v
         return 0
 
     lax.fori_loop(0, CX, column, 0, unroll=2)
     for c in range(6):
         scale = 2.0 if c < 3 else 1.0
-        table[pl.ds(FRONT + c * COMP + 2, CY, stride=2), :] = xm[c] * scale
-        table[pl.ds(FRONT + CX * PAIR + c * COMP + 3, CY, stride=2), :] = xp[c] * scale
-        for side, at in ((ym, 0), (yp, 2 * EY - 2)):
-            table[pl.ds(FRONT + c * COMP + at, CX + 1, stride=PAIR), :] = side[c, : CX + 1] * scale
-            table[pl.ds(FRONT + c * COMP + at + 1, CX + 1, stride=PAIR), :] = side[c, 1:] * scale
-    sub = iota((8, LANES), 0)
-    upper = sub < 4
-    place = ((sub & 1).astype(f32) * 2.0, ((sub >> 1) & 1).astype(f32) * 2.0, None)
-    for v in range(4):
+        table[pl.ds(row(c, 0, 1, 0), CY, stride=4), :] = xm[c] * scale
+        table[pl.ds(row(c, CX, 1, 1), CY, stride=4), :] = xp[c] * scale
+        for side, y in ((ym, 0), (yp, EY - 1)):
+            table[pl.ds(row(c, 0, y, 0), CX + 1, stride=PAIR), :] = side[c, : CX + 1] * scale
+            table[pl.ds(row(c, 0, y, 1), CX + 1, stride=PAIR), :] = side[c, 1:] * scale
+    zero = start[POINTS]
+
+    def fetch(i, stage, near):
+        for u in range(GROUPS):
+            g = jnp.minimum(i * GROUPS + u, POINTS // 8 - 1)
+            at = jnp.full((8, LANES), g & (LANES - 1), i32)
+            for c in range(3):
+                near[u, c] = lane_take(rel[g >> 7, c], at)
+            for s in range(8):
+                r = start[g * 8 + s]
+                for j in range(3):
+                    stage[u, j, pl.ds(zero + STEP * s, 8), :] = table[pl.ds(r + j * TWO, 8), :]
+
+    def weigh(i, stage, near):
+        for u in range(GROUPS):
+            close = [near[u, c] for c in range(3)]
+            far = [x - 2.0 for x in close]
+            total = [None] * 3
+            for k in range(4):
+                yy, xx = k >> 1, k & 1
+
+                def load(c):
+                    return stage[u, c // 2, pl.ds(4 * yy + 2 * xx + c % 2, 8, stride=STEP), :]
+
+                o = (far[0] if xx else close[0], far[1] if yy else close[1], close[2])
+                d = [load(c) - o[c] for c in range(3)]
+                dist = d[0] * d[0] + d[1] * d[1] + d[2] * d[2]
+                weight = jnp.maximum(1.0 - dist, 0.0)
+                for c in range(3):
+                    v = weight * load(3 + c)
+                    total[c] = v if k == 0 else total[c] + v
+            for c in range(3):
+                sums[c, pl.ds(8 * (i * GROUPS + u), 8), :] = total[c]
+
+    def step(i, _):
+        weigh(2 * i, stage_a, near_a)
+        fetch(2 * i + 1, stage_b, near_b)
+        weigh(2 * i + 1, stage_b, near_b)
+        fetch(2 * i + 2, stage_a, near_a)
+        return 0
+
+    fetch(0, stage_a, near_a)
+    trips = POINTS // 16 // GROUPS
+    lax.fori_loop(0, trips, step, 0)
+    ones = jnp.ones((8, 2 * LANES), f32).astype(bf16)
+
+    def lane_sums(r, _):
         for c in range(3):
-            for p in range(4):
-                a = jnp.broadcast_to(rel[c, 8 * p + v : 8 * p + v + 1, :], (8, LANES))
-                b = jnp.broadcast_to(rel[c, 8 * p + 4 + v : 8 * p + 5 + v, :], (8, LANES))
-                both = jnp.where(upper, a, b)
-                wide[v, c, p] = both if place[c] is None else both - place[c]
-
-    def block(v, _):
-        def groups(g, _):
-            for u in range(GROUPS):
-                L = g * GROUPS + u
-                at = jnp.full((8, LANES), L, i32)
-                rows = [start[s * 512 + v * LANES + L] for s in range(8)]
-                for p in range(4):
-                    ra, rb = rows[2 * p], rows[2 * p + 1]
-
-                    def load(c):
-                        return jnp.where(
-                            upper, table[pl.ds(ra + c * COMP, 8), :], table[pl.ds(rb + c * COMP, 8), :]
-                        )
-
-                    d = [load(c) - lane_take(wide[v, c, p], at) for c in range(3)]
-                    dist = d[0] * d[0] + d[1] * d[1] + d[2] * d[2]
-                    weight = jnp.maximum(1.0 - dist, 0.0)
-                    for c in range(3):
-                        prod[u, c, 8 * p : 8 * p + 8, :] = weight * load(3 + c)
-                for c in range(3):
-                    part = [prod[u, c, pl.ds(i, 8, stride=4), :] for i in range(4)]
-                    sums[c, L] = (part[0] + part[1]) + (part[2] + part[3])
-            return 0
-
-        lax.fori_loop(0, LANES // GROUPS, groups, 0)
-        lanes = iota((8, LANES), 1)
-
-        def reduce(c, first, size):
-            if size == 1:
-                return sums[c, first]
-            half = size // 2
-            a, b = reduce(c, first, half), reduce(c, first + half, half)
-            mine = (lanes & half) == 0
-            return jnp.where(mine, a, b) + pltpu.roll(jnp.where(mine, b, a), half, 1)
-
-        def channel(c, _):
-            rad[c, pl.ds(v, 8, stride=4), :] = reduce(c, 0, LANES)
-            return 0
-
-        lax.fori_loop(0, 3, channel, 0)
+            for k in range(2):
+                x = sums[c, pl.ds((2 * r + k) * LANES, LANES), :]
+                high = x.astype(bf16)
+                low = (x - high.astype(f32)).astype(bf16)
+                both = jnp.concatenate([high, low], axis=1)
+                y = lax.dot_general(ones, both, NT, preferred_element_type=f32)
+                rad[c, pl.ds(2 * r + k, 1), :] = y[:1]
         return 0
 
-    lax.fori_loop(0, 4, block, 0)
+    lax.fori_loop(0, ROWS // 2, lane_sums, 0)
     for c in range(3):
         for r in range(ROWS):
             rad[c, r : r + 1, :] = rad[c, r : r + 1, :] * alb[c : c + 1, r * LANES : (r + 1) * LANES]
@@ -178,12 +182,12 @@
             total = total + lax.dot_general(mine, rows, NT, preferred_element_type=f32)
         return total
 
-    send[...] = lax.fori_loop(0, ROWS // 2, scatter, jnp.zeros((OWNERS, 4 * CAP), f32), unroll=2)
+    send[:, 0, :] = lax.fori_loop(0, ROWS // 2, scatter, jnp.zeros((OWNERS, 4 * CAP), f32), unroll=2)
 
 
 def film_kernel(got, film, flipped, total):
     for j in range(3):
-        flipped[LANES * j : LANES * j + LANES, :] = jnp.transpose(got[:, LANES * j : LANES * j + LANES])
+        flipped[LANES * j : LANES * j + LANES, :] = jnp.transpose(got[:, 0, LANES * j : LANES * j + LANES])
     lo_sub = iota((LANES, 2 * LANES), 0)
     hi_sub = iota((16, 2 * LANES), 0)
 
@@ -241,22 +245,25 @@
         cost_estimate=pl.CostEstimate(flops=20_000_000, bytes_accessed=300_000, transcendentals=0),
         name="prep",
     )(first, gather_blocks, gather_offsets, gather_pixels.reshape(ROWS, LANES), tile_slot.reshape(8, LANES))
+    rel = rel.reshape(3, 4, LANES, 8).transpose(1, 0, 3, 2)
     counts = jnp.pad(block_counts.T, ((0, 0), (0, LANES - CX)))
     send = pl.pallas_call(
         main_kernel,
         in_specs=[SMEM] + [VMEM] * 11,
         out_specs=VMEM,
-        out_shape=jax.ShapeDtypeStruct((OWNERS, 4 * CAP), f32),
+        out_shape=jax.ShapeDtypeStruct((OWNERS, 1, 4 * CAP), f32),
         scratch_shapes=[
             pltpu.VMEM((TABLE_ROWS, LANES), f32),
-            pltpu.VMEM((4, 3, 4, 8, LANES), f32),
-            pltpu.VMEM((GROUPS, 3, 32, LANES), f32),
-            pltpu.VMEM((3, LANES, 8, LANES), f32),
+            pltpu.VMEM((GROUPS, 3, 8 * STEP + 8, LANES), f32),
+            pltpu.VMEM((GROUPS, 3, 8 * STEP + 8, LANES), f32),
+            pltpu.VMEM((GROUPS, 3, 8, LANES), f32),
+            pltpu.VMEM((GROUPS, 3, 8, LANES), f32),
+            pltpu.VMEM((3, POINTS, LANES), f32),
             pltpu.VMEM((3, ROWS, LANES), f32),
         ],
         compiler_params=params(),
         name="radiance",
-    )(start.reshape(POINTS), photon_data, counts, xm, xp, ym, yp, rel, albedo, owner, rank, target)
+    )(jnp.pad(start.reshape(POINTS), (0, LANES)), photon_data, counts, xm, xp, ym, yp, rel, albedo, owner, rank, target)
     got = lax.all_to_all(send, AXES, 0, 0, tiled=True)
     return pl.pallas_call(
         film_kernel,

time: 88.3 us -> 76.7 us (0.87)
  Pallas kernels: 46.4 us -> 33.7 us
  waiting for transfers between devices: 6.02 us -> 2.64 us
  blocking collectives: 15.7 us -> 18.4 us
  local copies, waits for them, and re-layouts: 8.57 us -> 10.1 us
    pallas_call x1, Pallas kernels: 38.4 us -> 25.8 us  [per_device(): pl.pallas_call(main_kernel, in_specs=[SMEM] + [VMEM] * 11, out_specs=VMEM...]
    ppermute x4, waiting for transfers between devices: 6.02 us -> 2.64 us  [shift(): return lax.ppermute(x, axis, [(i, (i + by) % n) for i in range(n)])]
    all_to_all x1, blocking collectives: 15.7 us -> 18.4 us  [per_device(): got = lax.all_to_all(send, AXES, 0, 0, tiled=True)]
    reshape x0 -> x2, local copies, waits for them, and re-layouts: none -> 2.09 us  [per_device(): rel = rel.reshape(3, 4, LANES, 8).transpose(1, 0, 3, 2)]
    pad x0 -> x1, local copies, waits for them, and re-layouts: none -> 1.32 us  [per_device(): jnp.pad(start.reshape(POINTS), (0, LANES))]
    all_to_all x1 -> x0, local copies, waits for them, and re-layouts: 1.13 us -> none  [per_device(): got = lax.all_to_all(send, AXES, 0, 0, tiled=True)]
  transfers between devices with their start and end apart: 4 -> 4, of which waited for: 2 -> 2; matrix products, arithmetic and copies ran while one was open for 6% -> 11% of each run, Pallas kernels for 4% -> 5%
where the time goes in v2:
time: 76.7 us; the launch traced here: 76.1 us
  Pallas kernels  33.7 us (44%)
  blocking collectives  18.4 us (24%)
  local copies, waits for them, and re-layouts  10.1 us (13%)
  starting transfers between devices  9.34 us (12%)
  waiting for transfers between devices  2.64 us (3%)
  other arithmetic  1.68 us (2%)
    pallas_call x1, Pallas kernels, per_device(): pl.pallas_call(main_kernel, in_specs=[SMEM] + [VMEM] * 11, out_specs=VMEM...  25.8 us
    all_to_all x1, blocking collectives, per_device(): got = lax.all_to_all(send, AXES, 0, 0, tiled=True)  18.4 us
    ppermute x4, starting transfers between devices, shift(): return lax.ppermute(x, axis, [(i, (i + by) % n) for i in range(n)])  9.34 us
    pallas_call x1, Pallas kernels, per_device(): pl.pallas_call(film_kernel, in_specs=[VMEM], out_specs=VMEM, out_shape=ja...  4.52 us
    pallas_call x1, Pallas kernels, per_device(): pl.pallas_call(prep_kernel, in_specs=[SMEM, VMEM, VMEM, VMEM, VMEM], out_...  3.45 us
    slice x2, local copies, waits for them, and re-layouts, live_only(): x[:3]  3.02 us
    ppermute x4, waiting for transfers between devices, shift(): return lax.ppermute(x, axis, [(i, (i + by) % n) for i in range(n)])  2.64 us
    reshape x2, local copies, waits for them, and re-layouts, per_device(): rel = rel.reshape(3, 4, LANES, 8).transpose(1, 0, 3, 2)  2.09 us
  transfers between devices with their start and end apart: 4, of which 2 were waited for; matrix products, arithmetic and copies ran while one was open for 11% of the time, Pallas kernels for 5%

profile of v2, /device:TPU:1, one launch (start us, length us, event | category | flops | bytes accessed | tf_op | source)
XLA Modules:
  0.0 76.1 jit_solution(17416491616343345185)
XLA Ops:
  0.0 1.0 %slice_reduce_fusion = (s32[32]{0:T(128)S(1)}, s32[32]{0:T(128)S(1)}) fusion(s32[64,32]{0,1:T(8,128)} %param.8), kind=kLoop, calls=%fused_computation.12 | loop fusion | bytes 512 | tf_op jit(solution)/shard_map/slice | solution.py:232
  1.0 0.8 %slice_bitcast_fusion = (f32[3,32,128]{2,1,0:T(8,128)S(1)}, f32[3,32,128]{2,1,0:T(8,128)S(1)}) fusion(f32[6,64,32,128]{3,2,1,0:T(8,128)} %ph.1), kind=kLoop, calls=%fused_computation.8 | loop fusion | bytes 196608 | tf_op jit(solution)/shard_map/slice | solution.py:226
  1.8 0.1 iota_compare_fusion.2
  1.9 0.8 %bitcast_select_fusion = (f32[3,32,128]{2,1,0:T(8,128)S(1)}, f32[3,32,128]{2,1,0:T(8,128)S(1)}) fusion(f32[6,64,32,128]{3,2,1,0:T(8,128)} %ph.1, pred[32,128]{1,0:T(8,128)(4,1)S(1)} %get-tuple-element.31, pred[32,128]{1,0:T(8,128)(4,1)S(1)} %get-tuple-element.32), kind=kLoop, calls=%fused_computation.4 | loop fusion | flops 24576 | bytes 204800 | tf_op jit(solution)/shard_map/jit(_where)/select_n | solution.py:226
  2.7 3.1 %collective-permute-start = (f32[6,32,128]{2,1,0:T(8,128)S(1)}, f32[6,32,128]{2,1,0:T(8,128)S(1)}, u32[]{:S(2)}, u32[]{:S(2)}) collective-permute-start(f32[6,32,128]{2,1,0:T(8,128)S(1)} %pad_maximum_fusion.2), channel_id=1, source_target_pairs={{0,8},{8,16},{16,24},{24,32},{32,40},{40,48},{48,56},{56,64},{64,7... | collective-permute-start | bytes 294920 | tf_op jit(solution)/shard_map/ppermute | solution.py:221
  5.8 0.1 collective-permute-start.1
  5.9 2.2 %fusion = (f32[3,64,1,128]{3,2,1,0:T(1,128)S(1)}, f32[3,64,1,128]{3,2,1,0:T(1,128)S(1)}, f32[3,64,1,128]{3,2,1,0:T(1,128)S(1)}, f32[3,64,1,128]{3,2,1,0:T(1,128)S(1)}) fusion(f32[6,64,32,128]{3,2,1,0:T(8,128)} %ph.1), kind=kLoop, calls=%fused_computation.19 | loop fusion | bytes 786432 | tf_op jit(solution)/shard_map/slice | solution.py:226
  8.1 0.7 slice_bitcast_fusion.2
  8.8 0.1 iota_compare_fusion
  8.9 0.0 collective-permute-done.xm
  9.0 0.0 copy-start.2
  9.0 1.7 %collective-permute-done.1.xp = f32[6,32,128]{2,1,0:T(8,128)S(1)} collective-permute-done((f32[6,32,128]{2,1,0:T(8,128)S(1)}, f32[6,32,128]{2,1,0:T(8,128)S(1)}, u32[]{:S(2)}, u32[]{:S(2)}) %collective-permute-start.1) | collective-permute-done | bytes 98336 | tf_op jit(solution)/shard_map/ppermute | solution.py:221
  10.7 0.0 copy-start.3
  10.8 6.1 %collective-permute-start.3 = (f32[6,66,128]{2,1,0:T(8,128)S(1)}, f32[6,66,128]{2,1,0:T(8,128)S(1)}, u32[]{:S(2)}, u32[]{:S(2)}) collective-permute-start(f32[6,66,128]{2,1,0:T(8,128)S(1)} %pad_maximum_fusion.1), channel_id=1, source_target_pairs={{0,7},{1,0},{2,1},{3,2},{4,3},{5,4},{6,5},{7,6},{8,15},{9,8},{10,9... | collective-permute-start | bytes 608264 | tf_op jit(solution)/shard_map/ppermute | solution.py:221
  16.9 0.1 collective-permute-start.2
  17.0 0.6 pad_add_fusion.first
  17.6 3.5 %prep.1 = (s32[32,128]{1,0:T(8,128)}, f32[3,32,128]{2,1,0:T(8,128)}, s32[32,128]{1,0:T(8,128)}, s32[32,128]{1,0:T(8,128)}, s32[32,128]{1,0:T(8,128)}) custom-call(s32[2]{0:T(128)} %pad_add_fusion.first, s32[4,4096]{1,0:T(4,128)} %blocks.1, f32[3,4096]{1,0:T(4,128)} %offs.1, s32[32,128]{1,0:T(8,128)} %bitcast.45, s32[8,128]{1,0:T(8,128)} %bitcast.47), custom_call_target="tpu_custom_call" | custom-call | flops 20000000 | bytes 300000 | tf_op jit(solution)/shard_map/prep/pallas_call | solution.py:238
  21.0 1.2 %reshape.25 = f32[3,4,128,8]{3,2,1,0:T(8,128)S(1)} reshape(f32[3,32,128]{2,1,0:T(8,128)} %get-tuple-element.11) | data formatting | bytes 98304 | tf_op jit(solution)/shard_map/reshape | solution.py:248
  22.3 0.9 %copy.24 = f32[3,4,128,8]{2,3,0,1:T(8,128)} copy(f32[3,4,128,8]{3,2,1,0:T(8,128)S(1)} %reshape.25) | data formatting | bytes 98304 | tf_op jit(solution)/shard_map/reshape | solution.py:248
  23.1 1.3 %pad.8.start = s32[4224]{0:T(1024)} pad(s32[4096]{0:T(1024)} %bitcast.46, s32[]{:T(128)} %constant.15.clone.1), padding=0_128 | pad | bytes 33284 | tf_op jit(solution)/shard_map/jit(_pad)/pad | solution.py:266
  24.4 1.3 %pad.9.counts = s32[32,128]{1,0:T(8,128)} pad(s32[32,64]{1,0:T(8,128)} %bitcast.44, s32[]{:T(128)} %constant.15.clone.1), padding=0_0x0_64 | pad | bytes 24580 | tf_op jit(solution)/shard_map/jit(_pad)/pad | solution.py:249
  25.8 0.0 collective-permute-done.3.yp
  25.8 0.0 copy-start
  25.8 0.9 %collective-permute-done.2.ym = f32[6,66,128]{2,1,0:T(8,128)S(1)} collective-permute-done((f32[6,66,128]{2,1,0:T(8,128)S(1)}, f32[6,66,128]{2,1,0:T(8,128)S(1)}, u32[]{:S(2)}, u32[]{:S(2)}) %collective-permute-start.2) | collective-permute-done | bytes 202784 | tf_op jit(solution)/shard_map/ppermute | solution.py:221
  26.7 0.0 copy-start.1
  26.7 0.0 copy-done.2
  26.7 0.0 copy-done.3
  26.7 0.0 copy-done
  26.7 0.7 copy-done.1
  27.4 25.8 %radiance.1 = f32[128,1,384]{2,1,0:T(1,128)} custom-call(s32[4224]{0:T(1024)} %pad.8.start, f32[6,64,32,128]{3,2,1,0:T(8,128)} %ph.1, s32[32,128]{1,0:T(8,128)} %pad.9.counts, f32[6,32,128]{2,1,0:T(8,128)} %copy-done.2, f32[6,32,128]{2,1,0:T(8,128)} %copy-done.3, f32[6,66,128]{2,1,0:T(8,128)} %copy-done.1, f32[6,66,128]{2,1,0:T(8,128)} %copy-done, ...), custom_call_target="tpu_custom_call" | custom-call | tf_op jit(solution)/shard_map/radiance/pallas_call | solution.py:250
  53.1 18.4 %all_to_all.5.got = f32[128,1,384]{2,1,0:T(1,128)} all-to-all(f32[128,1,384]{2,1,0:T(1,128)} %radiance.1), channel_id=1, replica_groups=mesh['bx'=16,'by'=8] {'bx','by'}, dimensions={0} | all-to-all | bytes 393216 | tf_op jit(solution)/shard_map/all_to_all | solution.py:267
  71.6 4.5 %film.1 = f32[3,8,256]{2,1,0:T(8,128)} custom-call(f32[128,1,384]{2,1,0:T(1,128)} %all_to_all.5.got), custom_call_target="tpu_custom_call" | custom-call | tf_op jit(solution)/shard_map/film/pallas_call | solution.py:268
  (8 shorter events, 0.1 us)
Async XLA Ops:
  2.7 6.2 %collective-permute-start = (f32[6,32,128]{2,1,0:T(8,128)S(1)}, f32[6,32,128]{2,1,0:T(8,128)S(1)}, u32[]{:S(2)}, u32[]{:S(2)}) collective-permute-start(f32[6,32,128]{2,1,0:T(8,128)S(1)} %pad_maximum_fusion.2), channel_id=1, source_target_pairs={{0,8},{8,16},{16,24},{24,32},{32,40},{40,48},{48,56},{56,64},{64,7... | collective-permute-start | bytes 294920 | tf_op jit(solution)/shard_map/ppermute | solution.py:221
  5.8 4.9 %collective-permute-start.1 = (f32[6,32,128]{2,1,0:T(8,128)S(1)}, f32[6,32,128]{2,1,0:T(8,128)S(1)}, u32[]{:S(2)}, u32[]{:S(2)}) collective-permute-start(f32[6,32,128]{2,1,0:T(8,128)S(1)} %pad_maximum_fusion.3), channel_id=1, source_target_pairs={{0,120},{8,0},{16,8},{24,16},{32,24},{40,32},{48,40},{56,48},{64,5... | collective-permute-start | bytes 294920 | tf_op jit(solution)/shard_map/ppermute | solution.py:221
  9.0 17.7 %copy-start.2 = (f32[6,32,128]{2,1,0:T(8,128)}, f32[6,32,128]{2,1,0:T(8,128)S(1)}, u32[]{:S(2)}) copy-start(f32[6,32,128]{2,1,0:T(8,128)S(1)} %collective-permute-done.xm) | copy-start | bytes 294916
  10.7 16.0 %copy-start.3 = (f32[6,32,128]{2,1,0:T(8,128)}, f32[6,32,128]{2,1,0:T(8,128)S(1)}, u32[]{:S(2)}) copy-start(f32[6,32,128]{2,1,0:T(8,128)S(1)} %collective-permute-done.1.xp) | copy-start | bytes 294916
  10.8 15.0 %collective-permute-start.3 = (f32[6,66,128]{2,1,0:T(8,128)S(1)}, f32[6,66,128]{2,1,0:T(8,128)S(1)}, u32[]{:S(2)}, u32[]{:S(2)}) collective-permute-start(f32[6,66,128]{2,1,0:T(8,128)S(1)} %pad_maximum_fusion.1), channel_id=1, source_target_pairs={{0,7},{1,0},{2,1},{3,2},{4,3},{5,4},{6,5},{7,6},{8,15},{9,8},{10,9... | collective-permute-start | bytes 608264 | tf_op jit(solution)/shard_map/ppermute | solution.py:221
  16.9 9.8 %collective-permute-start.2 = (f32[6,66,128]{2,1,0:T(8,128)S(1)}, f32[6,66,128]{2,1,0:T(8,128)S(1)}, u32[]{:S(2)}, u32[]{:S(2)}) collective-permute-start(f32[6,66,128]{2,1,0:T(8,128)S(1)} %pad_maximum_fusion), channel_id=1, source_target_pairs={{0,1},{1,2},{2,3},{3,4},{4,5},{5,6},{6,7},{7,0},{8,9},{9,10},{10,1... | collective-permute-start | bytes 608264 | tf_op jit(solution)/shard_map/ppermute | solution.py:221
  25.8 0.9 %copy-start = (f32[6,66,128]{2,1,0:T(8,128)}, f32[6,66,128]{2,1,0:T(8,128)S(1)}, u32[]{:S(2)}) copy-start(f32[6,66,128]{2,1,0:T(8,128)S(1)} %collective-permute-done.3.yp) | copy-start | bytes 608260
  26.7 0.7 copy-start.1

commit v3 on v2

v3 whole, which is shorter than its diff:
```python
import jax
import jax.numpy as jnp
from jax import lax
from jax.experimental import pallas as pl
from jax.experimental.pallas import tpu as pltpu
from jax.sharding import PartitionSpec as P

AXES = ("bx", "by")
CX, CY = 64, 32
EX, EY = CX + 2, CY + 2
NXC, NYC = 1024, 256
LANES = 128
POINTS = 4096
ROWS = POINTS // LANES
CAP = 96
OWNERS = 128
TWO = 4 * EY
PAIR = 3 * TWO
TABLE_ROWS = (CX + 1) * PAIR
APART = 513
EDGE_X, EDGE_Y = 4 * EY, 8 * (CX + 1)
EDGE = 2 * EDGE_X + 2 * EDGE_Y
LIST = POINTS + 128
CHUNKS = 8
STEP = 9
GROUPS = 2
i32, f32, bf16 = jnp.int32, jnp.float32, jnp.bfloat16
VMEM = pl.BlockSpec(memory_space=pltpu.VMEM)
SMEM = pl.BlockSpec(memory_space=pltpu.SMEM)
NT = (((1,), (1,)), ((), ()))


HBM = pl.BlockSpec(memory_space=pltpu.HBM)


def params(mib):
    return pltpu.CompilerParams(vmem_limit_bytes=mib * 1024 * 1024)


def iota(shape, dim):
    return lax.broadcasted_iota(i32, shape, dim)


def lane_take(x, idx):
    return jnp.take_along_axis(x, idx, axis=1, mode="promise_in_bounds")


def weigh_eight(stage, close):
    far = [x - 2.0 for x in close]
    total = [None] * 3
    for k in range(4):
        yy, xx = k >> 1, k & 1

        def load(c):
            return stage[c // 2, pl.ds(4 * yy + 2 * xx + c % 2, 8, stride=STEP), :]

        o = (far[0] if xx else close[0], far[1] if yy else close[1], close[2])
        d = [load(c) - o[c] for c in range(3)]
        dist = d[0] * d[0] + d[1] * d[1] + d[2] * d[2]
        weight = jnp.maximum(1.0 - dist, 0.0)
        for c in range(3):
            v = weight * load(3 + c)
            total[c] = v if k == 0 else total[c] + v
    return total


def inner_kernel(ph, counts, blocks, offs, pix, tile_slot, sums, rel, owner, rank, target, points, places,
                 photons, table, sb, so, square, flat, stage_a, stage_b, near_a, near_b, start, psem, ssem):
    part = CX // CHUNKS
    reads = [
        pltpu.make_async_copy(ph.at[:, pl.ds(k * part, part)], photons.at[:, pl.ds(k * part, part)], psem.at[k])
        for k in range(CHUNKS)
    ]
    for read in reads:
        read.start()
    for k in range(4):
        for r in range(ROWS):
            sb[k, r : r + 1, :] = blocks[k : k + 1, r * LANES : (r + 1) * LANES]
    for c in range(3):
        for r in range(ROWS):
            so[c, r : r + 1, :] = offs[c : c + 1, r * LANES : (r + 1) * LANES]
    fx, fy = lax.axis_index("bx") * CX, lax.axis_index("by") * CY
    lx = [((sb[k] >> 8) - fx + 1) & (NXC - 1) for k in range(4)]
    ly = [((sb[k] & (NYC - 1)) - fy + 1) & (NYC - 1) for k in range(4)]
    qx = jnp.minimum(jnp.minimum(lx[0], lx[1]), jnp.minimum(lx[2], lx[3]))
    qy = jnp.minimum(jnp.minimum(ly[0], ly[1]), jnp.minimum(ly[2], ly[3]))
    at = qx * PAIR + qy * 4
    at = jnp.where(qy == CY, -1 - (2 * EDGE_X + EDGE_Y + 8 * qx), at)
    at = jnp.where(qy == 0, -1 - (2 * EDGE_X + 8 * qx), at)
    at = jnp.where(qx == CX, -1 - (EDGE_X + 4 * qy), at)
    at = jnp.where(qx == 0, -1 - 4 * qy, at)
    flat[...] = at
    to_scalar = pltpu.make_async_copy(flat, start, ssem)
    to_scalar.start()
    rel[0] = 2.0 * (so[0] + (lx[0] - qx).astype(f32))
    rel[1] = 2.0 * (so[1] + (ly[0] - qy).astype(f32))
    rel[2] = 2.0 * so[2]
    for i in range(ROWS // 8):
        p = pix[8 * i : 8 * i + 8, :]
        tile = p >> 8
        low, high = tile & (LANES - 1), tile >> 7
        slot = jnp.zeros((8, LANES), i32)
        for t in range(8):
            row = jnp.broadcast_to(tile_slot[t : t + 1, :], (8, LANES))
            slot = jnp.where(high == t, lane_take(row, low), slot)
        owner[8 * i : 8 * i + 8, :] = slot >> 3
        target[8 * i : 8 * i + 8, :] = (slot & 7) * 256 + (p & 255)
    sub = iota((OWNERS, LANES), 0)
    upper = (iota((LANES, 2 * LANES), 0) <= iota((LANES, 2 * LANES), 1)).astype(f32).astype(bf16)

    def ranks(r, seen):
        hit = sub == jnp.broadcast_to(owner[pl.ds(r, 1), :], (OWNERS, LANES))
        tally = jnp.dot(jnp.where(hit, 1.0, 0.0).astype(bf16), upper, preferred_element_type=f32)
        rank[pl.ds(r, 1), :] = (
            jnp.sum(jnp.where(hit, tally[:, :LANES] + seen, 0.0), axis=0, keepdims=True) - 1.0
        ).astype(i32)
        return seen + tally[:, LANES:]

    lax.fori_loop(0, ROWS, ranks, jnp.zeros((OWNERS, LANES), f32), unroll=4)
    square[:CX, :CY] = counts[...].astype(f32)
    filled = jnp.transpose(square[...])[:CY, :].astype(i32)
    lane = iota((CY, LANES), 1)

    def row(c, x, y, right):
        return x * PAIR + (c // 2) * TWO + y * 4 + 2 * right + c % 2

    def column(x, _):
        live = lane < lane_take(filled, jnp.full((CY, LANES), x, i32))
        for c in range(6):
            v = photons[c, x]
            v = v + v if c < 3 else jnp.where(live, v, 0.0)
            table[pl.ds(row(c, x + 1, 1, 0), CY, stride=4), :] = v
            table[pl.ds(row(c, x, 1, 1), CY, stride=4), :] = v
        return 0

    for k in range(CHUNKS):
        reads[k].wait()
        lax.fori_loop(k * part, (k + 1) * part, column, 0, unroll=2)
    to_scalar.wait()
    zero = lax.axis_index("bx") * 0

    def fetch(i, count, stage, near):
        for u in range(GROUPS):
            g = jnp.minimum(i * GROUPS + u, POINTS // 8 - 1)
            v, lane = g >> 7, g & (LANES - 1)
            take = jnp.full((8, LANES), lane, i32)
            for c in range(3):
                near[u, c] = lane_take(rel[c, pl.ds(v, 8, stride=4), :], take)
            for s in range(8):
                at = start[4 * s + v, lane]
                points[count] = g + 512 * s
                places[count] = -1 - at
                count = count + lax.shift_right_logical(at, 31)
                r = jnp.maximum(at, 0)
                for j in range(3):
                    stage[u, j, pl.ds(zero + STEP * s, 8), :] = table[pl.ds(r + j * TWO, 8), :]
        return count

    def weigh(i, stage, near):
        for u in range(GROUPS):
            total = weigh_eight(stage.at[u], [near[u, c] for c in range(3)])
            for c in range(3):
                sums[c, pl.ds(i * GROUPS + u, 8, stride=APART), :] = total[c]

    def step(i, count):
        weigh(2 * i, stage_a, near_a)
        count = fetch(2 * i + 1, count, stage_b, near_b)
        weigh(2 * i + 1, stage_b, near_b)
        return fetch(2 * i + 2, count, stage_a, near_a)

    count = fetch(0, 0, stage_a, near_a)
    points[LIST - 1] = lax.fori_loop(0, POINTS // 16 // GROUPS, step, count)


def outer_kernel(points, places, sums, rel, alb, owner, rank, target, xm, xp, c0, c63, ym, yp, bottom, top,
                 send, edge, stage, rad):
    for c in range(6):
        scale = 2.0 if c < 3 else 1.0
        plane = (c // 2) * EDGE + c % 2
        for base, cols in ((0, ((xm, 0), (c0, 1))), (EDGE_X, ((c63, CX), (xp, CX + 1)))):
            for right, (col, x) in enumerate(cols):
                at = plane + base + 2 * right
                edge[pl.ds(at + 4, CY, stride=4), :] = col[c] * scale
                edge[at : at + 1, :] = ym[c, x : x + 1] * scale
                edge[at + 4 * EY - 4 : at + 4 * EY - 3, :] = yp[c, x : x + 1] * scale
        for base, lines in ((2 * EDGE_X, (ym, bottom)), (2 * EDGE_X + EDGE_Y, (top, yp))):
            for yy, line in enumerate(lines):
                for right in range(2):
                    at = plane + base + 4 * yy + 2 * right
                    edge[pl.ds(at, CX + 1, stride=8), :] = line[c, right : right + CX + 1] * scale
    sub = iota((8, LANES), 0)
    zero = lax.axis_index("bx") * 0
    count = points[LIST - 1]

    def eight(i, _):
        close = [jnp.zeros((8, LANES), f32)] * 3
        where = []
        for s in range(8):
            k = jnp.minimum(8 * i + s, count - 1)
            p, r = points[k], places[k]
            where.append((p >> 9) * APART + (p & 511))
            take = jnp.full((8, LANES), p & (LANES - 1), i32)
            for c in range(3):
                line = jnp.broadcast_to(rel[c, pl.ds(p >> 7, 1), :], (8, LANES))
                close[c] = jnp.where(sub == s, lane_take(line, take), close[c])
            for j in range(3):
                stage[j, pl.ds(zero + STEP * s, 8), :] = edge[pl.ds(r + j * EDGE, 8), :]
        total = weigh_eight(stage, close)
        for c in range(3):
            for s in range(8):
                sums[c, pl.ds(where[s], 1), :] = total[c][s : s + 1]
        return 0

    lax.fori_loop(0, (count + 7) >> 3, eight, 0)
    ones = jnp.ones((8, 2 * LANES), f32).astype(bf16)

    def lane_sums(r, _):
        for c in range(3):
            for k in range(2):
                line = 2 * r + k
                x = sums[c, pl.ds((line >> 2) * APART + (line & 3) * LANES, LANES), :]
                high = x.astype(bf16)
                low = (x - high.astype(f32)).astype(bf16)
                both = jnp.concatenate([high, low], axis=1)
                y = lax.dot_general(ones, both, NT, preferred_element_type=f32)
                rad[c, pl.ds(line, 1), :] = y[:1]
        return 0

    lax.fori_loop(0, ROWS // 2, lane_sums, 0)
    for c in range(3):
        for r in range(ROWS):
            rad[c, r : r + 1, :] = rad[c, r : r + 1, :] * alb[c : c + 1, r * LANES : (r + 1) * LANES]
    wide_sub = iota((OWNERS, 2 * LANES), 0)
    rank_sub = iota((CAP, 2 * LANES), 0)

    def two(ref, r):
        return jnp.concatenate([ref[pl.ds(2 * r, 1), :], ref[pl.ds(2 * r + 1, 1), :]], axis=1)

    def scatter(r, total):
        mine = jnp.where(wide_sub == two(owner, r), 1.0, 0.0).astype(bf16)
        hit = rank_sub == two(rank, r)
        where = two(target, r)
        vals = [two(rad.at[c], r) for c in range(3)]
        high = [x.astype(bf16).astype(f32) for x in vals]
        low = [x - h for x, h in zip(vals, high)]
        high.append((where & ~255).astype(f32))
        low.append((where & 255).astype(f32))
        for part in (high, low):
            rows = jnp.concatenate([jnp.where(hit, x, 0.0) for x in part], axis=0).astype(bf16)
            total = total + lax.dot_general(mine, rows, NT, preferred_element_type=f32)
        return total

    send[:, 0, :] = lax.fori_loop(0, ROWS // 2, scatter, jnp.zeros((OWNERS, 4 * CAP), f32), unroll=2)


def film_kernel(got, film, flipped, total):
    for j in range(3):
        flipped[LANES * j : LANES * j + LANES, :] = jnp.transpose(got[:, 0, LANES * j : LANES * j + LANES])
    lo_sub = iota((LANES, 2 * LANES), 0)
    hi_sub = iota((16, 2 * LANES), 0)

    def two(row):
        return jnp.concatenate(
            [flipped[pl.ds(row, 1), :], flipped[pl.ds(row + CAP // 2, 1), :]], axis=1
        )

    def step(k, acc):
        where = two(3 * CAP + k).astype(i32)
        low_hit = jnp.where(lo_sub == (where & 127), 1.0, 0.0).astype(bf16)
        hit = hi_sub == (where >> 7)
        high, low = [], []
        for c in range(3):
            x = two(c * CAP + k)
            h = x.astype(bf16).astype(f32)
            high.append(jnp.where(hit, h, 0.0))
            low.append(jnp.where(hit, x - h, 0.0))
        rows = jnp.concatenate(high + low, axis=0).astype(bf16)
        return acc + lax.dot_general(rows, low_hit, NT, preferred_element_type=f32)

    acc = lax.fori_loop(0, CAP // 2, step, jnp.zeros((96, LANES), f32), unroll=4)
    total[...] = acc[:48] + acc[48:]
    for c in range(3):
        film[c, :, :LANES] = total[pl.ds(16 * c, 8, stride=2), :]
        film[c, :, LANES:] = total[pl.ds(16 * c + 1, 8, stride=2), :]


def shift(x, axis, by):
    n = lax.axis_size(axis)
    return lax.ppermute(x, axis, [(i, (i + by) % n) for i in range(n)])


def live_only(x, counts):
    slots = lax.broadcasted_iota(i32, x.shape[1:], x.ndim - 2)
    return jnp.concatenate([x[:3], jnp.where(slots < counts[..., None], x[3:], 0.0)], axis=0)


def per_device(photon_data, block_counts, gather_offsets, gather_blocks, albedo, gather_pixels, tile_slot):
    small_i = jax.ShapeDtypeStruct((ROWS, LANES), i32)
    listed = jax.ShapeDtypeStruct((LIST,), i32)
    c63 = live_only(photon_data[:, -1], block_counts[-1])
    c0 = live_only(photon_data[:, 0], block_counts[0])
    xm, xp = shift(c63, "bx", 1), shift(c0, "bx", -1)
    top = live_only(photon_data[:, :, -1], block_counts[:, -1])
    bottom = live_only(photon_data[:, :, 0], block_counts[:, 0])
    top = jnp.concatenate([xm[:, -1:], top, xp[:, -1:]], axis=1)
    bottom = jnp.concatenate([xm[:, :1], bottom, xp[:, :1]], axis=1)
    ym, yp = shift(top, "by", 1), shift(bottom, "by", -1)
    sums, rel, owner, rank, target, points, places = pl.pallas_call(
        inner_kernel,
        in_specs=[HBM] + [VMEM] * 5,
        out_specs=[VMEM] * 5 + [SMEM] * 2,
        out_shape=[
            jax.ShapeDtypeStruct((3, 8 * APART, LANES), f32),
            jax.ShapeDtypeStruct((3, ROWS, LANES), f32),
            small_i, small_i, small_i, listed, listed,
        ],
        scratch_shapes=[
            pltpu.VMEM((6, CX, CY, LANES), f32),
            pltpu.VMEM((TABLE_ROWS, LANES), f32),
            pltpu.VMEM((4, ROWS, LANES), i32),
            pltpu.VMEM((3, ROWS, LANES), f32),
            pltpu.VMEM((LANES, LANES), f32),
            pltpu.VMEM((ROWS, LANES), i32),
            pltpu.VMEM((GROUPS, 3, 8 * STEP + 8, LANES), f32),
            pltpu.VMEM((GROUPS, 3, 8 * STEP + 8, LANES), f32),
            pltpu.VMEM((GROUPS, 3, 8, LANES), f32),
            pltpu.VMEM((GROUPS, 3, 8, LANES), f32),
            pltpu.SMEM((ROWS, LANES), i32),
            pltpu.SemaphoreType.DMA((CHUNKS,)),
            pltpu.SemaphoreType.DMA,
        ],
        compiler_params=params(34),
        cost_estimate=pl.CostEstimate(flops=60_000_000, bytes_accessed=7_000_000, transcendentals=0),
        name="inner",
    )(photon_data, block_counts, gather_blocks, gather_offsets,
      gather_pixels.reshape(ROWS, LANES), tile_slot.reshape(8, LANES))
    send = pl.pallas_call(
        outer_kernel,
        in_specs=[SMEM] * 2 + [VMEM] * 14,
        out_specs=VMEM,
        out_shape=jax.ShapeDtypeStruct((OWNERS, 1, 4 * CAP), f32),
        scratch_shapes=[
            pltpu.VMEM((3 * EDGE + 8, LANES), f32),
            pltpu.VMEM((3, 8 * STEP + 8, LANES), f32),
            pltpu.VMEM((3, ROWS, LANES), f32),
        ],
        compiler_params=params(16),
        name="outer",
    )(points, places, sums, rel, albedo, owner, rank, target, xm, xp, c0, c63, ym, yp, bottom, top)
    got = lax.all_to_all(send, AXES, 0, 0, tiled=True)
    return pl.pallas_call(
        film_kernel,
        in_specs=[VMEM],
        out_specs=VMEM,
        out_shape=jax.ShapeDtypeStruct((3, 8, 256), f32),
        scratch_shapes=[pltpu.VMEM((4 * CAP, LANES), f32), pltpu.VMEM((48, LANES), f32)],
        compiler_params=params(16),
        name="film",
    )(got)


def solution(mesh):
    in_specs = (P(None, "bx", "by", None), P("bx", "by"), P(None, AXES), P(None, AXES), P(None, AXES), P(AXES), P())
    return jax.shard_map(per_device, mesh=mesh, in_specs=in_specs, out_specs=P(None, AXES, None), check_vma=False)
```

time: 76.7 us -> 88.2 us (1.15)
  Pallas kernels: 33.7 us -> 44.7 us
  local copies, waits for them, and re-layouts: 10.1 us -> 11.4 us
    pallas_call x2, Pallas kernels: 29.2 us -> 41.1 us  [the longest x1 29 us: per_device(): pl.pallas_call(inner_kernel, in_specs=[HBM] + [VMEM] * 5, out_specs=[VMEM...]
    unnamed x8 -> x13, local copies, waits for them, and re-layouts: 0.7 us -> 6.67 us
    pad x2 -> x0, local copies, waits for them, and re-layouts: 2.64 us -> none  [the longest x1 1.32 us: per_device(): jnp.pad(start.reshape(POINTS), (0, LANES))]
    reshape x2 -> x0, local copies, waits for them, and re-layouts: 2.09 us -> none  [per_device(): rel = rel.reshape(3, 4, LANES, 8).transpose(1, 0, 3, 2)]
    pallas_call x1, Pallas kernels: 4.52 us -> 3.6 us  [per_device(): pl.pallas_call(film_kernel, in_specs=[VMEM], out_specs=VMEM, out_shape=ja...]
  transfers between devices with their start and end apart: 4 -> 4, of which waited for: 2 -> 1; matrix products, arithmetic and copies ran while one was open for 11% -> 4% of each run, Pallas kernels for 5% -> 33%
where the time goes in v3:
time: 88.2 us; the launch traced here: 87.6 us
  Pallas kernels  44.7 us (51%)
  blocking collectives  19.2 us (22%)
  local copies, waits for them, and re-layouts  11.4 us (13%)
  starting transfers between devices  9.34 us (11%)
  waiting for transfers between devices  1.78 us (2%)
  other arithmetic  1.09 us (1%)
    pallas_call x1, Pallas kernels, per_device(): pl.pallas_call(inner_kernel, in_specs=[HBM] + [VMEM] * 5, out_specs=[VMEM...  29 us
    all_to_all x1, blocking collectives, per_device(): got = lax.all_to_all(send, AXES, 0, 0, tiled=True)  19.2 us
    pallas_call x1, Pallas kernels, per_device(): pl.pallas_call(outer_kernel, in_specs=[SMEM] * 2 + [VMEM] * 14, out_specs...  12.1 us
    ppermute x4, starting transfers between devices, shift(): return lax.ppermute(x, axis, [(i, (i + by) % n) for i in range(n)])  9.34 us
    unnamed x13, local copies, waits for them, and re-layouts  6.67 us
    pallas_call x1, Pallas kernels, per_device(): pl.pallas_call(film_kernel, in_specs=[VMEM], out_specs=VMEM, out_shape=ja...  3.6 us
    slice x2, local copies, waits for them, and re-layouts, live_only(): x[:3]  2.99 us
    ppermute x4, waiting for transfers between devices, shift(): return lax.ppermute(x, axis, [(i, (i + by) % n) for i in range(n)])  1.78 us
  transfers between devices with their start and end apart: 4, of which 1 were waited for; matrix products, arithmetic and copies ran while one was open for 4% of the time, Pallas kernels for 33%

profile of v3, /device:TPU:1, one launch (start us, length us, event | category | flops | bytes accessed | tf_op | source)
XLA Modules:
  0.0 87.6 jit_solution(4524049077090012381)
XLA Ops:
  0.0 0.0 copy-start.3
  0.0 1.0 %slice_reduce_fusion = (s32[32]{0:T(128)S(1)}, s32[32]{0:T(128)S(1)}) fusion(s32[64,32]{0,1:T(8,128)} %param.8), kind=kLoop, calls=%fused_computation.12 | loop fusion | bytes 512 | tf_op jit(solution)/shard_map/slice | solution.py:301
  1.0 0.8 slice_bitcast_fusion
  1.8 0.1 iota_compare_fusion.2
  1.9 0.8 bitcast_select_fusion
  2.7 3.1 %collective-permute-start = (f32[6,32,128]{2,1,0:T(8,128)S(1)}, f32[6,32,128]{2,1,0:T(8,128)S(1)}, u32[]{:S(2)}, u32[]{:S(2)}) collective-permute-start(f32[6,32,128]{2,1,0:T(8,128)S(1)} %pad_maximum_fusion.2.c63), channel_id=1, source_target_pairs={{0,8},{8,16},{16,24},{24,32},{32,40},{40,48},{48,56},{56,64},{64,7... | collective-permute-start | bytes 294920 | tf_op jit(solution)/shard_map/ppermute | solution.py:289
  5.8 0.1 collective-permute-start.1
  5.9 0.7 slice_bitcast_fusion.2
  6.6 2.2 %fusion = (f32[3,64,1,128]{3,2,1,0:T(1,128)S(1)}, f32[3,64,1,128]{3,2,1,0:T(1,128)S(1)}, f32[3,64,1,128]{3,2,1,0:T(1,128)S(1)}, f32[3,64,1,128]{3,2,1,0:T(1,128)S(1)}) fusion(f32[6,64,32,128]{3,2,1,0:T(8,128)} %ph.1), kind=kLoop, calls=%fused_computation.18 | loop fusion | bytes 786432 | tf_op jit(solution)/shard_map/slice | solution.py:294
  8.8 0.1 iota_compare_fusion
  8.9 0.0 collective-permute-done.xm
  8.9 1.8 %collective-permute-done.1.xp = f32[6,32,128]{2,1,0:T(8,128)S(1)} collective-permute-done((f32[6,32,128]{2,1,0:T(8,128)S(1)}, f32[6,32,128]{2,1,0:T(8,128)S(1)}, u32[]{:S(2)}, u32[]{:S(2)}) %collective-permute-start.1) | collective-permute-done | bytes 98336 | tf_op jit(solution)/shard_map/ppermute | solution.py:289
  10.8 6.1 %collective-permute-start.3 = (f32[6,66,128]{2,1,0:T(8,128)S(1)}, f32[6,66,128]{2,1,0:T(8,128)S(1)}, u32[]{:S(2)}, u32[]{:S(2)}) collective-permute-start(f32[6,66,128]{2,1,0:T(8,128)S(1)} %pad_maximum_fusion.1.bottom), channel_id=1, source_target_pairs={{0,7},{1,0},{2,1},{3,2},{4,3},{5,4},{6,5},{7,6},{8,15},{9,8},{10,9... | collective-permute-start | bytes 608264 | tf_op jit(solution)/shard_map/ppermute | solution.py:289
  16.9 0.1 collective-permute-start.2
  17.0 0.8 copy.17.counts
  17.8 0.0 copy-start
  17.8 2.8 %copy-done = f32[6,64,32,128]{3,2,1,0:T(8,128)S(1)} copy-done((f32[6,64,32,128]{3,2,1,0:T(8,128)S(1)}, f32[6,64,32,128]{3,2,1,0:T(8,128)}, u32[]{:S(2)}) %copy-start) | copy-done | bytes 6291480
  20.6 0.0 copy-start.1
  20.6 0.8 copy-done.1
  21.4 0.0 copy-start.2
  21.4 0.8 copy-done.2
  22.2 0.0 copy-start.4
  22.2 0.7 copy-done.4
  23.0 0.0 copy-start.5
  23.0 0.7 copy-done.5
  23.6 29.0 %inner.1 = (f32[3,4104,128]{2,1,0:T(8,128)S(1)}, f32[3,32,128]{2,1,0:T(8,128)S(1)}, s32[32,128]{1,0:T(8,128)S(1)}, s32[32,128]{1,0:T(8,128)S(1)}, s32[32,128]{1,...) custom-call(f32[6,64,32,128]{3,2,1,0:T(8,128)S(1)} %copy-done, s32[64,32]{1,0:T(8,128)S(1)} %copy.17.counts, ...), custom_call_target="tpu_custom_call" | custom-call | flops 60000000 | bytes 7000000 | tf_op jit(solution)/shard_map/inner/pallas_call | solution.py:308
  52.7 0.0 collective-permute-done.3.yp
  52.7 0.0 collective-permute-done.2.ym
  52.7 0.0 copy-done.3
  52.7 12.1 %outer.1 = f32[128,1,384]{2,1,0:T(1,128)S(1)} custom-call(s32[4224]{0:T(1024)S(1)} %get-tuple-element.12.points, s32[4224]{0:T(1024)S(1)} %get-tuple-element.13.places, f32[3,4104,128]{2,1,0:T(8,128)S(1)} %get-tuple-element.14.sums, f32[3,32,128]{2,1,0:T(8,128)S(1)} %get-tuple-element.15.rel, f32[3,4096]{1,0:T(4,128)S(1)} %copy-done.3, ...), custom_call_target="tpu_custom_call" | custom-call | tf_op jit(solution)/shard_map/outer/pallas_call | solution.py:337
  64.8 19.2 %all_to_all.5.got = f32[128,1,384]{2,1,0:T(1,128)S(1)} all-to-all(f32[128,1,384]{2,1,0:T(1,128)S(1)} %outer.1), channel_id=1, replica_groups=mesh['bx'=16,'by'=8] {'bx','by'}, dimensions={0} | all-to-all | bytes 393216 | tf_op jit(solution)/shard_map/all_to_all | solution.py:350
  84.1 3.6 %film.1 = f32[3,8,256]{2,1,0:T(8,128)} custom-call(f32[128,1,384]{2,1,0:T(1,128)S(1)} %all_to_all.5.got), custom_call_target="tpu_custom_call" | custom-call | tf_op jit(solution)/shard_map/film/pallas_call | solution.py:351
  (8 shorter events, 0.1 us)
Async XLA Ops:
  0.0 52.7 %copy-start.3 = (f32[3,4096]{1,0:T(4,128)S(1)}, f32[3,4096]{1,0:T(4,128)}, u32[]{:S(2)}) copy-start(f32[3,4096]{1,0:T(4,128)} %alb.1) | copy-start | bytes 147460
  2.7 6.2 %collective-permute-start = (f32[6,32,128]{2,1,0:T(8,128)S(1)}, f32[6,32,128]{2,1,0:T(8,128)S(1)}, u32[]{:S(2)}, u32[]{:S(2)}) collective-permute-start(f32[6,32,128]{2,1,0:T(8,128)S(1)} %pad_maximum_fusion.2.c63), channel_id=1, source_target_pairs={{0,8},{8,16},{16,24},{24,32},{32,40},{40,48},{48,56},{56,64},{64,7... | collective-permute-start | bytes 294920 | tf_op jit(solution)/shard_map/ppermute | solution.py:289
  5.8 4.9 %collective-permute-start.1 = (f32[6,32,128]{2,1,0:T(8,128)S(1)}, f32[6,32,128]{2,1,0:T(8,128)S(1)}, u32[]{:S(2)}, u32[]{:S(2)}) collective-permute-start(f32[6,32,128]{2,1,0:T(8,128)S(1)} %pad_maximum_fusion.3.c0), channel_id=1, source_target_pairs={{0,120},{8,0},{16,8},{24,16},{32,24},{40,32},{48,40},{56,48},{64,5... | collective-permute-start | bytes 294920 | tf_op jit(solution)/shard_map/ppermute | solution.py:289
  10.8 41.9 %collective-permute-start.3 = (f32[6,66,128]{2,1,0:T(8,128)S(1)}, f32[6,66,128]{2,1,0:T(8,128)S(1)}, u32[]{:S(2)}, u32[]{:S(2)}) collective-permute-start(f32[6,66,128]{2,1,0:T(8,128)S(1)} %pad_maximum_fusion.1.bottom), channel_id=1, source_target_pairs={{0,7},{1,0},{2,1},{3,2},{4,3},{5,4},{6,5},{7,6},{8,15},{9,8},{10,9... | collective-permute-start | bytes 608264 | tf_op jit(solution)/shard_map/ppermute | solution.py:289
  16.9 35.8 %collective-permute-start.2 = (f32[6,66,128]{2,1,0:T(8,128)S(1)}, f32[6,66,128]{2,1,0:T(8,128)S(1)}, u32[]{:S(2)}, u32[]{:S(2)}) collective-permute-start(f32[6,66,128]{2,1,0:T(8,128)S(1)} %pad_maximum_fusion.top), channel_id=1, source_target_pairs={{0,1},{1,2},{2,3},{3,4},{4,5},{5,6},{6,7},{7,0},{8,9},{9,10},{10,1... | collective-permute-start | bytes 608264 | tf_op jit(solution)/shard_map/ppermute | solution.py:289
  17.8 2.8 %copy-start = (f32[6,64,32,128]{3,2,1,0:T(8,128)S(1)}, f32[6,64,32,128]{3,2,1,0:T(8,128)}, u32[]{:S(2)}) copy-start(f32[6,64,32,128]{3,2,1,0:T(8,128)} %ph.1) | copy-start | bytes 18874372
  20.6 0.8 copy-start.1
  21.4 0.8 copy-start.2
  22.2 0.7 copy-start.4
  23.0 0.7 copy-start.5

commit v4 on v3

--- a/solution.py
+++ b/solution.py
@@ -20,10 +20,9 @@
 APART = 513
 EDGE_X, EDGE_Y = 4 * EY, 8 * (CX + 1)
 EDGE = 2 * EDGE_X + 2 * EDGE_Y
-LIST = POINTS + 128
-CHUNKS = 8
+LIST = ROWS + 8
 STEP = 9
-GROUPS = 2
+GROUPS = 4
 i32, f32, bf16 = jnp.int32, jnp.float32, jnp.bfloat16
 VMEM = pl.BlockSpec(memory_space=pltpu.VMEM)
 SMEM = pl.BlockSpec(memory_space=pltpu.SMEM)
@@ -34,7 +33,7 @@
 
 
 def params(mib):
-    return pltpu.CompilerParams(vmem_limit_bytes=mib * 1024 * 1024)
+    return pltpu.CompilerParams(vmem_limit_bytes=int(mib * 1024 * 1024))
 
 
 def iota(shape, dim):
@@ -64,15 +63,21 @@
     return total
 
 
-def inner_kernel(ph, counts, blocks, offs, pix, tile_slot, sums, rel, owner, rank, target, points, places,
-                 photons, table, sb, so, square, flat, stage_a, stage_b, near_a, near_b, start, psem, ssem):
-    part = CX // CHUNKS
-    reads = [
-        pltpu.make_async_copy(ph.at[:, pl.ds(k * part, part)], photons.at[:, pl.ds(k * part, part)], psem.at[k])
-        for k in range(CHUNKS)
-    ]
-    for read in reads:
-        read.start()
+def prep_kernel(ph, counts, blocks, offs, pix, tile_slot,
+                c63, c0, top, bottom, flat, rel, owner, rank, target, points, places, square, sb, so, where):
+    square[:CX, :CY] = counts[...].astype(f32)
+    by_x = square[:CX, :].astype(i32)
+    by_y = jnp.transpose(square[...])[:CY, :].astype(i32)
+    for out, x in ((c63, CX - 1), (c0, 0)):
+        live = iota((CY, LANES), 1) < lane_take(by_y, jnp.full((CY, LANES), x, i32))
+        for c in range(6):
+            v = ph[c, x]
+            out[c] = v if c < 3 else jnp.where(live, v, 0.0)
+    for out, y in ((top, CY - 1), (bottom, 0)):
+        live = iota((CX, LANES), 1) < lane_take(by_x, jnp.full((CX, LANES), y, i32))
+        for c in range(6):
+            v = ph[c, :, y, :]
+            out[c] = v if c < 3 else jnp.where(live, v, 0.0)
     for k in range(4):
         for r in range(ROWS):
             sb[k, r : r + 1, :] = blocks[k : k + 1, r * LANES : (r + 1) * LANES]
@@ -89,9 +94,7 @@
     at = jnp.where(qy == 0, -1 - (2 * EDGE_X + 8 * qx), at)
     at = jnp.where(qx == CX, -1 - (EDGE_X + 4 * qy), at)
     at = jnp.where(qx == 0, -1 - 4 * qy, at)
-    flat[...] = at
-    to_scalar = pltpu.make_async_copy(flat, start, ssem)
-    to_scalar.start()
+    flat[...] = jnp.maximum(at, 0)
     rel[0] = 2.0 * (so[0] + (lx[0] - qx).astype(f32))
     rel[1] = 2.0 * (so[1] + (ly[0] - qy).astype(f32))
     rel[2] = 2.0 * so[2]
@@ -116,7 +119,41 @@
         ).astype(i32)
         return seen + tally[:, LANES:]
 
-    lax.fori_loop(0, ROWS, ranks, jnp.zeros((OWNERS, LANES), f32), unroll=4)
+    lax.fori_loop(0, ROWS, ranks, jnp.zeros((OWNERS, LANES), f32), unroll=16)
+    outside = at < 0
+    tally = jnp.dot(jnp.where(outside, 1.0, 0.0).astype(bf16), upper, preferred_element_type=f32)
+    before = iota((ROWS, ROWS), 1) < iota((ROWS, ROWS), 0)
+    ahead = jnp.dot(
+        jnp.where(before, 1.0, 0.0).astype(bf16), tally[:, LANES:].astype(bf16), preferred_element_type=f32
+    )
+    count = (ahead + tally[:, LANES:])[ROWS - 1 :].astype(i32)
+    where[0] = jnp.where(outside, (ahead + tally[:, :LANES] - 1.0).astype(i32), -1)
+    where[1] = iota((ROWS, LANES), 0) * LANES + iota((ROWS, LANES), 1)
+    where[2] = -1 - at
+    low_sub = iota((LANES, 2 * LANES), 0)
+    high_sub = iota((ROWS, 2 * LANES), 0)
+
+    def collect(r, total):
+        spot, point, place = [
+            jnp.concatenate([where[k, pl.ds(2 * r, 1), :], where[k, pl.ds(2 * r + 1, 1), :]], axis=1)
+            for k in range(3)
+        ]
+        low_hit = jnp.where(low_sub == (spot & (LANES - 1)), 1.0, 0.0).astype(bf16)
+        hit = high_sub == (spot >> 7)
+        parts = [(point >> 8), (point & 255), (place >> 8), (place & 255)]
+        rows = jnp.concatenate([jnp.where(hit, x.astype(f32), 0.0) for x in parts], axis=0).astype(bf16)
+        return total + lax.dot_general(rows, low_hit, NT, preferred_element_type=f32)
+
+    found = lax.fori_loop(0, ROWS // 2, collect, jnp.zeros((4 * ROWS, LANES), f32), unroll=8).astype(i32)
+    points[:ROWS] = found[:ROWS] * 256 + found[ROWS : 2 * ROWS]
+    places[:ROWS] = found[2 * ROWS : 3 * ROWS] * 256 + found[3 * ROWS :]
+    points[ROWS:] = jnp.broadcast_to(count, (8, LANES))
+    places[ROWS:] = jnp.broadcast_to(count, (8, LANES))
+
+def inner_kernel(ph, counts, flat, rel, sums, near, table, square, stage_a, stage_b, ssem, *start):
+    to_scalar = [pltpu.make_async_copy(flat.at[pl.ds(4 * s, 4)], start[s], ssem.at[s]) for s in range(8)]
+    for copy in to_scalar:
+        copy.start()
     square[:CX, :CY] = counts[...].astype(f32)
     filled = jnp.transpose(square[...])[:CY, :].astype(i32)
     lane = iota((CY, LANES), 1)
@@ -127,53 +164,56 @@
     def column(x, _):
         live = lane < lane_take(filled, jnp.full((CY, LANES), x, i32))
         for c in range(6):
-            v = photons[c, x]
+            v = ph[c, x]
             v = v + v if c < 3 else jnp.where(live, v, 0.0)
             table[pl.ds(row(c, x + 1, 1, 0), CY, stride=4), :] = v
             table[pl.ds(row(c, x, 1, 1), CY, stride=4), :] = v
         return 0
 
-    for k in range(CHUNKS):
-        reads[k].wait()
-        lax.fori_loop(k * part, (k + 1) * part, column, 0, unroll=2)
-    to_scalar.wait()
+    lax.fori_loop(0, CX, column, 0, unroll=8)
+    for copy in to_scalar:
+        copy.wait()
     zero = lax.axis_index("bx") * 0
 
-    def fetch(i, count, stage, near):
+    parts = [[rel[c, pl.ds(v, 8, stride=4), :] for c in range(3)] for v in range(4)]
+
+    def spread(lane, _):
+        take = jnp.full((8, LANES), lane, i32)
+        for v in range(4):
+            for c in range(3):
+                near[c, v * LANES + lane] = lane_take(parts[v][c], take)
+        return 0
+
+    lax.fori_loop(0, LANES, spread, 0, unroll=8)
+
+    def fetch(i, stage):
         for u in range(GROUPS):
             g = jnp.minimum(i * GROUPS + u, POINTS // 8 - 1)
             v, lane = g >> 7, g & (LANES - 1)
-            take = jnp.full((8, LANES), lane, i32)
-            for c in range(3):
-                near[u, c] = lane_take(rel[c, pl.ds(v, 8, stride=4), :], take)
             for s in range(8):
-                at = start[4 * s + v, lane]
-                points[count] = g + 512 * s
-                places[count] = -1 - at
-                count = count + lax.shift_right_logical(at, 31)
-                r = jnp.maximum(at, 0)
+                r = start[s][v, lane]
                 for j in range(3):
                     stage[u, j, pl.ds(zero + STEP * s, 8), :] = table[pl.ds(r + j * TWO, 8), :]
-        return count
-
-    def weigh(i, stage, near):
+
+    def weigh(i, stage):
         for u in range(GROUPS):
-            total = weigh_eight(stage.at[u], [near[u, c] for c in range(3)])
+            total = weigh_eight(stage.at[u], [near[c, i * GROUPS + u] for c in range(3)])
             for c in range(3):
                 sums[c, pl.ds(i * GROUPS + u, 8, stride=APART), :] = total[c]
 
-    def step(i, count):
-        weigh(2 * i, stage_a, near_a)
-        count = fetch(2 * i + 1, count, stage_b, near_b)
-        weigh(2 * i + 1, stage_b, near_b)
-        return fetch(2 * i + 2, count, stage_a, near_a)
-
-    count = fetch(0, 0, stage_a, near_a)
-    points[LIST - 1] = lax.fori_loop(0, POINTS // 16 // GROUPS, step, count)
-
-
-def outer_kernel(points, places, sums, rel, alb, owner, rank, target, xm, xp, c0, c63, ym, yp, bottom, top,
-                 send, edge, stage, rad):
+    def step(i, _):
+        weigh(2 * i, stage_a)
+        fetch(2 * i + 1, stage_b)
+        weigh(2 * i + 1, stage_b)
+        fetch(2 * i + 2, stage_a)
+        return 0
+
+    fetch(0, stage_a)
+    lax.fori_loop(0, POINTS // 16 // GROUPS, step, 0)
+
+
+def outer_kernel(points, places, sums, near, alb, owner, rank, target, xm, xp, c0, c63, ym, yp, bottom, top,
+                 send, edge, stage, close, rad):
     for c in range(6):
         scale = 2.0 if c < 3 else 1.0
         plane = (c // 2) * EDGE + c % 2
@@ -190,22 +230,19 @@
                     edge[pl.ds(at, CX + 1, stride=8), :] = line[c, right : right + CX + 1] * scale
     sub = iota((8, LANES), 0)
     zero = lax.axis_index("bx") * 0
-    count = points[LIST - 1]
+    count = points[ROWS, 0]
 
     def eight(i, _):
-        close = [jnp.zeros((8, LANES), f32)] * 3
         where = []
         for s in range(8):
             k = jnp.minimum(8 * i + s, count - 1)
-            p, r = points[k], places[k]
+            p, r = points[k >> 7, k & (LANES - 1)], places[k >> 7, k & (LANES - 1)]
             where.append((p >> 9) * APART + (p & 511))
-            take = jnp.full((8, LANES), p & (LANES - 1), i32)
             for c in range(3):
-                line = jnp.broadcast_to(rel[c, pl.ds(p >> 7, 1), :], (8, LANES))
-                close[c] = jnp.where(sub == s, lane_take(line, take), close[c])
+                close[c, s : s + 1, :] = near[c, p & 511, pl.ds(p >> 9, 1), :]
             for j in range(3):
                 stage[j, pl.ds(zero + STEP * s, 8), :] = edge[pl.ds(r + j * EDGE, 8), :]
-        total = weigh_eight(stage, close)
+        total = weigh_eight(stage, [close[c] for c in range(3)])
         for c in range(3):
             for s in range(8):
                 sums[c, pl.ds(where[s], 1), :] = total[c][s : s + 1]
@@ -226,7 +263,7 @@
                 rad[c, pl.ds(line, 1), :] = y[:1]
         return 0
 
-    lax.fori_loop(0, ROWS // 2, lane_sums, 0)
+    lax.fori_loop(0, ROWS // 2, lane_sums, 0, unroll=8)
     for c in range(3):
         for r in range(ROWS):
             rad[c, r : r + 1, :] = rad[c, r : r + 1, :] * alb[c : c + 1, r * LANES : (r + 1) * LANES]
@@ -250,7 +287,7 @@
             total = total + lax.dot_general(mine, rows, NT, preferred_element_type=f32)
         return total
 
-    send[:, 0, :] = lax.fori_loop(0, ROWS // 2, scatter, jnp.zeros((OWNERS, 4 * CAP), f32), unroll=2)
+    send[:, 0, :] = lax.fori_loop(0, ROWS // 2, scatter, jnp.zeros((OWNERS, 4 * CAP), f32), unroll=8)
 
 
 def film_kernel(got, film, flipped, total):
@@ -277,7 +314,7 @@
         rows = jnp.concatenate(high + low, axis=0).astype(bf16)
         return acc + lax.dot_general(rows, low_hit, NT, preferred_element_type=f32)
 
-    acc = lax.fori_loop(0, CAP // 2, step, jnp.zeros((96, LANES), f32), unroll=4)
+    acc = lax.fori_loop(0, CAP // 2, step, jnp.zeros((96, LANES), f32), unroll=16)
     total[...] = acc[:48] + acc[48:]
     for c in range(3):
         film[c, :, :LANES] = total[pl.ds(16 * c, 8, stride=2), :]
@@ -289,64 +326,65 @@
     return lax.ppermute(x, axis, [(i, (i + by) % n) for i in range(n)])
 
 
-def live_only(x, counts):
-    slots = lax.broadcasted_iota(i32, x.shape[1:], x.ndim - 2)
-    return jnp.concatenate([x[:3], jnp.where(slots < counts[..., None], x[3:], 0.0)], axis=0)
-
-
 def per_device(photon_data, block_counts, gather_offsets, gather_blocks, albedo, gather_pixels, tile_slot):
     small_i = jax.ShapeDtypeStruct((ROWS, LANES), i32)
-    listed = jax.ShapeDtypeStruct((LIST,), i32)
-    c63 = live_only(photon_data[:, -1], block_counts[-1])
-    c0 = live_only(photon_data[:, 0], block_counts[0])
+    listed = jax.ShapeDtypeStruct((LIST, LANES), i32)
+    column, line = jax.ShapeDtypeStruct((6, CY, LANES), f32), jax.ShapeDtypeStruct((6, CX, LANES), f32)
+    c63, c0, top, bottom, flat, rel, owner, rank, target, points, places = pl.pallas_call(
+        prep_kernel,
+        in_specs=[VMEM] * 6,
+        out_specs=[VMEM] * 11,
+        out_shape=[column, column, line, line]
+        + [small_i, jax.ShapeDtypeStruct((3, ROWS, LANES), f32), small_i, small_i, small_i, listed, listed],
+        scratch_shapes=[
+            pltpu.VMEM((LANES, LANES), f32),
+            pltpu.VMEM((4, ROWS, LANES), i32),
+            pltpu.VMEM((3, ROWS, LANES), f32),
+            pltpu.VMEM((3, ROWS, LANES), i32),
+        ],
+        compiler_params=params(16),
+        cost_estimate=pl.CostEstimate(flops=20_000_000, bytes_accessed=300_000, transcendentals=0),
+        name="prep",
+    )(photon_data, block_counts, gather_blocks, gather_offsets,
+      gather_pixels.reshape(ROWS, LANES), tile_slot.reshape(8, LANES))
     xm, xp = shift(c63, "bx", 1), shift(c0, "bx", -1)
-    top = live_only(photon_data[:, :, -1], block_counts[:, -1])
-    bottom = live_only(photon_data[:, :, 0], block_counts[:, 0])
     top = jnp.concatenate([xm[:, -1:], top, xp[:, -1:]], axis=1)
     bottom = jnp.concatenate([xm[:, :1], bottom, xp[:, :1]], axis=1)
     ym, yp = shift(top, "by", 1), shift(bottom, "by", -1)
-    sums, rel, owner, rank, target, points, places = pl.pallas_call(
+    sums, near = pl.pallas_call(
         inner_kernel,
-        in_specs=[HBM] + [VMEM] * 5,
-        out_specs=[VMEM] * 5 + [SMEM] * 2,
+        in_specs=[VMEM] * 4,
+        out_specs=[VMEM] * 2,
         out_shape=[
             jax.ShapeDtypeStruct((3, 8 * APART, LANES), f32),
-            jax.ShapeDtypeStruct((3, ROWS, LANES), f32),
-            small_i, small_i, small_i, listed, listed,
+            jax.ShapeDtypeStruct((3, POINTS // 8, 8, LANES), f32),
         ],
         scratch_shapes=[
-            pltpu.VMEM((6, CX, CY, LANES), f32),
             pltpu.VMEM((TABLE_ROWS, LANES), f32),
-            pltpu.VMEM((4, ROWS, LANES), i32),
-            pltpu.VMEM((3, ROWS, LANES), f32),
             pltpu.VMEM((LANES, LANES), f32),
-            pltpu.VMEM((ROWS, LANES), i32),
             pltpu.VMEM((GROUPS, 3, 8 * STEP + 8, LANES), f32),
             pltpu.VMEM((GROUPS, 3, 8 * STEP + 8, LANES), f32),
-            pltpu.VMEM((GROUPS, 3, 8, LANES), f32),
-            pltpu.VMEM((GROUPS, 3, 8, LANES), f32),
-            pltpu.SMEM((ROWS, LANES), i32),
-            pltpu.SemaphoreType.DMA((CHUNKS,)),
-            pltpu.SemaphoreType.DMA,
-        ],
+            pltpu.SemaphoreType.DMA((8,)),
+        ]
+        + [pltpu.SMEM((4, LANES), i32)] * 8,
         compiler_params=params(34),
         cost_estimate=pl.CostEstimate(flops=60_000_000, bytes_accessed=7_000_000, transcendentals=0),
         name="inner",
-    )(photon_data, block_counts, gather_blocks, gather_offsets,
-      gather_pixels.reshape(ROWS, LANES), tile_slot.reshape(8, LANES))
+    )(photon_data, block_counts, flat, rel)
     send = pl.pallas_call(
         outer_kernel,
         in_specs=[SMEM] * 2 + [VMEM] * 14,
         out_specs=VMEM,
         out_shape=jax.ShapeDtypeStruct((OWNERS, 1, 4 * CAP), f32),
         scratch_shapes=[
-            pltpu.VMEM((3 * EDGE + 8, LANES), f32),
+            pltpu.VMEM((3 * EDGE + 64, LANES), f32),
             pltpu.VMEM((3, 8 * STEP + 8, LANES), f32),
+            pltpu.VMEM((3, 8, LANES), f32),
             pltpu.VMEM((3, ROWS, LANES), f32),
         ],
         compiler_params=params(16),
         name="outer",
-    )(points, places, sums, rel, albedo, owner, rank, target, xm, xp, c0, c63, ym, yp, bottom, top)
+    )(points, places, sums, near, albedo, owner, rank, target, xm, xp, c0, c63, ym, yp, bottom, top)
     got = lax.all_to_all(send, AXES, 0, 0, tiled=True)
     return pl.pallas_call(
         film_kernel,

time: 88.2 us -> 61.4 us (0.70)
  Pallas kernels: 44.7 us -> 23.7 us
  local copies, waits for them, and re-layouts: 11.4 us -> 6.68 us
  waiting for transfers between devices: 1.78 us -> 4.86 us
  blocking collectives: 19.2 us -> 16.4 us
  other arithmetic: 1.09 us -> 0.05 us
    pallas_call x1 -> x2, Pallas kernels: 29 us -> 13.9 us  [the longest x1 11.6 us: per_device(): pl.pallas_call(inner_kernel, in_specs=[VMEM] * 4, out_specs=[VMEM] * 2, o...]
    pallas_call x1, Pallas kernels: 12.1 us -> 7.55 us  [per_device(): pl.pallas_call(outer_kernel, in_specs=[SMEM] * 2 + [VMEM] * 14, out_specs...]
    slice x3 -> x0, local copies, waits for them, and re-layouts: 3.96 us -> none  [the longest x2 2.99 us: live_only(): x[:3]]
    ppermute x4, waiting for transfers between devices: 1.78 us -> 4.86 us  [shift(): return lax.ppermute(x, axis, [(i, (i + by) % n) for i in range(n)])]
    all_to_all x1, blocking collectives: 19.2 us -> 16.4 us  [per_device(): got = lax.all_to_all(send, AXES, 0, 0, tiled=True)]
    pallas_call x1, Pallas kernels: 3.6 us -> 2.22 us  [per_device(): pl.pallas_call(film_kernel, in_specs=[VMEM], out_specs=VMEM, out_shape=ja...]
    unnamed x13 -> x15, local copies, waits for them, and re-layouts: 6.67 us -> 6.67 us
  transfers between devices with their start and end apart: 4 -> 4, of which waited for: 1 -> 2; matrix products, arithmetic and copies ran while one was open for 4% -> 0% of each run, Pallas kernels for 33% -> 19%
where the time goes in v4:
time: 61.4 us; the launch traced here: 61 us
  Pallas kernels  23.7 us (39%)
  blocking collectives  16.4 us (27%)
  starting transfers between devices  9.22 us (15%)
  local copies, waits for them, and re-layouts  6.68 us (11%)
  waiting for transfers between devices  4.86 us (8%)
    all_to_all x1, blocking collectives, per_device(): got = lax.all_to_all(send, AXES, 0, 0, tiled=True)  16.4 us
    pallas_call x1, Pallas kernels, per_device(): pl.pallas_call(inner_kernel, in_specs=[VMEM] * 4, out_specs=[VMEM] * 2, o...  11.6 us
    ppermute x4, starting transfers between devices, shift(): return lax.ppermute(x, axis, [(i, (i + by) % n) for i in range(n)])  9.22 us
    pallas_call x1, Pallas kernels, per_device(): pl.pallas_call(outer_kernel, in_specs=[SMEM] * 2 + [VMEM] * 14, out_specs...  7.55 us
    unnamed x15, local copies, waits for them, and re-layouts  6.67 us
    ppermute x4, waiting for transfers between devices, shift(): return lax.ppermute(x, axis, [(i, (i + by) % n) for i in range(n)])  4.86 us
    pallas_call x1, Pallas kernels, per_device(): pl.pallas_call(prep_kernel, in_specs=[VMEM] * 6, out_specs=[VMEM] * 11, o...  2.35 us
    pallas_call x1, Pallas kernels, per_device(): pl.pallas_call(film_kernel, in_specs=[VMEM], out_specs=VMEM, out_shape=ja...  2.22 us
  transfers between devices with their start and end apart: 4, of which 2 were waited for; matrix products, arithmetic and copies ran while one was open for 0% of the time, Pallas kernels for 19%

profile of v4, /device:TPU:1, one launch (start us, length us, event | category | flops | bytes accessed | tf_op | source)
XLA Modules:
  0.0 61.0 jit_solution(16194393913738962198)
XLA Ops:
  0.0 0.8 %copy.8.counts = s32[64,32]{1,0:T(8,128)S(1)} copy(s32[64,32]{0,1:T(8,128)} %param.8) | data formatting | bytes 16384 | tf_op args[1]
  0.8 0.0 copy-start
  0.8 2.8 %copy-done = f32[6,64,32,128]{3,2,1,0:T(8,128)S(1)} copy-done((f32[6,64,32,128]{3,2,1,0:T(8,128)S(1)}, f32[6,64,32,128]{3,2,1,0:T(8,128)}, u32[]{:S(2)}) %copy-start) | copy-done | bytes 6291480
  3.6 0.0 copy-start.2
  3.6 0.8 %copy-done.2 = s32[4,4096]{1,0:T(4,128)S(1)} copy-done((s32[4,4096]{1,0:T(4,128)S(1)}, s32[4,4096]{1,0:T(4,128)}, u32[]{:S(2)}) %copy-start.2) | copy-done | bytes 65560
  4.4 0.0 copy-start.3
  4.4 0.8 %copy-done.3 = f32[3,4096]{1,0:T(4,128)S(1)} copy-done((f32[3,4096]{1,0:T(4,128)S(1)}, f32[3,4096]{1,0:T(4,128)}, u32[]{:S(2)}) %copy-start.3) | copy-done | bytes 49176
  5.3 0.0 copy-start.5
  5.3 0.7 %copy-done.5 = s32[4096]{0:T(1024)S(1)} copy-done((s32[4096]{0:T(1024)S(1)}, s32[4096]{0:T(1024)}, u32[]{:S(2)}) %copy-start.5) | copy-done | bytes 16408
  6.0 0.0 copy-start.6
  6.0 0.7 %copy-done.6 = s32[1024]{0:T(1024)S(1)} copy-done((s32[1024]{0:T(1024)S(1)}, s32[1024]{0:T(1024)}, u32[]{:S(2)}) %copy-start.6) | copy-done | bytes 4120
  6.7 0.0 copy-start.1
  6.7 0.0 copy-start.4
  6.7 2.4 %prep.1 = (f32[6,32,128]{2,1,0:T(8,128)S(1)}, f32[6,32,128]{2,1,0:T(8,128)S(1)}, f32[6,64,128]{2,1,0:T(8,128)S(1)}, f32[6,64,128]{2,1,0:T(8,128)S(1)}, s32[32,12...) custom-call(f32[6,64,32,128]{3,2,1,0:T(8,128)S(1)} %copy-done, ...), custom_call_target="tpu_custom_call" | custom-call | flops 20000000 | bytes 300000 | tf_op jit(solution)/shard_map/prep/pallas_call | solution.py:333
  9.0 3.1 %collective-permute-start = (f32[6,32,128]{2,1,0:T(8,128)S(1)}, f32[6,32,128]{2,1,0:T(8,128)S(1)}, u32[]{:S(2)}, u32[]{:S(2)}) collective-permute-start(f32[6,32,128]{2,1,0:T(8,128)S(1)} %get-tuple-element.27.c63), channel_id=1, source_target_pairs={{0,8},{8,16},{16,24},{24,32},{32,40},{40,48},{48,56},{56,64},{64,7... | collective-permute-start | bytes 294920 | tf_op jit(solution)/shard_map/ppermute | solution.py:326
  12.1 0.0 collective-permute-start.1
  12.1 1.6 %collective-permute-done.xm = f32[6,32,128]{2,1,0:T(8,128)S(1)} collective-permute-done((f32[6,32,128]{2,1,0:T(8,128)S(1)}, f32[6,32,128]{2,1,0:T(8,128)S(1)}, u32[]{:S(2)}, u32[]{:S(2)}) %collective-permute-start) | collective-permute-done | bytes 98336 | tf_op jit(solution)/shard_map/ppermute | solution.py:326
  13.8 3.2 %collective-permute-done.1.xp = f32[6,32,128]{2,1,0:T(8,128)S(1)} collective-permute-done((f32[6,32,128]{2,1,0:T(8,128)S(1)}, f32[6,32,128]{2,1,0:T(8,128)S(1)}, u32[]{:S(2)}, u32[]{:S(2)}) %collective-permute-start.1) | collective-permute-done | bytes 98336 | tf_op jit(solution)/shard_map/ppermute | solution.py:326
  17.0 1.5 %collective-permute-start.2 = (f32[6,66,128]{2,1,0:T(8,128)S(1)}, f32[6,66,128]{2,1,0:T(8,128)S(1)}, u32[]{:S(2)}, u32[]{:S(2)}) collective-permute-start(f32[6,66,128]{2,1,0:T(8,128)S(1)} %pad_maximum_fusion.top), channel_id=1, source_target_pairs={{0,1},{1,2},{2,3},{3,4},{4,5},{5,6},{6,7},{7,0},{8,9},{9,10},{10,1... | collective-permute-start | bytes 608264 | tf_op jit(solution)/shard_map/ppermute | solution.py:326
  18.5 4.6 %collective-permute-start.3 = (f32[6,66,128]{2,1,0:T(8,128)S(1)}, f32[6,66,128]{2,1,0:T(8,128)S(1)}, u32[]{:S(2)}, u32[]{:S(2)}) collective-permute-start(f32[6,66,128]{2,1,0:T(8,128)S(1)} %pad_maximum_fusion.1.bottom), channel_id=1, source_target_pairs={{0,7},{1,0},{2,1},{3,2},{4,3},{5,4},{6,5},{7,6},{8,15},{9,8},{10,9... | collective-permute-start | bytes 608264 | tf_op jit(solution)/shard_map/ppermute | solution.py:326
  23.2 0.0 copy-done.1
  23.2 11.6 %inner.1 = (f32[3,4104,128]{2,1,0:T(8,128)S(1)}, f32[3,512,8,128]{3,2,1,0:T(8,128)S(1)}) custom-call(f32[6,64,32,128]{3,2,1,0:T(8,128)S(1)} %copy-done.1, s32[64,32]{1,0:T(8,128)S(1)} %copy.8.counts, s32[32,128]{1,0:T(8,128)S(1)} %get-tuple-element.20.flat, f32[3,32,128]{2,1,0:T(8,128)S(1)} %get-tuple-element.21.rel), custom_call_target="tpu_custom_call" | custom-call | flops 60000000 | bytes 7000000 | tf_op jit(solution)/shard_map/inner/pallas_call | solution.py:354
  34.8 0.0 collective-permute-done.2.ym
  34.8 0.0 collective-permute-done.3.yp
  34.8 0.0 copy-done.4
  34.8 7.6 %outer.1 = f32[128,1,384]{2,1,0:T(1,128)S(1)} custom-call(s32[40,128]{1,0:T(8,128)S(1)} %get-tuple-element.18.points, s32[40,128]{1,0:T(8,128)S(1)} %get-tuple-element.19.places, f32[3,4104,128]{2,1,0:T(8,128)S(1)} %get-tuple-element.22.sums, f32[3,512,8,128]{3,2,1,0:T(8,128)S(1)} %get-tuple-element.23.near, f32[3,4096]{1,0:T(4,128)S(1)} %copy-done.4, ...), custom_call_target="tpu_custom_call" | custom-call | tf_op jit(solution)/shard_map/outer/pallas_call | solution.py:374
  42.4 16.4 %all_to_all.5.got = f32[128,1,384]{2,1,0:T(1,128)S(1)} all-to-all(f32[128,1,384]{2,1,0:T(1,128)S(1)} %outer.1), channel_id=1, replica_groups=mesh['bx'=16,'by'=8] {'bx','by'}, dimensions={0} | all-to-all | bytes 393216 | tf_op jit(solution)/shard_map/all_to_all | solution.py:388
  58.8 2.2 %film.1 = f32[3,8,256]{2,1,0:T(8,128)} custom-call(f32[128,1,384]{2,1,0:T(1,128)S(1)} %all_to_all.5.got), custom_call_target="tpu_custom_call" | custom-call | tf_op jit(solution)/shard_map/film/pallas_call | solution.py:389
  (4 shorter events, 0.1 us)
Async XLA Ops:
  0.8 2.8 %copy-start = (f32[6,64,32,128]{3,2,1,0:T(8,128)S(1)}, f32[6,64,32,128]{3,2,1,0:T(8,128)}, u32[]{:S(2)}) copy-start(f32[6,64,32,128]{3,2,1,0:T(8,128)} %ph.3) | copy-start | bytes 18874372
  3.6 0.8 %copy-start.2 = (s32[4,4096]{1,0:T(4,128)S(1)}, s32[4,4096]{1,0:T(4,128)}, u32[]{:S(2)}) copy-start(s32[4,4096]{1,0:T(4,128)} %blocks.1) | copy-start | bytes 196612
  4.4 0.8 %copy-start.3 = (f32[3,4096]{1,0:T(4,128)S(1)}, f32[3,4096]{1,0:T(4,128)}, u32[]{:S(2)}) copy-start(f32[3,4096]{1,0:T(4,128)} %offs.1) | copy-start | bytes 147460
  5.3 0.7 %copy-start.5 = (s32[4096]{0:T(1024)S(1)}, s32[4096]{0:T(1024)}, u32[]{:S(2)}) copy-start(s32[4096]{0:T(1024)} %param.12) | copy-start | bytes 49156
  6.0 0.7 %copy-start.6 = (s32[1024]{0:T(1024)S(1)}, s32[1024]{0:T(1024)}, u32[]{:S(2)}) copy-start(s32[1024]{0:T(1024)} %param.13) | copy-start | bytes 12292
  6.7 16.5 %copy-start.1 = (f32[6,64,32,128]{3,2,1,0:T(8,128)S(1)}, f32[6,64,32,128]{3,2,1,0:T(8,128)}, u32[]{:S(2)}) copy-start(f32[6,64,32,128]{3,2,1,0:T(8,128)} %ph.3) | copy-start | bytes 18874372
  6.7 28.1 %copy-start.4 = (f32[3,4096]{1,0:T(4,128)S(1)}, f32[3,4096]{1,0:T(4,128)}, u32[]{:S(2)}) copy-start(f32[3,4096]{1,0:T(4,128)} %alb.1) | copy-start | bytes 147460
  9.0 4.7 %collective-permute-start = (f32[6,32,128]{2,1,0:T(8,128)S(1)}, f32[6,32,128]{2,1,0:T(8,128)S(1)}, u32[]{:S(2)}, u32[]{:S(2)}) collective-permute-start(f32[6,32,128]{2,1,0:T(8,128)S(1)} %get-tuple-element.27.c63), channel_id=1, source_target_pairs={{0,8},{8,16},{16,24},{24,32},{32,40},{40,48},{48,56},{56,64},{64,7... | collective-permute-start | bytes 294920 | tf_op jit(solution)/shard_map/ppermute | solution.py:326
  12.1 4.9 %collective-permute-start.1 = (f32[6,32,128]{2,1,0:T(8,128)S(1)}, f32[6,32,128]{2,1,0:T(8,128)S(1)}, u32[]{:S(2)}, u32[]{:S(2)}) collective-permute-start(f32[6,32,128]{2,1,0:T(8,128)S(1)} %get-tuple-element.28.c0), channel_id=1, source_target_pairs={{0,120},{8,0},{16,8},{24,16},{32,24},{40,32},{48,40},{56,48},{64,5... | collective-permute-start | bytes 294920 | tf_op jit(solution)/shard_map/ppermute | solution.py:326
  17.0 17.8 %collective-permute-start.2 = (f32[6,66,128]{2,1,0:T(8,128)S(1)}, f32[6,66,128]{2,1,0:T(8,128)S(1)}, u32[]{:S(2)}, u32[]{:S(2)}) collective-permute-start(f32[6,66,128]{2,1,0:T(8,128)S(1)} %pad_maximum_fusion.top), channel_id=1, source_target_pairs={{0,1},{1,2},{2,3},{3,4},{4,5},{5,6},{6,7},{7,0},{8,9},{9,10},{10,1... | collective-permute-start | bytes 608264 | tf_op jit(solution)/shard_map/ppermute | solution.py:326
  18.5 16.3 %collective-permute-start.3 = (f32[6,66,128]{2,1,0:T(8,128)S(1)}, f32[6,66,128]{2,1,0:T(8,128)S(1)}, u32[]{:S(2)}, u32[]{:S(2)}) collective-permute-start(f32[6,66,128]{2,1,0:T(8,128)S(1)} %pad_maximum_fusion.1.bottom), channel_id=1, source_target_pairs={{0,7},{1,0},{2,1},{3,2},{4,3},{5,4},{6,5},{7,6},{8,15},{9,8},{10,9... | collective-permute-start | bytes 608264 | tf_op jit(solution)/shard_map/ppermute | solution.py:326

commit v5 on v4

--- a/solution.py
+++ b/solution.py
@@ -22,6 +22,7 @@
 EDGE = 2 * EDGE_X + 2 * EDGE_Y
 LIST = ROWS + 8
 STEP = 9
+TOGETHER = 4
 GROUPS = 4
 i32, f32, bf16 = jnp.int32, jnp.float32, jnp.bfloat16
 VMEM = pl.BlockSpec(memory_space=pltpu.VMEM)
@@ -63,21 +64,29 @@
     return total
 
 
-def prep_kernel(ph, counts, blocks, offs, pix, tile_slot,
-                c63, c0, top, bottom, flat, rel, owner, rank, target, points, places, square, sb, so, where):
-    square[:CX, :CY] = counts[...].astype(f32)
-    by_x = square[:CX, :].astype(i32)
-    by_y = jnp.transpose(square[...])[:CY, :].astype(i32)
-    for out, x in ((c63, CX - 1), (c0, 0)):
+def edge_kernel(ph, counts, c63, c0, top, bottom, square, raw_x, raw_y, sem):
+    reads = [pltpu.make_async_copy(ph.at[:, x], raw_x.at[k], sem.at[k]) for k, x in enumerate((CX - 1, 0))]
+    reads += [pltpu.make_async_copy(ph.at[:, :, y, :], raw_y.at[k], sem.at[2 + k]) for k, y in enumerate((CY - 1, 0))]
+    for read in reads:
+        read.start()
+    square[:CY, :CX] = counts[...].astype(f32)
+    by_y = square[:CY, :].astype(i32)
+    by_x = jnp.transpose(square[...])[:CX, :].astype(i32)
+    for read in reads:
+        read.wait()
+    for k, (out, x) in enumerate(((c63, CX - 1), (c0, 0))):
         live = iota((CY, LANES), 1) < lane_take(by_y, jnp.full((CY, LANES), x, i32))
         for c in range(6):
-            v = ph[c, x]
+            v = raw_x[k, c]
             out[c] = v if c < 3 else jnp.where(live, v, 0.0)
-    for out, y in ((top, CY - 1), (bottom, 0)):
+    for k, (out, y) in enumerate(((top, CY - 1), (bottom, 0))):
         live = iota((CX, LANES), 1) < lane_take(by_x, jnp.full((CX, LANES), y, i32))
         for c in range(6):
-            v = ph[c, :, y, :]
+            v = raw_y[k, c]
             out[c] = v if c < 3 else jnp.where(live, v, 0.0)
+
+
+def prep_kernel(blocks, offs, pix, tile_slot, flat, rel, owner, rank, target, points, places, sb, so, where):
     for k in range(4):
         for r in range(ROWS):
             sb[k, r : r + 1, :] = blocks[k : k + 1, r * LANES : (r + 1) * LANES]
@@ -119,7 +128,7 @@
         ).astype(i32)
         return seen + tally[:, LANES:]
 
-    lax.fori_loop(0, ROWS, ranks, jnp.zeros((OWNERS, LANES), f32), unroll=16)
+    lax.fori_loop(0, ROWS, ranks, jnp.zeros((OWNERS, LANES), f32), unroll=32)
     outside = at < 0
     tally = jnp.dot(jnp.where(outside, 1.0, 0.0).astype(bf16), upper, preferred_element_type=f32)
     before = iota((ROWS, ROWS), 1) < iota((ROWS, ROWS), 0)
@@ -144,18 +153,30 @@
         rows = jnp.concatenate([jnp.where(hit, x.astype(f32), 0.0) for x in parts], axis=0).astype(bf16)
         return total + lax.dot_general(rows, low_hit, NT, preferred_element_type=f32)
 
-    found = lax.fori_loop(0, ROWS // 2, collect, jnp.zeros((4 * ROWS, LANES), f32), unroll=8).astype(i32)
+    found = lax.fori_loop(0, ROWS // 2, collect, jnp.zeros((4 * ROWS, LANES), f32), unroll=16).astype(i32)
     points[:ROWS] = found[:ROWS] * 256 + found[ROWS : 2 * ROWS]
     places[:ROWS] = found[2 * ROWS : 3 * ROWS] * 256 + found[3 * ROWS :]
     points[ROWS:] = jnp.broadcast_to(count, (8, LANES))
     places[ROWS:] = jnp.broadcast_to(count, (8, LANES))
 
-def inner_kernel(ph, counts, flat, rel, sums, near, table, square, stage_a, stage_b, ssem, *start):
+def inner_kernel(photons, counts, flat, rel, sums, near, ph, table, square, stage_a, stage_b, psem, ssem, *start):
+    read = pltpu.make_async_copy(photons, ph, psem)
+    read.start()
     to_scalar = [pltpu.make_async_copy(flat.at[pl.ds(4 * s, 4)], start[s], ssem.at[s]) for s in range(8)]
     for copy in to_scalar:
         copy.start()
-    square[:CX, :CY] = counts[...].astype(f32)
-    filled = jnp.transpose(square[...])[:CY, :].astype(i32)
+    parts = [[rel[c, pl.ds(v, 8, stride=4), :] for c in range(3)] for v in range(4)]
+
+    def spread(lane, _):
+        take = jnp.full((8, LANES), lane, i32)
+        for v in range(4):
+            for c in range(3):
+                near[c, v * LANES + lane] = lane_take(parts[v][c], take)
+        return 0
+
+    lax.fori_loop(0, LANES, spread, 0, unroll=16)
+    square[:CY, :CX] = counts[...].astype(f32)
+    filled = square[:CY, :].astype(i32)
     lane = iota((CY, LANES), 1)
 
     def row(c, x, y, right):
@@ -170,21 +191,11 @@
             table[pl.ds(row(c, x, 1, 1), CY, stride=4), :] = v
         return 0
 
+    read.wait()
     lax.fori_loop(0, CX, column, 0, unroll=8)
     for copy in to_scalar:
         copy.wait()
     zero = lax.axis_index("bx") * 0
-
-    parts = [[rel[c, pl.ds(v, 8, stride=4), :] for c in range(3)] for v in range(4)]
-
-    def spread(lane, _):
-        take = jnp.full((8, LANES), lane, i32)
-        for v in range(4):
-            for c in range(3):
-                near[c, v * LANES + lane] = lane_take(parts[v][c], take)
-        return 0
-
-    lax.fori_loop(0, LANES, spread, 0, unroll=8)
 
     def fetch(i, stage):
         for u in range(GROUPS):
@@ -232,7 +243,7 @@
     zero = lax.axis_index("bx") * 0
     count = points[ROWS, 0]
 
-    def eight(i, _):
+    def eight(i, stage, close):
         where = []
         for s in range(8):
             k = jnp.minimum(8 * i + s, count - 1)
@@ -246,9 +257,13 @@
         for c in range(3):
             for s in range(8):
                 sums[c, pl.ds(where[s], 1), :] = total[c][s : s + 1]
+
+    def eights(i, _):
+        for u in range(TOGETHER):
+            eight(TOGETHER * i + u, stage.at[u], close.at[u])
         return 0
 
-    lax.fori_loop(0, (count + 7) >> 3, eight, 0)
+    lax.fori_loop(0, lax.div(count + 8 * TOGETHER - 1, 8 * TOGETHER), eights, 0)
     ones = jnp.ones((8, 2 * LANES), f32).astype(bf16)
 
     def lane_sums(r, _):
@@ -263,7 +278,7 @@
                 rad[c, pl.ds(line, 1), :] = y[:1]
         return 0
 
-    lax.fori_loop(0, ROWS // 2, lane_sums, 0, unroll=8)
+    lax.fori_loop(0, ROWS // 2, lane_sums, 0, unroll=16)
     for c in range(3):
         for r in range(ROWS):
             rad[c, r : r + 1, :] = rad[c, r : r + 1, :] * alb[c : c + 1, r * LANES : (r + 1) * LANES]
@@ -287,7 +302,7 @@
             total = total + lax.dot_general(mine, rows, NT, preferred_element_type=f32)
         return total
 
-    send[:, 0, :] = lax.fori_loop(0, ROWS // 2, scatter, jnp.zeros((OWNERS, 4 * CAP), f32), unroll=8)
+    send[:, 0, :] = lax.fori_loop(0, ROWS // 2, scatter, jnp.zeros((OWNERS, 4 * CAP), f32), unroll=16)
 
 
 def film_kernel(got, film, flipped, total):
@@ -314,7 +329,7 @@
         rows = jnp.concatenate(high + low, axis=0).astype(bf16)
         return acc + lax.dot_general(rows, low_hit, NT, preferred_element_type=f32)
 
-    acc = lax.fori_loop(0, CAP // 2, step, jnp.zeros((96, LANES), f32), unroll=16)
+    acc = lax.fori_loop(0, CAP // 2, step, jnp.zeros((96, LANES), f32), unroll=48)
     total[...] = acc[:48] + acc[48:]
     for c in range(3):
         film[c, :, :LANES] = total[pl.ds(16 * c, 8, stride=2), :]
@@ -330,47 +345,62 @@
     small_i = jax.ShapeDtypeStruct((ROWS, LANES), i32)
     listed = jax.ShapeDtypeStruct((LIST, LANES), i32)
     column, line = jax.ShapeDtypeStruct((6, CY, LANES), f32), jax.ShapeDtypeStruct((6, CX, LANES), f32)
-    c63, c0, top, bottom, flat, rel, owner, rank, target, points, places = pl.pallas_call(
-        prep_kernel,
-        in_specs=[VMEM] * 6,
-        out_specs=[VMEM] * 11,
-        out_shape=[column, column, line, line]
-        + [small_i, jax.ShapeDtypeStruct((3, ROWS, LANES), f32), small_i, small_i, small_i, listed, listed],
+    counts = block_counts.T
+    c63, c0, top, bottom = pl.pallas_call(
+        edge_kernel,
+        in_specs=[HBM, VMEM],
+        out_specs=[VMEM] * 4,
+        out_shape=[column, column, line, line],
         scratch_shapes=[
             pltpu.VMEM((LANES, LANES), f32),
+            pltpu.VMEM((2, 6, CY, LANES), f32),
+            pltpu.VMEM((2, 6, CX, LANES), f32),
+            pltpu.SemaphoreType.DMA((4,)),
+        ],
+        compiler_params=params(60),
+        name="edges",
+    )(photon_data, counts)
+    xm, xp = shift(c63, "bx", 1), shift(c0, "bx", -1)
+    flat, rel, owner, rank, target, points, places = pl.pallas_call(
+        prep_kernel,
+        in_specs=[VMEM] * 4,
+        out_specs=[VMEM] * 7,
+        out_shape=[small_i, jax.ShapeDtypeStruct((3, ROWS, LANES), f32), small_i, small_i, small_i, listed, listed],
+        scratch_shapes=[
             pltpu.VMEM((4, ROWS, LANES), i32),
             pltpu.VMEM((3, ROWS, LANES), f32),
             pltpu.VMEM((3, ROWS, LANES), i32),
         ],
         compiler_params=params(16),
-        cost_estimate=pl.CostEstimate(flops=20_000_000, bytes_accessed=300_000, transcendentals=0),
+        cost_estimate=pl.CostEstimate(flops=4000000000, bytes_accessed=40000000, transcendentals=0),
         name="prep",
-    )(photon_data, block_counts, gather_blocks, gather_offsets,
-      gather_pixels.reshape(ROWS, LANES), tile_slot.reshape(8, LANES))
-    xm, xp = shift(c63, "bx", 1), shift(c0, "bx", -1)
+    )(gather_blocks, gather_offsets, gather_pixels.reshape(ROWS, LANES), tile_slot.reshape(8, LANES))
+    top, bottom, rank = lax.optimization_barrier((top, bottom, rank))
     top = jnp.concatenate([xm[:, -1:], top, xp[:, -1:]], axis=1)
     bottom = jnp.concatenate([xm[:, :1], bottom, xp[:, :1]], axis=1)
     ym, yp = shift(top, "by", 1), shift(bottom, "by", -1)
     sums, near = pl.pallas_call(
         inner_kernel,
-        in_specs=[VMEM] * 4,
+        in_specs=[HBM] + [VMEM] * 3,
         out_specs=[VMEM] * 2,
         out_shape=[
             jax.ShapeDtypeStruct((3, 8 * APART, LANES), f32),
             jax.ShapeDtypeStruct((3, POINTS // 8, 8, LANES), f32),
         ],
         scratch_shapes=[
+            pltpu.VMEM((6, CX, CY, LANES), f32),
             pltpu.VMEM((TABLE_ROWS, LANES), f32),
-            pltpu.VMEM((LANES, LANES), f32),
+            pltpu.VMEM((CY, LANES), f32),
             pltpu.VMEM((GROUPS, 3, 8 * STEP + 8, LANES), f32),
             pltpu.VMEM((GROUPS, 3, 8 * STEP + 8, LANES), f32),
+            pltpu.SemaphoreType.DMA,
             pltpu.SemaphoreType.DMA((8,)),
         ]
         + [pltpu.SMEM((4, LANES), i32)] * 8,
         compiler_params=params(34),
         cost_estimate=pl.CostEstimate(flops=60_000_000, bytes_accessed=7_000_000, transcendentals=0),
         name="inner",
-    )(photon_data, block_counts, flat, rel)
+    )(photon_data, counts, flat, rel)
     send = pl.pallas_call(
         outer_kernel,
         in_specs=[SMEM] * 2 + [VMEM] * 14,
@@ -378,8 +408,8 @@
         out_shape=jax.ShapeDtypeStruct((OWNERS, 1, 4 * CAP), f32),
         scratch_shapes=[
             pltpu.VMEM((3 * EDGE + 64, LANES), f32),
-            pltpu.VMEM((3, 8 * STEP + 8, LANES), f32),
-            pltpu.VMEM((3, 8, LANES), f32),
+            pltpu.VMEM((TOGETHER, 3, 8 * STEP + 8, LANES), f32),
+            pltpu.VMEM((TOGETHER, 3, 8, LANES), f32),
             pltpu.VMEM((3, ROWS, LANES), f32),
         ],
         compiler_params=params(16),

time: 61.4 us -> 53.8 us (0.88)
  local copies, waits for them, and re-layouts: 6.68 us -> 0.07 us
  waiting for transfers between devices: 4.86 us -> 3.02 us
  Pallas kernels: 23.7 us -> 24.8 us
    unnamed x15 -> x24, local copies, waits for them, and re-layouts: 6.67 us -> 0.06 us
    pallas_call x2 -> x3, Pallas kernels: 13.9 us -> 16.3 us  [the longest x1 11.4 us: per_device(): pl.pallas_call(inner_kernel, in_specs=[HBM] + [VMEM] * 3, out_specs=[VMEM...]
    ppermute x4, waiting for transfers between devices: 4.86 us -> 3.02 us  [shift(): return lax.ppermute(x, axis, [(i, (i + by) % n) for i in range(n)])]
    pallas_call x1, Pallas kernels: 7.55 us -> 6.63 us  [per_device(): pl.pallas_call(outer_kernel, in_specs=[SMEM] * 2 + [VMEM] * 14, out_specs...]
  transfers between devices with their start and end apart: 4 -> 4, of which waited for: 2 -> 1; matrix products, arithmetic and copies ran while one was open for 0% -> 0% of each run, Pallas kernels for 19% -> 25%
where the time goes in v5:
time: 53.8 us; the launch traced here: 53.6 us
  Pallas kernels  24.8 us (46%)
  blocking collectives  16.3 us (30%)
  starting transfers between devices  9.23 us (17%)
  waiting for transfers between devices  3.02 us (6%)
    all_to_all x1, blocking collectives, per_device(): got = lax.all_to_all(send, AXES, 0, 0, tiled=True)  16.3 us
    pallas_call x1, Pallas kernels, per_device(): pl.pallas_call(inner_kernel, in_specs=[HBM] + [VMEM] * 3, out_specs=[VMEM...  11.4 us
    ppermute x4, starting transfers between devices, shift(): return lax.ppermute(x, axis, [(i, (i + by) % n) for i in range(n)])  9.23 us
    pallas_call x1, Pallas kernels, per_device(): pl.pallas_call(outer_kernel, in_specs=[SMEM] * 2 + [VMEM] * 14, out_specs...  6.63 us
    ppermute x4, waiting for transfers between devices, shift(): return lax.ppermute(x, axis, [(i, (i + by) % n) for i in range(n)])  3.02 us
    pallas_call x1, Pallas kernels, per_device(): pl.pallas_call(edge_kernel, in_specs=[HBM, VMEM], out_specs=[VMEM] * 4, o...  2.93 us
    pallas_call x1, Pallas kernels, per_device(): pl.pallas_call(prep_kernel, in_specs=[VMEM] * 4, out_specs=[VMEM] * 7, ou...  1.92 us
    pallas_call x1, Pallas kernels, per_device(): pl.pallas_call(film_kernel, in_specs=[VMEM], out_specs=VMEM, out_shape=ja...  1.87 us
  transfers between devices with their start and end apart: 4, of which 1 were waited for; matrix products, arithmetic and copies ran while one was open for 0% of the time, Pallas kernels for 25%

profile of v5, /device:TPU:1, one launch (start us, length us, event | category | flops | bytes accessed | tf_op | source)
XLA Modules:
  0.0 53.6 jit_solution(8178275694585240545)
XLA Ops:
  0.0 0.0 copy-start.5
  0.0 0.0 slice-start
  0.0 2.9 %edges.1 = (f32[6,32,128]{2,1,0:T(8,128)}, f32[6,32,128]{2,1,0:T(8,128)}, f32[6,64,128]{2,1,0:T(8,128)}, f32[6,64,128]{2,1,0:T(8,128)}) custom-call(f32[6,64,32,128]{3,2,1,0:T(8,128)} %ph.1, s32[32,64]{1,0:T(8,128)} %bitcast.5), custom_call_target="tpu_custom_call" | custom-call | tf_op jit(solution)/shard_map/edges/pallas_call | solution.py:349
  3.0 3.1 %collective-permute-start = (f32[6,32,128]{2,1,0:T(8,128)}, f32[6,32,128]{2,1,0:T(8,128)S(1)}, u32[]{:S(2)}, u32[]{:S(2)}) collective-permute-start(f32[6,32,128]{2,1,0:T(8,128)} %get-tuple-element.33.c63), channel_id=1, source_target_pairs={{0,8},{8,16},{16,24},{24,32},{32,40},{40,48},{48,56},{56,64},{64,7... | collective-permute-start | bytes 294920 | tf_op jit(solution)/shard_map/ppermute | solution.py:341
  6.1 0.0 collective-permute-start.1
  6.1 0.0 copy-done.7
  6.1 0.0 copy-done.6
  6.1 0.0 copy-done.4
  6.1 0.0 copy-done.5
  6.1 0.0 copy-start.9
  6.1 0.0 copy-start.8
  6.1 0.0 slice-start.1
  6.1 0.0 copy-start.3
  6.1 1.9 %prep.1 = (s32[32,128]{1,0:T(8,128)S(1)}, f32[3,32,128]{2,1,0:T(8,128)S(1)}, s32[32,128]{1,0:T(8,128)S(1)}, s32[32,128]{1,0:T(8,128)S(1)}, s32[32,128]{1,0:T(8,1...) custom-call(s32[4,4096]{1,0:T(4,128)S(1)} %copy-done.4, f32[3,4096]{1,0:T(4,128)S(1)} %copy-done.5, ...), custom_call_target="tpu_custom_call" | custom-call | flops 4000000000 | bytes 40000000 | tf_op jit(solution)/shard_map/prep/pallas_call | solution.py:364
  8.1 0.0 copy-start
  8.1 0.0 copy-start.1
  8.1 0.0 copy-start.2
  8.1 0.0 collective-permute-done.xm
  8.1 3.0 %collective-permute-done.1.xp = f32[6,32,128]{2,1,0:T(8,128)S(1)} collective-permute-done((f32[6,32,128]{2,1,0:T(8,128)}, f32[6,32,128]{2,1,0:T(8,128)S(1)}, u32[]{:S(2)}, u32[]{:S(2)}) %collective-permute-start.1) | collective-permute-done | bytes 98336 | tf_op jit(solution)/shard_map/ppermute | solution.py:341
  11.1 0.0 copy-done.9
  11.2 1.5 %collective-permute-start.2 = (f32[6,66,128]{2,1,0:T(8,128)S(1)}, f32[6,66,128]{2,1,0:T(8,128)S(1)}, u32[]{:S(2)}, u32[]{:S(2)}) collective-permute-start(f32[6,66,128]{2,1,0:T(8,128)S(1)} %pad_maximum_fusion.top), channel_id=1, source_target_pairs={{0,1},{1,2},{2,3},{3,4},{4,5},{5,6},{6,7},{7,0},{8,9},{9,10},{10,1... | collective-permute-start | bytes 608264 | tf_op jit(solution)/shard_map/ppermute | solution.py:341
  12.7 0.0 copy-done.8
  12.7 4.7 %collective-permute-start.3 = (f32[6,66,128]{2,1,0:T(8,128)S(1)}, f32[6,66,128]{2,1,0:T(8,128)S(1)}, u32[]{:S(2)}, u32[]{:S(2)}) collective-permute-start(f32[6,66,128]{2,1,0:T(8,128)S(1)} %pad_maximum_fusion.1.bottom), channel_id=1, source_target_pairs={{0,7},{1,0},{2,1},{3,2},{4,3},{5,4},{6,5},{7,6},{8,15},{9,8},{10,9... | collective-permute-start | bytes 608264 | tf_op jit(solution)/shard_map/ppermute | solution.py:341
  17.4 0.0 slice-done
  17.4 0.0 slice-done.1
  17.4 0.0 copy-done.3
  17.4 11.4 %inner.1 = (f32[3,4104,128]{2,1,0:T(8,128)S(1)}, f32[3,512,8,128]{3,2,1,0:T(8,128)S(1)}) custom-call(f32[6,64,32,128]{3,2,1,0:T(8,128)S(1)} %bitcast.4, s32[32,64]{1,0:T(8,128)S(1)} %bitcast.6, s32[32,128]{1,0:T(8,128)S(1)} %get-tuple-element.23.flat, f32[3,32,128]{2,1,0:T(8,128)S(1)} %get-tuple-element.24.rel), custom_call_target="tpu_custom_call" | custom-call | flops 60000000 | bytes 7000000 | tf_op jit(solution)/shard_map/inner/pallas_call | solution.py:382
  28.8 0.0 collective-permute-done.2.ym
  28.8 0.0 collective-permute-done.3.yp
  28.9 6.6 %outer.1 = f32[128,1,384]{2,1,0:T(1,128)S(1)} custom-call(s32[40,128]{1,0:T(8,128)S(1)} %get-tuple-element.21.points, s32[40,128]{1,0:T(8,128)S(1)} %get-tuple-element.22.places, f32[3,4104,128]{2,1,0:T(8,128)S(1)} %get-tuple-element.25.sums, f32[3,512,8,128]{3,2,1,0:T(8,128)S(1)} %get-tuple-element.26.near, f32[3,4096]{1,0:T(4,128)S(1)} %copy-done.2, ...), custom_call_target="tpu_custom_call" | custom-call | tf_op jit(solution)/shard_map/outer/pallas_call | solution.py:404
  35.5 16.3 %all_to_all.5.got = f32[128,1,384]{2,1,0:T(1,128)S(1)} all-to-all(f32[128,1,384]{2,1,0:T(1,128)S(1)} %outer.1), channel_id=1, replica_groups=mesh['bx'=16,'by'=8] {'bx','by'}, dimensions={0} | all-to-all | bytes 393216 | tf_op jit(solution)/shard_map/all_to_all | solution.py:418
  51.7 1.9 %film.1 = f32[3,8,256]{2,1,0:T(8,128)} custom-call(f32[128,1,384]{2,1,0:T(1,128)S(1)} %all_to_all.5.got), custom_call_target="tpu_custom_call" | custom-call | tf_op jit(solution)/shard_map/film/pallas_call | solution.py:419
  (11 shorter events, 0.1 us)
Async XLA Ops:
  0.0 6.1 %copy-start.7 = (s32[1024]{0:T(1024)S(1)}, s32[1024]{0:T(1024)}, u32[]{:S(2)}) copy-start(s32[1024]{0:T(1024)} %param.13) | copy-start | bytes 12292
  0.0 6.1 %copy-start.6 = (s32[4096]{0:T(1024)S(1)}, s32[4096]{0:T(1024)}, u32[]{:S(2)}) copy-start(s32[4096]{0:T(1024)} %param.12) | copy-start | bytes 49156
  0.0 6.1 %copy-start.4 = (s32[4,4096]{1,0:T(4,128)S(1)}, s32[4,4096]{1,0:T(4,128)}, u32[]{:S(2)}) copy-start(s32[4,4096]{1,0:T(4,128)} %blocks.1) | copy-start | bytes 196612
  0.0 6.1 %copy-start.5 = (f32[3,4096]{1,0:T(4,128)S(1)}, f32[3,4096]{1,0:T(4,128)}, u32[]{:S(2)}) copy-start(f32[3,4096]{1,0:T(4,128)} %offs.1) | copy-start | bytes 147460
  0.0 17.3 %slice-start = ((s8[6291456]{0:T(1024)(128)(4,1)}), s8[2097152]{0:T(1024)(128)(4,1)S(1)}, s32[]{:S(2)}) async-start(s8[6291456]{0:T(1024)(128)(4,1)} %bitcast.3), calls=%async_computation.1 | async-start | bytes 4194304
  3.0 5.1 %collective-permute-start = (f32[6,32,128]{2,1,0:T(8,128)}, f32[6,32,128]{2,1,0:T(8,128)S(1)}, u32[]{:S(2)}, u32[]{:S(2)}) collective-permute-start(f32[6,32,128]{2,1,0:T(8,128)} %get-tuple-element.33.c63), channel_id=1, source_target_pairs={{0,8},{8,16},{16,24},{24,32},{32,40},{40,48},{48,56},{56,64},{64,7... | collective-permute-start | bytes 294920 | tf_op jit(solution)/shard_map/ppermute | solution.py:341
  6.1 5.1 %collective-permute-start.1 = (f32[6,32,128]{2,1,0:T(8,128)}, f32[6,32,128]{2,1,0:T(8,128)S(1)}, u32[]{:S(2)}, u32[]{:S(2)}) collective-permute-start(f32[6,32,128]{2,1,0:T(8,128)} %get-tuple-element.34.c0), channel_id=1, source_target_pairs={{0,120},{8,0},{16,8},{24,16},{32,24},{40,32},{48,40},{56,48},{64,5... | collective-permute-start | bytes 294920 | tf_op jit(solution)/shard_map/ppermute | solution.py:341
  6.1 5.1 %copy-start.9 = (f32[6,64,128]{2,1,0:T(8,128)S(1)}, f32[6,64,128]{2,1,0:T(8,128)}, u32[]{:S(2)}) copy-start(f32[6,64,128]{2,1,0:T(8,128)} %get-tuple-element.35) | copy-start | bytes 589828
  6.1 6.6 %copy-start.8 = (f32[6,64,128]{2,1,0:T(8,128)S(1)}, f32[6,64,128]{2,1,0:T(8,128)}, u32[]{:S(2)}) copy-start(f32[6,64,128]{2,1,0:T(8,128)} %get-tuple-element.36) | copy-start | bytes 589828
  6.1 11.3 %slice-start.1 = ((s8[6291456]{0:T(1024)(128)(4,1)}), s8[4194304]{0:T(1024)(128)(4,1)S(1)}, s32[]{:S(2)}) async-start(s8[6291456]{0:T(1024)(128)(4,1)} %bitcast.3), calls=%async_computation.2 | async-start | bytes 8388608
  6.1 11.2 %copy-start.3 = (s32[64,32]{0,1:T(8,128)S(1)}, s32[64,32]{0,1:T(8,128)}, u32[]{:S(2)}) copy-start(s32[64,32]{0,1:T(8,128)} %param.8) | copy-start | bytes 24580
  8.1 20.8 %copy-start = (f32[6,32,128]{2,1,0:T(8,128)S(1)}, f32[6,32,128]{2,1,0:T(8,128)}, u32[]{:S(2)}) copy-start(f32[6,32,128]{2,1,0:T(8,128)} %get-tuple-element.33.c63) | copy-start | bytes 294916
  8.1 20.8 %copy-start.1 = (f32[6,32,128]{2,1,0:T(8,128)S(1)}, f32[6,32,128]{2,1,0:T(8,128)}, u32[]{:S(2)}) copy-start(f32[6,32,128]{2,1,0:T(8,128)} %get-tuple-element.34.c0) | copy-start | bytes 294916
  8.1 20.8 %copy-start.2 = (f32[3,4096]{1,0:T(4,128)S(1)}, f32[3,4096]{1,0:T(4,128)}, u32[]{:S(2)}) copy-start(f32[3,4096]{1,0:T(4,128)} %alb.1) | copy-start | bytes 147460
  11.2 17.6 %collective-permute-start.2 = (f32[6,66,128]{2,1,0:T(8,128)S(1)}, f32[6,66,128]{2,1,0:T(8,128)S(1)}, u32[]{:S(2)}, u32[]{:S(2)}) collective-permute-start(f32[6,66,128]{2,1,0:T(8,128)S(1)} %pad_maximum_fusion.top), channel_id=1, source_target_pairs={{0,1},{1,2},{2,3},{3,4},{4,5},{5,6},{6,7},{7,0},{8,9},{9,10},{10,1... | collective-permute-start | bytes 608264 | tf_op jit(solution)/shard_map/ppermute | solution.py:341
  12.7 16.1 %collective-permute-start.3 = (f32[6,66,128]{2,1,0:T(8,128)S(1)}, f32[6,66,128]{2,1,0:T(8,128)S(1)}, u32[]{:S(2)}, u32[]{:S(2)}) collective-permute-start(f32[6,66,128]{2,1,0:T(8,128)S(1)} %pad_maximum_fusion.1.bottom), channel_id=1, source_target_pairs={{0,7},{1,0},{2,1},{3,2},{4,3},{5,4},{6,5},{7,6},{8,15},{9,8},{10,9... | collective-permute-start | bytes 608264 | tf_op jit(solution)/shard_map/ppermute | solution.py:341

commit v6 on v5

--- a/solution.py
+++ b/solution.py
@@ -22,7 +22,7 @@
 EDGE = 2 * EDGE_X + 2 * EDGE_Y
 LIST = ROWS + 8
 STEP = 9
-TOGETHER = 4
+TOGETHER = 8
 GROUPS = 4
 i32, f32, bf16 = jnp.int32, jnp.float32, jnp.bfloat16
 VMEM = pl.BlockSpec(memory_space=pltpu.VMEM)
@@ -174,7 +174,7 @@
                 near[c, v * LANES + lane] = lane_take(parts[v][c], take)
         return 0
 
-    lax.fori_loop(0, LANES, spread, 0, unroll=16)
+    lax.fori_loop(0, LANES, spread, 0, unroll=32)
     square[:CY, :CX] = counts[...].astype(f32)
     filled = square[:CY, :].astype(i32)
     lane = iota((CY, LANES), 1)
@@ -192,7 +192,7 @@
         return 0
 
     read.wait()
-    lax.fori_loop(0, CX, column, 0, unroll=8)
+    lax.fori_loop(0, CX, column, 0, unroll=16)
     for copy in to_scalar:
         copy.wait()
     zero = lax.axis_index("bx") * 0

time: 53.8 us -> 54 us (level)
  no operation moved by 1% of the time
where the time goes in v6:
time: 54 us; the launch traced here: 53.8 us
  Pallas kernels  24.9 us (46%)
  blocking collectives  16.3 us (30%)
  starting transfers between devices  9.23 us (17%)
  waiting for transfers between devices  3.02 us (6%)
    all_to_all x1, blocking collectives, per_device(): got = lax.all_to_all(send, AXES, 0, 0, tiled=True)  16.3 us
    pallas_call x1, Pallas kernels, per_device(): pl.pallas_call(inner_kernel, in_specs=[HBM] + [VMEM] * 3, out_specs=[VMEM...  11.3 us
    ppermute x4, starting transfers between devices, shift(): return lax.ppermute(x, axis, [(i, (i + by) % n) for i in range(n)])  9.23 us
    pallas_call x1, Pallas kernels, per_device(): pl.pallas_call(outer_kernel, in_specs=[SMEM] * 2 + [VMEM] * 14, out_specs...  6.95 us
    ppermute x4, waiting for transfers between devices, shift(): return lax.ppermute(x, axis, [(i, (i + by) % n) for i in range(n)])  3.02 us
    pallas_call x1, Pallas kernels, per_device(): pl.pallas_call(edge_kernel, in_specs=[HBM, VMEM], out_specs=[VMEM] * 4, o...  2.93 us
    pallas_call x1, Pallas kernels, per_device(): pl.pallas_call(prep_kernel, in_specs=[VMEM] * 4, out_specs=[VMEM] * 7, ou...  1.92 us
    pallas_call x1, Pallas kernels, per_device(): pl.pallas_call(film_kernel, in_specs=[VMEM], out_specs=VMEM, out_shape=ja...  1.87 us
  transfers between devices with their start and end apart: 4, of which 1 were waited for; matrix products, arithmetic and copies ran while one was open for 0% of the time, Pallas kernels for 25%

profile of v6, /device:TPU:1, one launch (start us, length us, event | category | flops | bytes accessed | tf_op | source)
XLA Modules:
  0.0 53.8 jit_solution(9529240466694078961)
XLA Ops:
  0.0 0.0 copy-start.5
  0.0 0.0 slice-start
  0.0 2.9 %edges.1 = (f32[6,32,128]{2,1,0:T(8,128)}, f32[6,32,128]{2,1,0:T(8,128)}, f32[6,64,128]{2,1,0:T(8,128)}, f32[6,64,128]{2,1,0:T(8,128)}) custom-call(f32[6,64,32,128]{3,2,1,0:T(8,128)} %ph.1, s32[32,64]{1,0:T(8,128)} %bitcast.5), custom_call_target="tpu_custom_call" | custom-call | tf_op jit(solution)/shard_map/edges/pallas_call | solution.py:349
  3.0 3.1 %collective-permute-start = (f32[6,32,128]{2,1,0:T(8,128)}, f32[6,32,128]{2,1,0:T(8,128)S(1)}, u32[]{:S(2)}, u32[]{:S(2)}) collective-permute-start(f32[6,32,128]{2,1,0:T(8,128)} %get-tuple-element.33.c63), channel_id=1, source_target_pairs={{0,8},{8,16},{16,24},{24,32},{32,40},{40,48},{48,56},{56,64},{64,7... | collective-permute-start | bytes 294920 | tf_op jit(solution)/shard_map/ppermute | solution.py:341
  6.1 0.0 collective-permute-start.1
  6.1 0.0 copy-done.7
  6.1 0.0 copy-done.6
  6.1 0.0 copy-done.4
  6.1 0.0 copy-done.5
  6.1 0.0 copy-start.9
  6.1 0.0 copy-start.8
  6.1 0.0 slice-start.1
  6.1 0.0 copy-start.3
  6.1 1.9 %prep.1 = (s32[32,128]{1,0:T(8,128)S(1)}, f32[3,32,128]{2,1,0:T(8,128)S(1)}, s32[32,128]{1,0:T(8,128)S(1)}, s32[32,128]{1,0:T(8,128)S(1)}, s32[32,128]{1,0:T(8,1...) custom-call(s32[4,4096]{1,0:T(4,128)S(1)} %copy-done.4, f32[3,4096]{1,0:T(4,128)S(1)} %copy-done.5, ...), custom_call_target="tpu_custom_call" | custom-call | flops 4000000000 | bytes 40000000 | tf_op jit(solution)/shard_map/prep/pallas_call | solution.py:364
  8.1 0.0 copy-start
  8.1 0.0 copy-start.2
  8.1 0.0 collective-permute-done.xm
  8.1 3.0 %collective-permute-done.1.xp = f32[6,32,128]{2,1,0:T(8,128)S(1)} collective-permute-done((f32[6,32,128]{2,1,0:T(8,128)}, f32[6,32,128]{2,1,0:T(8,128)S(1)}, u32[]{:S(2)}, u32[]{:S(2)}) %collective-permute-start.1) | collective-permute-done | bytes 98336 | tf_op jit(solution)/shard_map/ppermute | solution.py:341
  11.1 0.0 copy-done.9
  11.2 1.5 %collective-permute-start.2 = (f32[6,66,128]{2,1,0:T(8,128)S(1)}, f32[6,66,128]{2,1,0:T(8,128)S(1)}, u32[]{:S(2)}, u32[]{:S(2)}) collective-permute-start(f32[6,66,128]{2,1,0:T(8,128)S(1)} %pad_maximum_fusion.top), channel_id=1, source_target_pairs={{0,1},{1,2},{2,3},{3,4},{4,5},{5,6},{6,7},{7,0},{8,9},{9,10},{10,1... | collective-permute-start | bytes 608264 | tf_op jit(solution)/shard_map/ppermute | solution.py:341
  12.7 0.0 copy-done.8
  12.7 4.7 %collective-permute-start.3 = (f32[6,66,128]{2,1,0:T(8,128)S(1)}, f32[6,66,128]{2,1,0:T(8,128)S(1)}, u32[]{:S(2)}, u32[]{:S(2)}) collective-permute-start(f32[6,66,128]{2,1,0:T(8,128)S(1)} %pad_maximum_fusion.1.bottom), channel_id=1, source_target_pairs={{0,7},{1,0},{2,1},{3,2},{4,3},{5,4},{6,5},{7,6},{8,15},{9,8},{10,9... | collective-permute-start | bytes 608264 | tf_op jit(solution)/shard_map/ppermute | solution.py:341
  17.4 0.0 slice-done.1
  17.4 11.3 %inner.1 = (f32[3,4104,128]{2,1,0:T(8,128)S(1)}, f32[3,512,8,128]{3,2,1,0:T(8,128)S(1)}) custom-call(f32[6,64,32,128]{3,2,1,0:T(8,128)S(1)} %bitcast.4, s32[32,64]{1,0:T(8,128)S(1)} %bitcast.6, s32[32,128]{1,0:T(8,128)S(1)} %get-tuple-element.23.flat, f32[3,32,128]{2,1,0:T(8,128)S(1)} %get-tuple-element.24.rel), custom_call_target="tpu_custom_call" | custom-call | flops 60000000 | bytes 7000000 | tf_op jit(solution)/shard_map/inner/pallas_call | solution.py:382
  28.6 0.0 collective-permute-done.2.ym
  28.6 0.0 collective-permute-done.3.yp
  28.7 0.0 copy-done
  28.7 0.0 copy-done.1
  28.7 0.0 copy-done.2
  28.7 6.9 %outer.1 = f32[128,1,384]{2,1,0:T(1,128)S(1)} custom-call(s32[40,128]{1,0:T(8,128)S(1)} %get-tuple-element.21.points, s32[40,128]{1,0:T(8,128)S(1)} %get-tuple-element.22.places, f32[3,4104,128]{2,1,0:T(8,128)S(1)} %get-tuple-element.25.sums, f32[3,512,8,128]{3,2,1,0:T(8,128)S(1)} %get-tuple-element.26.near, f32[3,4096]{1,0:T(4,128)S(1)} %copy-done.2, ...), custom_call_target="tpu_custom_call" | custom-call | tf_op jit(solution)/shard_map/outer/pallas_call | solution.py:404
  35.6 16.3 %all_to_all.5.got = f32[128,1,384]{2,1,0:T(1,128)S(1)} all-to-all(f32[128,1,384]{2,1,0:T(1,128)S(1)} %outer.1), channel_id=1, replica_groups=mesh['bx'=16,'by'=8] {'bx','by'}, dimensions={0} | all-to-all | bytes 393216 | tf_op jit(solution)/shard_map/all_to_all | solution.py:418
  51.9 1.9 %film.1 = f32[3,8,256]{2,1,0:T(8,128)} custom-call(f32[128,1,384]{2,1,0:T(1,128)S(1)} %all_to_all.5.got), custom_call_target="tpu_custom_call" | custom-call | tf_op jit(solution)/shard_map/film/pallas_call | solution.py:419
  (11 shorter events, 0.1 us)
Async XLA Ops:
  0.0 6.1 %copy-start.7 = (s32[1024]{0:T(1024)S(1)}, s32[1024]{0:T(1024)}, u32[]{:S(2)}) copy-start(s32[1024]{0:T(1024)} %param.13) | copy-start | bytes 12292
  0.0 6.1 %copy-start.6 = (s32[4096]{0:T(1024)S(1)}, s32[4096]{0:T(1024)}, u32[]{:S(2)}) copy-start(s32[4096]{0:T(1024)} %param.12) | copy-start | bytes 49156
  0.0 6.1 %copy-start.4 = (s32[4,4096]{1,0:T(4,128)S(1)}, s32[4,4096]{1,0:T(4,128)}, u32[]{:S(2)}) copy-start(s32[4,4096]{1,0:T(4,128)} %blocks.1) | copy-start | bytes 196612
  0.0 6.1 %copy-start.5 = (f32[3,4096]{1,0:T(4,128)S(1)}, f32[3,4096]{1,0:T(4,128)}, u32[]{:S(2)}) copy-start(f32[3,4096]{1,0:T(4,128)} %offs.1) | copy-start | bytes 147460
  0.0 17.3 %slice-start = ((s8[6291456]{0:T(1024)(128)(4,1)}), s8[2097152]{0:T(1024)(128)(4,1)S(1)}, s32[]{:S(2)}) async-start(s8[6291456]{0:T(1024)(128)(4,1)} %bitcast.3), calls=%async_computation.1 | async-start | bytes 4194304
  3.0 5.1 %collective-permute-start = (f32[6,32,128]{2,1,0:T(8,128)}, f32[6,32,128]{2,1,0:T(8,128)S(1)}, u32[]{:S(2)}, u32[]{:S(2)}) collective-permute-start(f32[6,32,128]{2,1,0:T(8,128)} %get-tuple-element.33.c63), channel_id=1, source_target_pairs={{0,8},{8,16},{16,24},{24,32},{32,40},{40,48},{48,56},{56,64},{64,7... | collective-permute-start | bytes 294920 | tf_op jit(solution)/shard_map/ppermute | solution.py:341
  6.1 5.1 %collective-permute-start.1 = (f32[6,32,128]{2,1,0:T(8,128)}, f32[6,32,128]{2,1,0:T(8,128)S(1)}, u32[]{:S(2)}, u32[]{:S(2)}) collective-permute-start(f32[6,32,128]{2,1,0:T(8,128)} %get-tuple-element.34.c0), channel_id=1, source_target_pairs={{0,120},{8,0},{16,8},{24,16},{32,24},{40,32},{48,40},{56,48},{64,5... | collective-permute-start | bytes 294920 | tf_op jit(solution)/shard_map/ppermute | solution.py:341
  6.1 5.1 %copy-start.9 = (f32[6,64,128]{2,1,0:T(8,128)S(1)}, f32[6,64,128]{2,1,0:T(8,128)}, u32[]{:S(2)}) copy-start(f32[6,64,128]{2,1,0:T(8,128)} %get-tuple-element.35) | copy-start | bytes 589828
  6.1 6.6 %copy-start.8 = (f32[6,64,128]{2,1,0:T(8,128)S(1)}, f32[6,64,128]{2,1,0:T(8,128)}, u32[]{:S(2)}) copy-start(f32[6,64,128]{2,1,0:T(8,128)} %get-tuple-element.36) | copy-start | bytes 589828
  6.1 11.3 %slice-start.1 = ((s8[6291456]{0:T(1024)(128)(4,1)}), s8[4194304]{0:T(1024)(128)(4,1)S(1)}, s32[]{:S(2)}) async-start(s8[6291456]{0:T(1024)(128)(4,1)} %bitcast.3), calls=%async_computation.2 | async-start | bytes 8388608
  6.1 11.2 %copy-start.3 = (s32[64,32]{0,1:T(8,128)S(1)}, s32[64,32]{0,1:T(8,128)}, u32[]{:S(2)}) copy-start(s32[64,32]{0,1:T(8,128)} %param.8) | copy-start | bytes 24580
  8.1 20.6 %copy-start = (f32[6,32,128]{2,1,0:T(8,128)S(1)}, f32[6,32,128]{2,1,0:T(8,128)}, u32[]{:S(2)}) copy-start(f32[6,32,128]{2,1,0:T(8,128)} %get-tuple-element.33.c63) | copy-start | bytes 294916
  8.1 20.6 %copy-start.1 = (f32[6,32,128]{2,1,0:T(8,128)S(1)}, f32[6,32,128]{2,1,0:T(8,128)}, u32[]{:S(2)}) copy-start(f32[6,32,128]{2,1,0:T(8,128)} %get-tuple-element.34.c0) | copy-start | bytes 294916
  8.1 20.6 %copy-start.2 = (f32[3,4096]{1,0:T(4,128)S(1)}, f32[3,4096]{1,0:T(4,128)}, u32[]{:S(2)}) copy-start(f32[3,4096]{1,0:T(4,128)} %alb.1) | copy-start | bytes 147460
  11.2 17.5 %collective-permute-start.2 = (f32[6,66,128]{2,1,0:T(8,128)S(1)}, f32[6,66,128]{2,1,0:T(8,128)S(1)}, u32[]{:S(2)}, u32[]{:S(2)}) collective-permute-start(f32[6,66,128]{2,1,0:T(8,128)S(1)} %pad_maximum_fusion.top), channel_id=1, source_target_pairs={{0,1},{1,2},{2,3},{3,4},{4,5},{5,6},{6,7},{7,0},{8,9},{9,10},{10,1... | collective-permute-start | bytes 608264 | tf_op jit(solution)/shard_map/ppermute | solution.py:341
  12.7 15.9 %collective-permute-start.3 = (f32[6,66,128]{2,1,0:T(8,128)S(1)}, f32[6,66,128]{2,1,0:T(8,128)S(1)}, u32[]{:S(2)}, u32[]{:S(2)}) collective-permute-start(f32[6,66,128]{2,1,0:T(8,128)S(1)} %pad_maximum_fusion.1.bottom), channel_id=1, source_target_pairs={{0,7},{1,0},{2,1},{3,2},{4,3},{5,4},{6,5},{7,6},{8,15},{9,8},{10,9... | collective-permute-start | bytes 608264 | tf_op jit(solution)/shard_map/ppermute | solution.py:341

commit v7 on v6

--- a/solution.py
+++ b/solution.py
@@ -159,9 +159,7 @@
     points[ROWS:] = jnp.broadcast_to(count, (8, LANES))
     places[ROWS:] = jnp.broadcast_to(count, (8, LANES))
 
-def inner_kernel(photons, counts, flat, rel, sums, near, ph, table, square, stage_a, stage_b, psem, ssem, *start):
-    read = pltpu.make_async_copy(photons, ph, psem)
-    read.start()
+def inner_kernel(ph, counts, flat, rel, sums, near, table, square, stage_a, stage_b, ssem, *start):
     to_scalar = [pltpu.make_async_copy(flat.at[pl.ds(4 * s, 4)], start[s], ssem.at[s]) for s in range(8)]
     for copy in to_scalar:
         copy.start()
@@ -191,7 +189,6 @@
             table[pl.ds(row(c, x, 1, 1), CY, stride=4), :] = v
         return 0
 
-    read.wait()
     lax.fori_loop(0, CX, column, 0, unroll=16)
     for copy in to_scalar:
         copy.wait()
@@ -381,19 +378,17 @@
     ym, yp = shift(top, "by", 1), shift(bottom, "by", -1)
     sums, near = pl.pallas_call(
         inner_kernel,
-        in_specs=[HBM] + [VMEM] * 3,
+        in_specs=[VMEM] * 4,
         out_specs=[VMEM] * 2,
         out_shape=[
             jax.ShapeDtypeStruct((3, 8 * APART, LANES), f32),
             jax.ShapeDtypeStruct((3, POINTS // 8, 8, LANES), f32),
         ],
         scratch_shapes=[
-            pltpu.VMEM((6, CX, CY, LANES), f32),
             pltpu.VMEM((TABLE_ROWS, LANES), f32),
             pltpu.VMEM((CY, LANES), f32),
             pltpu.VMEM((GROUPS, 3, 8 * STEP + 8, LANES), f32),
             pltpu.VMEM((GROUPS, 3, 8 * STEP + 8, LANES), f32),
-            pltpu.SemaphoreType.DMA,
             pltpu.SemaphoreType.DMA((8,)),
         ]
         + [pltpu.SMEM((4, LANES), i32)] * 8,

time: 54 us -> 53.5 us (level)
  Pallas kernels: 24.9 us -> 24.1 us
  transfers between devices with their start and end apart: 4 -> 4, of which waited for: 1 -> 1; matrix products, arithmetic and copies ran while one was open for 0% -> 0% of each run, Pallas kernels for 25% -> 24%
where the time goes in v7:
time: 53.5 us; the launch traced here: 53.4 us
  Pallas kernels  24.1 us (45%)
  blocking collectives  16.7 us (31%)
  starting transfers between devices  9.23 us (17%)
  waiting for transfers between devices  3.02 us (6%)
    all_to_all x1, blocking collectives, per_device(): got = lax.all_to_all(send, AXES, 0, 0, tiled=True)  16.7 us
    pallas_call x1, Pallas kernels, per_device(): pl.pallas_call(inner_kernel, in_specs=[VMEM] * 4, out_specs=[VMEM] * 2, o...  10.8 us
    ppermute x4, starting transfers between devices, shift(): return lax.ppermute(x, axis, [(i, (i + by) % n) for i in range(n)])  9.23 us
    pallas_call x1, Pallas kernels, per_device(): pl.pallas_call(outer_kernel, in_specs=[SMEM] * 2 + [VMEM] * 14, out_specs...  6.54 us
    ppermute x4, waiting for transfers between devices, shift(): return lax.ppermute(x, axis, [(i, (i + by) % n) for i in range(n)])  3.02 us
    pallas_call x1, Pallas kernels, per_device(): pl.pallas_call(edge_kernel, in_specs=[HBM, VMEM], out_specs=[VMEM] * 4, o...  2.93 us
    pallas_call x1, Pallas kernels, per_device(): pl.pallas_call(prep_kernel, in_specs=[VMEM] * 4, out_specs=[VMEM] * 7, ou...  1.92 us
    pallas_call x1, Pallas kernels, per_device(): pl.pallas_call(film_kernel, in_specs=[VMEM], out_specs=VMEM, out_shape=ja...  1.87 us
  transfers between devices with their start and end apart: 4, of which 1 were waited for; matrix products, arithmetic and copies ran while one was open for 0% of the time, Pallas kernels for 24%

profile of v7, /device:TPU:1, one launch (start us, length us, event | category | flops | bytes accessed | tf_op | source)
XLA Modules:
  0.0 53.4 jit_solution(9512229028580394294)
XLA Ops:
  0.0 0.0 copy-start.5
  0.0 0.0 slice-start
  0.0 2.9 %edges.1 = (f32[6,32,128]{2,1,0:T(8,128)}, f32[6,32,128]{2,1,0:T(8,128)}, f32[6,64,128]{2,1,0:T(8,128)}, f32[6,64,128]{2,1,0:T(8,128)}) custom-call(f32[6,64,32,128]{3,2,1,0:T(8,128)} %ph.3, s32[32,64]{1,0:T(8,128)} %bitcast.5), custom_call_target="tpu_custom_call" | custom-call | tf_op jit(solution)/shard_map/edges/pallas_call | solution.py:346
  3.0 3.1 %collective-permute-start = (f32[6,32,128]{2,1,0:T(8,128)}, f32[6,32,128]{2,1,0:T(8,128)S(1)}, u32[]{:S(2)}, u32[]{:S(2)}) collective-permute-start(f32[6,32,128]{2,1,0:T(8,128)} %get-tuple-element.33.c63), channel_id=1, source_target_pairs={{0,8},{8,16},{16,24},{24,32},{32,40},{40,48},{48,56},{56,64},{64,7... | collective-permute-start | bytes 294920 | tf_op jit(solution)/shard_map/ppermute | solution.py:338
  6.1 0.0 collective-permute-start.1
  6.1 0.0 copy-done.7
  6.1 0.0 copy-done.6
  6.1 0.0 copy-done.4
  6.1 0.0 copy-done.5
  6.1 0.0 copy-start.9
  6.1 0.0 copy-start.8
  6.1 0.0 slice-start.1
  6.1 0.0 copy-start.3
  6.1 1.9 %prep.1 = (s32[32,128]{1,0:T(8,128)S(1)}, f32[3,32,128]{2,1,0:T(8,128)S(1)}, s32[32,128]{1,0:T(8,128)S(1)}, s32[32,128]{1,0:T(8,128)S(1)}, s32[32,128]{1,0:T(8,1...) custom-call(s32[4,4096]{1,0:T(4,128)S(1)} %copy-done.4, f32[3,4096]{1,0:T(4,128)S(1)} %copy-done.5, ...), custom_call_target="tpu_custom_call" | custom-call | flops 4000000000 | bytes 40000000 | tf_op jit(solution)/shard_map/prep/pallas_call | solution.py:361
  8.1 0.0 copy-start
  8.1 0.0 copy-start.2
  8.1 0.0 collective-permute-done.xm
  8.1 3.0 %collective-permute-done.1.xp = f32[6,32,128]{2,1,0:T(8,128)S(1)} collective-permute-done((f32[6,32,128]{2,1,0:T(8,128)}, f32[6,32,128]{2,1,0:T(8,128)S(1)}, u32[]{:S(2)}, u32[]{:S(2)}) %collective-permute-start.1) | collective-permute-done | bytes 98336 | tf_op jit(solution)/shard_map/ppermute | solution.py:338
  11.1 0.0 copy-done.9
  11.2 1.5 %collective-permute-start.2 = (f32[6,66,128]{2,1,0:T(8,128)S(1)}, f32[6,66,128]{2,1,0:T(8,128)S(1)}, u32[]{:S(2)}, u32[]{:S(2)}) collective-permute-start(f32[6,66,128]{2,1,0:T(8,128)S(1)} %pad_maximum_fusion.top), channel_id=1, source_target_pairs={{0,1},{1,2},{2,3},{3,4},{4,5},{5,6},{6,7},{7,0},{8,9},{9,10},{10,1... | collective-permute-start | bytes 608264 | tf_op jit(solution)/shard_map/ppermute | solution.py:338
  12.7 0.0 copy-done.8
  12.7 4.7 %collective-permute-start.3 = (f32[6,66,128]{2,1,0:T(8,128)S(1)}, f32[6,66,128]{2,1,0:T(8,128)S(1)}, u32[]{:S(2)}, u32[]{:S(2)}) collective-permute-start(f32[6,66,128]{2,1,0:T(8,128)S(1)} %pad_maximum_fusion.1.bottom), channel_id=1, source_target_pairs={{0,7},{1,0},{2,1},{3,2},{4,3},{5,4},{6,5},{7,6},{8,15},{9,8},{10,9... | collective-permute-start | bytes 608264 | tf_op jit(solution)/shard_map/ppermute | solution.py:338
  17.4 0.0 slice-done.1
  17.4 10.8 %inner.1 = (f32[3,4104,128]{2,1,0:T(8,128)S(1)}, f32[3,512,8,128]{3,2,1,0:T(8,128)S(1)}) custom-call(f32[6,64,32,128]{3,2,1,0:T(8,128)S(1)} %bitcast.4, s32[32,64]{1,0:T(8,128)S(1)} %bitcast.6, s32[32,128]{1,0:T(8,128)S(1)} %get-tuple-element.23.flat, f32[3,32,128]{2,1,0:T(8,128)S(1)} %get-tuple-element.24.rel), custom_call_target="tpu_custom_call" | custom-call | flops 60000000 | bytes 7000000 | tf_op jit(solution)/shard_map/inner/pallas_call | solution.py:379
  28.2 0.0 collective-permute-done.2.ym
  28.2 0.0 collective-permute-done.3.yp
  28.2 0.0 copy-done
  28.2 0.0 copy-done.1
  28.2 0.0 copy-done.2
  28.3 6.5 %outer.1 = f32[128,1,384]{2,1,0:T(1,128)S(1)} custom-call(s32[40,128]{1,0:T(8,128)S(1)} %get-tuple-element.21.points, s32[40,128]{1,0:T(8,128)S(1)} %get-tuple-element.22.places, f32[3,4104,128]{2,1,0:T(8,128)S(1)} %get-tuple-element.25.sums, f32[3,512,8,128]{3,2,1,0:T(8,128)S(1)} %get-tuple-element.26.near, f32[3,4096]{1,0:T(4,128)S(1)} %copy-done.2, ...), custom_call_target="tpu_custom_call" | custom-call | tf_op jit(solution)/shard_map/outer/pallas_call | solution.py:399
  34.8 16.7 %all_to_all.5.got = f32[128,1,384]{2,1,0:T(1,128)S(1)} all-to-all(f32[128,1,384]{2,1,0:T(1,128)S(1)} %outer.1), channel_id=1, replica_groups=mesh['bx'=16,'by'=8] {'bx','by'}, dimensions={0} | all-to-all | bytes 393216 | tf_op jit(solution)/shard_map/all_to_all | solution.py:413
  51.5 1.9 %film.1 = f32[3,8,256]{2,1,0:T(8,128)} custom-call(f32[128,1,384]{2,1,0:T(1,128)S(1)} %all_to_all.5.got), custom_call_target="tpu_custom_call" | custom-call | tf_op jit(solution)/shard_map/film/pallas_call | solution.py:414
  (11 shorter events, 0.1 us)
Async XLA Ops:
  0.0 6.1 %copy-start.7 = (s32[1024]{0:T(1024)S(1)}, s32[1024]{0:T(1024)}, u32[]{:S(2)}) copy-start(s32[1024]{0:T(1024)} %param.13) | copy-start | bytes 12292
  0.0 6.1 %copy-start.6 = (s32[4096]{0:T(1024)S(1)}, s32[4096]{0:T(1024)}, u32[]{:S(2)}) copy-start(s32[4096]{0:T(1024)} %param.12) | copy-start | bytes 49156
  0.0 6.1 %copy-start.4 = (s32[4,4096]{1,0:T(4,128)S(1)}, s32[4,4096]{1,0:T(4,128)}, u32[]{:S(2)}) copy-start(s32[4,4096]{1,0:T(4,128)} %blocks.1) | copy-start | bytes 196612
  0.0 6.1 %copy-start.5 = (f32[3,4096]{1,0:T(4,128)S(1)}, f32[3,4096]{1,0:T(4,128)}, u32[]{:S(2)}) copy-start(f32[3,4096]{1,0:T(4,128)} %offs.1) | copy-start | bytes 147460
  0.0 17.3 %slice-start = ((s8[6291456]{0:T(1024)(128)(4,1)}), s8[2097152]{0:T(1024)(128)(4,1)S(1)}, s32[]{:S(2)}) async-start(s8[6291456]{0:T(1024)(128)(4,1)} %bitcast.3), calls=%async_computation.1 | async-start | bytes 4194304
  3.0 5.1 %collective-permute-start = (f32[6,32,128]{2,1,0:T(8,128)}, f32[6,32,128]{2,1,0:T(8,128)S(1)}, u32[]{:S(2)}, u32[]{:S(2)}) collective-permute-start(f32[6,32,128]{2,1,0:T(8,128)} %get-tuple-element.33.c63), channel_id=1, source_target_pairs={{0,8},{8,16},{16,24},{24,32},{32,40},{40,48},{48,56},{56,64},{64,7... | collective-permute-start | bytes 294920 | tf_op jit(solution)/shard_map/ppermute | solution.py:338
  6.1 5.1 %collective-permute-start.1 = (f32[6,32,128]{2,1,0:T(8,128)}, f32[6,32,128]{2,1,0:T(8,128)S(1)}, u32[]{:S(2)}, u32[]{:S(2)}) collective-permute-start(f32[6,32,128]{2,1,0:T(8,128)} %get-tuple-element.34.c0), channel_id=1, source_target_pairs={{0,120},{8,0},{16,8},{24,16},{32,24},{40,32},{48,40},{56,48},{64,5... | collective-permute-start | bytes 294920 | tf_op jit(solution)/shard_map/ppermute | solution.py:338
  6.1 5.1 %copy-start.9 = (f32[6,64,128]{2,1,0:T(8,128)S(1)}, f32[6,64,128]{2,1,0:T(8,128)}, u32[]{:S(2)}) copy-start(f32[6,64,128]{2,1,0:T(8,128)} %get-tuple-element.35) | copy-start | bytes 589828
  6.1 6.6 %copy-start.8 = (f32[6,64,128]{2,1,0:T(8,128)S(1)}, f32[6,64,128]{2,1,0:T(8,128)}, u32[]{:S(2)}) copy-start(f32[6,64,128]{2,1,0:T(8,128)} %get-tuple-element.36) | copy-start | bytes 589828
  6.1 11.3 %slice-start.1 = ((s8[6291456]{0:T(1024)(128)(4,1)}), s8[4194304]{0:T(1024)(128)(4,1)S(1)}, s32[]{:S(2)}) async-start(s8[6291456]{0:T(1024)(128)(4,1)} %bitcast.3), calls=%async_computation.2 | async-start | bytes 8388608
  6.1 11.2 %copy-start.3 = (s32[64,32]{0,1:T(8,128)S(1)}, s32[64,32]{0,1:T(8,128)}, u32[]{:S(2)}) copy-start(s32[64,32]{0,1:T(8,128)} %param.8) | copy-start | bytes 24580
  8.1 20.2 %copy-start = (f32[6,32,128]{2,1,0:T(8,128)S(1)}, f32[6,32,128]{2,1,0:T(8,128)}, u32[]{:S(2)}) copy-start(f32[6,32,128]{2,1,0:T(8,128)} %get-tuple-element.33.c63) | copy-start | bytes 294916
  8.1 20.2 %copy-start.1 = (f32[6,32,128]{2,1,0:T(8,128)S(1)}, f32[6,32,128]{2,1,0:T(8,128)}, u32[]{:S(2)}) copy-start(f32[6,32,128]{2,1,0:T(8,128)} %get-tuple-element.34.c0) | copy-start | bytes 294916
  8.1 20.2 %copy-start.2 = (f32[3,4096]{1,0:T(4,128)S(1)}, f32[3,4096]{1,0:T(4,128)}, u32[]{:S(2)}) copy-start(f32[3,4096]{1,0:T(4,128)} %alb.1) | copy-start | bytes 147460
  11.2 17.0 %collective-permute-start.2 = (f32[6,66,128]{2,1,0:T(8,128)S(1)}, f32[6,66,128]{2,1,0:T(8,128)S(1)}, u32[]{:S(2)}, u32[]{:S(2)}) collective-permute-start(f32[6,66,128]{2,1,0:T(8,128)S(1)} %pad_maximum_fusion.top), channel_id=1, source_target_pairs={{0,1},{1,2},{2,3},{3,4},{4,5},{5,6},{6,7},{7,0},{8,9},{9,10},{10,1... | collective-permute-start | bytes 608264 | tf_op jit(solution)/shard_map/ppermute | solution.py:338
  12.7 15.5 %collective-permute-start.3 = (f32[6,66,128]{2,1,0:T(8,128)S(1)}, f32[6,66,128]{2,1,0:T(8,128)S(1)}, u32[]{:S(2)}, u32[]{:S(2)}) collective-permute-start(f32[6,66,128]{2,1,0:T(8,128)S(1)} %pad_maximum_fusion.1.bottom), channel_id=1, source_target_pairs={{0,7},{1,0},{2,1},{3,2},{4,3},{5,4},{6,5},{7,6},{8,15},{9,8},{10,9... | collective-permute-start | bytes 608264 | tf_op jit(solution)/shard_map/ppermute | solution.py:338

commit v8 on v7

--- a/solution.py
+++ b/solution.py
@@ -225,17 +225,18 @@
     for c in range(6):
         scale = 2.0 if c < 3 else 1.0
         plane = (c // 2) * EDGE + c % 2
+        for base, lines in ((2 * EDGE_X + EDGE_Y, (top, yp)), (2 * EDGE_X, (ym, bottom))):
+            for yy, line in enumerate(lines):
+                at = plane + base + 4 * yy
+                value = line[c] * scale
+                edge[pl.ds(at - 6, CX + 2, stride=8), :] = value
+                edge[pl.ds(at, CX + 1, stride=8), :] = value[: CX + 1]
         for base, cols in ((0, ((xm, 0), (c0, 1))), (EDGE_X, ((c63, CX), (xp, CX + 1)))):
             for right, (col, x) in enumerate(cols):
                 at = plane + base + 2 * right
                 edge[pl.ds(at + 4, CY, stride=4), :] = col[c] * scale
                 edge[at : at + 1, :] = ym[c, x : x + 1] * scale
                 edge[at + 4 * EY - 4 : at + 4 * EY - 3, :] = yp[c, x : x + 1] * scale
-        for base, lines in ((2 * EDGE_X, (ym, bottom)), (2 * EDGE_X + EDGE_Y, (top, yp))):
-            for yy, line in enumerate(lines):
-                for right in range(2):
-                    at = plane + base + 4 * yy + 2 * right
-                    edge[pl.ds(at, CX + 1, stride=8), :] = line[c, right : right + CX + 1] * scale
     sub = iota((8, LANES), 0)
     zero = lax.axis_index("bx") * 0
     count = points[ROWS, 0]

time: 53.5 us -> 53.1 us (level)
  no operation moved by 1% of the time
where the time goes in v8:
time: 53.1 us; the launch traced here: 52.8 us
  Pallas kernels  24 us (45%)
  blocking collectives  16.3 us (31%)
  starting transfers between devices  9.23 us (17%)
  waiting for transfers between devices  3.02 us (6%)
    all_to_all x1, blocking collectives, per_device(): got = lax.all_to_all(send, AXES, 0, 0, tiled=True)  16.3 us
    pallas_call x1, Pallas kernels, per_device(): pl.pallas_call(inner_kernel, in_specs=[VMEM] * 4, out_specs=[VMEM] * 2, o...  10.8 us
    ppermute x4, starting transfers between devices, shift(): return lax.ppermute(x, axis, [(i, (i + by) % n) for i in range(n)])  9.23 us
    pallas_call x1, Pallas kernels, per_device(): pl.pallas_call(outer_kernel, in_specs=[SMEM] * 2 + [VMEM] * 14, out_specs...  6.43 us
    ppermute x4, waiting for transfers between devices, shift(): return lax.ppermute(x, axis, [(i, (i + by) % n) for i in range(n)])  3.02 us
    pallas_call x1, Pallas kernels, per_device(): pl.pallas_call(edge_kernel, in_specs=[HBM, VMEM], out_specs=[VMEM] * 4, o...  2.93 us
    pallas_call x1, Pallas kernels, per_device(): pl.pallas_call(prep_kernel, in_specs=[VMEM] * 4, out_specs=[VMEM] * 7, ou...  1.92 us
    pallas_call x1, Pallas kernels, per_device(): pl.pallas_call(film_kernel, in_specs=[VMEM], out_specs=VMEM, out_shape=ja...  1.87 us
  transfers between devices with their start and end apart: 4, of which 1 were waited for; matrix products, arithmetic and copies ran while one was open for 0% of the time, Pallas kernels for 24%

profile of v8, /device:TPU:1, one launch (start us, length us, event | category | flops | bytes accessed | tf_op | source)
XLA Modules:
  0.0 52.8 jit_solution(3124498871385333815)
XLA Ops:
  0.0 0.0 copy-start.5
  0.0 0.0 slice-start
  0.0 2.9 %edges.1 = (f32[6,32,128]{2,1,0:T(8,128)}, f32[6,32,128]{2,1,0:T(8,128)}, f32[6,64,128]{2,1,0:T(8,128)}, f32[6,64,128]{2,1,0:T(8,128)}) custom-call(f32[6,64,32,128]{3,2,1,0:T(8,128)} %ph.3, s32[32,64]{1,0:T(8,128)} %bitcast.5), custom_call_target="tpu_custom_call" | custom-call | tf_op jit(solution)/shard_map/edges/pallas_call | solution.py:347
  3.0 3.1 %collective-permute-start = (f32[6,32,128]{2,1,0:T(8,128)}, f32[6,32,128]{2,1,0:T(8,128)S(1)}, u32[]{:S(2)}, u32[]{:S(2)}) collective-permute-start(f32[6,32,128]{2,1,0:T(8,128)} %get-tuple-element.33.c63), channel_id=1, source_target_pairs={{0,8},{8,16},{16,24},{24,32},{32,40},{40,48},{48,56},{56,64},{64,7... | collective-permute-start | bytes 294920 | tf_op jit(solution)/shard_map/ppermute | solution.py:339
  6.1 0.0 collective-permute-start.1
  6.1 0.0 copy-done.7
  6.1 0.0 copy-done.6
  6.1 0.0 copy-done.4
  6.1 0.0 copy-done.5
  6.1 0.0 copy-start.9
  6.1 0.0 copy-start.8
  6.1 0.0 slice-start.1
  6.1 0.0 copy-start.3
  6.1 1.9 %prep.1 = (s32[32,128]{1,0:T(8,128)S(1)}, f32[3,32,128]{2,1,0:T(8,128)S(1)}, s32[32,128]{1,0:T(8,128)S(1)}, s32[32,128]{1,0:T(8,128)S(1)}, s32[32,128]{1,0:T(8,1...) custom-call(s32[4,4096]{1,0:T(4,128)S(1)} %copy-done.4, f32[3,4096]{1,0:T(4,128)S(1)} %copy-done.5, ...), custom_call_target="tpu_custom_call" | custom-call | flops 4000000000 | bytes 40000000 | tf_op jit(solution)/shard_map/prep/pallas_call | solution.py:362
  8.1 0.0 copy-start
  8.1 0.0 copy-start.1
  8.1 0.0 copy-start.2
  8.1 0.0 collective-permute-done.xm
  8.1 3.0 %collective-permute-done.1.xp = f32[6,32,128]{2,1,0:T(8,128)S(1)} collective-permute-done((f32[6,32,128]{2,1,0:T(8,128)}, f32[6,32,128]{2,1,0:T(8,128)S(1)}, u32[]{:S(2)}, u32[]{:S(2)}) %collective-permute-start.1) | collective-permute-done | bytes 98336 | tf_op jit(solution)/shard_map/ppermute | solution.py:339
  11.1 0.0 copy-done.9
  11.2 1.5 %collective-permute-start.2 = (f32[6,66,128]{2,1,0:T(8,128)S(1)}, f32[6,66,128]{2,1,0:T(8,128)S(1)}, u32[]{:S(2)}, u32[]{:S(2)}) collective-permute-start(f32[6,66,128]{2,1,0:T(8,128)S(1)} %pad_maximum_fusion.top), channel_id=1, source_target_pairs={{0,1},{1,2},{2,3},{3,4},{4,5},{5,6},{6,7},{7,0},{8,9},{9,10},{10,1... | collective-permute-start | bytes 608264 | tf_op jit(solution)/shard_map/ppermute | solution.py:339
  12.7 0.0 copy-done.8
  12.7 4.7 %collective-permute-start.3 = (f32[6,66,128]{2,1,0:T(8,128)S(1)}, f32[6,66,128]{2,1,0:T(8,128)S(1)}, u32[]{:S(2)}, u32[]{:S(2)}) collective-permute-start(f32[6,66,128]{2,1,0:T(8,128)S(1)} %pad_maximum_fusion.1.bottom), channel_id=1, source_target_pairs={{0,7},{1,0},{2,1},{3,2},{4,3},{5,4},{6,5},{7,6},{8,15},{9,8},{10,9... | collective-permute-start | bytes 608264 | tf_op jit(solution)/shard_map/ppermute | solution.py:339
  17.4 0.0 slice-done
  17.4 0.0 slice-done.1
  17.4 0.0 copy-done.3
  17.4 10.8 %inner.1 = (f32[3,4104,128]{2,1,0:T(8,128)S(1)}, f32[3,512,8,128]{3,2,1,0:T(8,128)S(1)}) custom-call(f32[6,64,32,128]{3,2,1,0:T(8,128)S(1)} %bitcast.4, s32[32,64]{1,0:T(8,128)S(1)} %bitcast.6, s32[32,128]{1,0:T(8,128)S(1)} %get-tuple-element.23.flat, f32[3,32,128]{2,1,0:T(8,128)S(1)} %get-tuple-element.24.rel), custom_call_target="tpu_custom_call" | custom-call | flops 60000000 | bytes 7000000 | tf_op jit(solution)/shard_map/inner/pallas_call | solution.py:380
  28.2 0.0 collective-permute-done.2.ym
  28.2 0.0 collective-permute-done.3.yp
  28.3 6.4 %outer.1 = f32[128,1,384]{2,1,0:T(1,128)S(1)} custom-call(s32[40,128]{1,0:T(8,128)S(1)} %get-tuple-element.21.points, s32[40,128]{1,0:T(8,128)S(1)} %get-tuple-element.22.places, f32[3,4104,128]{2,1,0:T(8,128)S(1)} %get-tuple-element.25.sums, f32[3,512,8,128]{3,2,1,0:T(8,128)S(1)} %get-tuple-element.26.near, f32[3,4096]{1,0:T(4,128)S(1)} %copy-done.2, ...), custom_call_target="tpu_custom_call" | custom-call | tf_op jit(solution)/shard_map/outer/pallas_call | solution.py:400
  34.7 16.3 %all_to_all.5.got = f32[128,1,384]{2,1,0:T(1,128)S(1)} all-to-all(f32[128,1,384]{2,1,0:T(1,128)S(1)} %outer.1), channel_id=1, replica_groups=mesh['bx'=16,'by'=8] {'bx','by'}, dimensions={0} | all-to-all | bytes 393216 | tf_op jit(solution)/shard_map/all_to_all | solution.py:414
  51.0 1.9 %film.1 = f32[3,8,256]{2,1,0:T(8,128)} custom-call(f32[128,1,384]{2,1,0:T(1,128)S(1)} %all_to_all.5.got), custom_call_target="tpu_custom_call" | custom-call | tf_op jit(solution)/shard_map/film/pallas_call | solution.py:415
  (11 shorter events, 0.1 us)
Async XLA Ops:
  0.0 6.1 %copy-start.7 = (s32[1024]{0:T(1024)S(1)}, s32[1024]{0:T(1024)}, u32[]{:S(2)}) copy-start(s32[1024]{0:T(1024)} %param.13) | copy-start | bytes 12292
  0.0 6.1 %copy-start.6 = (s32[4096]{0:T(1024)S(1)}, s32[4096]{0:T(1024)}, u32[]{:S(2)}) copy-start(s32[4096]{0:T(1024)} %param.12) | copy-start | bytes 49156
  0.0 6.1 %copy-start.4 = (s32[4,4096]{1,0:T(4,128)S(1)}, s32[4,4096]{1,0:T(4,128)}, u32[]{:S(2)}) copy-start(s32[4,4096]{1,0:T(4,128)} %blocks.1) | copy-start | bytes 196612
  0.0 6.1 %copy-start.5 = (f32[3,4096]{1,0:T(4,128)S(1)}, f32[3,4096]{1,0:T(4,128)}, u32[]{:S(2)}) copy-start(f32[3,4096]{1,0:T(4,128)} %offs.1) | copy-start | bytes 147460
  0.0 17.3 %slice-start = ((s8[6291456]{0:T(1024)(128)(4,1)}), s8[2097152]{0:T(1024)(128)(4,1)S(1)}, s32[]{:S(2)}) async-start(s8[6291456]{0:T(1024)(128)(4,1)} %bitcast.3), calls=%async_computation.1 | async-start | bytes 4194304
  3.0 5.1 %collective-permute-start = (f32[6,32,128]{2,1,0:T(8,128)}, f32[6,32,128]{2,1,0:T(8,128)S(1)}, u32[]{:S(2)}, u32[]{:S(2)}) collective-permute-start(f32[6,32,128]{2,1,0:T(8,128)} %get-tuple-element.33.c63), channel_id=1, source_target_pairs={{0,8},{8,16},{16,24},{24,32},{32,40},{40,48},{48,56},{56,64},{64,7... | collective-permute-start | bytes 294920 | tf_op jit(solution)/shard_map/ppermute | solution.py:339
  6.1 5.1 %collective-permute-start.1 = (f32[6,32,128]{2,1,0:T(8,128)}, f32[6,32,128]{2,1,0:T(8,128)S(1)}, u32[]{:S(2)}, u32[]{:S(2)}) collective-permute-start(f32[6,32,128]{2,1,0:T(8,128)} %get-tuple-element.34.c0), channel_id=1, source_target_pairs={{0,120},{8,0},{16,8},{24,16},{32,24},{40,32},{48,40},{56,48},{64,5... | collective-permute-start | bytes 294920 | tf_op jit(solution)/shard_map/ppermute | solution.py:339
  6.1 5.1 %copy-start.9 = (f32[6,64,128]{2,1,0:T(8,128)S(1)}, f32[6,64,128]{2,1,0:T(8,128)}, u32[]{:S(2)}) copy-start(f32[6,64,128]{2,1,0:T(8,128)} %get-tuple-element.35) | copy-start | bytes 589828
  6.1 6.6 %copy-start.8 = (f32[6,64,128]{2,1,0:T(8,128)S(1)}, f32[6,64,128]{2,1,0:T(8,128)}, u32[]{:S(2)}) copy-start(f32[6,64,128]{2,1,0:T(8,128)} %get-tuple-element.36) | copy-start | bytes 589828
  6.1 11.3 %slice-start.1 = ((s8[6291456]{0:T(1024)(128)(4,1)}), s8[4194304]{0:T(1024)(128)(4,1)S(1)}, s32[]{:S(2)}) async-start(s8[6291456]{0:T(1024)(128)(4,1)} %bitcast.3), calls=%async_computation.2 | async-start | bytes 8388608
  6.1 11.2 %copy-start.3 = (s32[64,32]{0,1:T(8,128)S(1)}, s32[64,32]{0,1:T(8,128)}, u32[]{:S(2)}) copy-start(s32[64,32]{0,1:T(8,128)} %param.8) | copy-start | bytes 24580
  8.1 20.2 %copy-start = (f32[6,32,128]{2,1,0:T(8,128)S(1)}, f32[6,32,128]{2,1,0:T(8,128)}, u32[]{:S(2)}) copy-start(f32[6,32,128]{2,1,0:T(8,128)} %get-tuple-element.33.c63) | copy-start | bytes 294916
  8.1 20.2 %copy-start.1 = (f32[6,32,128]{2,1,0:T(8,128)S(1)}, f32[6,32,128]{2,1,0:T(8,128)}, u32[]{:S(2)}) copy-start(f32[6,32,128]{2,1,0:T(8,128)} %get-tuple-element.34.c0) | copy-start | bytes 294916
  8.1 20.2 %copy-start.2 = (f32[3,4096]{1,0:T(4,128)S(1)}, f32[3,4096]{1,0:T(4,128)}, u32[]{:S(2)}) copy-start(f32[3,4096]{1,0:T(4,128)} %alb.1) | copy-start | bytes 147460
  11.2 17.0 %collective-permute-start.2 = (f32[6,66,128]{2,1,0:T(8,128)S(1)}, f32[6,66,128]{2,1,0:T(8,128)S(1)}, u32[]{:S(2)}, u32[]{:S(2)}) collective-permute-start(f32[6,66,128]{2,1,0:T(8,128)S(1)} %pad_maximum_fusion.top), channel_id=1, source_target_pairs={{0,1},{1,2},{2,3},{3,4},{4,5},{5,6},{6,7},{7,0},{8,9},{9,10},{10,1... | collective-permute-start | bytes 608264 | tf_op jit(solution)/shard_map/ppermute | solution.py:339
  12.7 15.5 %collective-permute-start.3 = (f32[6,66,128]{2,1,0:T(8,128)S(1)}, f32[6,66,128]{2,1,0:T(8,128)S(1)}, u32[]{:S(2)}, u32[]{:S(2)}) collective-permute-start(f32[6,66,128]{2,1,0:T(8,128)S(1)} %pad_maximum_fusion.1.bottom), channel_id=1, source_target_pairs={{0,7},{1,0},{2,1},{3,2},{4,3},{5,4},{6,5},{7,6},{8,15},{9,8},{10,9... | collective-permute-start | bytes 608264 | tf_op jit(solution)/shard_map/ppermute | solution.py:339
